TPU v7x, 32 devices: a whole 2x2x4 slice. The times are simulated.
32 devices in a mesh: fsdp: 8 (over z, core), tp: 4 (over y, x).
Axes of the slice: x: 2, y: 2, z: 4, core: 2. Of those that a mesh axis runs over, the one named last changes fastest.
Arguments:
- tokens: bfloat16 [16384, 2048], P(('fsdp', 'tp')), may hold values from -6 to 6
- gain_attn: float32 [2048], replicated, may hold values from 0.25 to 1.75
- gain_mlp: float32 [2048], replicated, may hold values from 0.25 to 1.75
- w_query: bfloat16 [2048, 2048], P('fsdp', 'tp'), may hold values from -0.125 to 0.125
- w_key: bfloat16 [2048, 2048], P('fsdp', 'tp'), may hold values from -0.125 to 0.125
- w_value: bfloat16 [2048, 2048], P('fsdp', 'tp'), may hold values from -0.125 to 0.125
- w_out: bfloat16 [2048, 2048], P('fsdp', 'tp'), may hold values from -0.5 to 0.5
- w_gate: bfloat16 [2048, 8192], P('fsdp', 'tp'), may hold values from -0.125 to 0.125
- w_up: bfloat16 [2048, 8192], P('fsdp', 'tp'), may hold values from -0.125 to 0.125
- w_down: bfloat16 [2048, 8192], P('fsdp', 'tp'), may hold values from -0.0625 to 0.0625
- lengths: int32 [16], P('fsdp'), may hold values from 256 to 1024, as said below
- out_grad: bfloat16 [16384, 2048], P(('fsdp', 'tp')), may hold values from -6 to 6
Outputs:
- output: bfloat16 [16384, 2048], P(('fsdp', 'tp'))
- input_grad: bfloat16 [16384, 2048], P(('fsdp', 'tp'))
- gain_attn_grad: float32 [2048], P(('fsdp', 'tp'))
- gain_mlp_grad: float32 [2048], P(('fsdp', 'tp'))
- query_grad: float32 [2048, 2048], P('fsdp', 'tp')
- key_grad: float32 [2048, 2048], P('fsdp', 'tp')
- value_grad: float32 [2048, 2048], P('fsdp', 'tp')
- out_proj_grad: float32 [2048, 2048], P('fsdp', 'tp')
- gate_grad: float32 [2048, 8192], P('fsdp', 'tp')
- up_grad: float32 [2048, 8192], P('fsdp', 'tp')
- down_grad: float32 [2048, 8192], P('fsdp', 'tp')
Inputs may be any that keep to these rules, and one draw needn't show every extreme that they name: `lengths`: valid tokens of each slot, the first ones of the slot; some slot holds exactly 1024.
All inputs are finite; a program needn't handle non-finite values.
Results may differ from a plain program's by a relative error of at most 0.02.
Values may be sent and summed in bfloat16 or wider, within the bound.
A program may use at most 448 MiB of HBM per device.

v0:
```python
import jax
import jax.numpy as jnp
from jax import lax
from jax.sharding import PartitionSpec as P

HD = 64


EPS = 1e-05
THETA = 130000.0
NEGATIVE = -1e30


def matmul(left, right):
    return jnp.dot(left, right, preferred_element_type=jnp.float32)


def matmul_nt(left, right):
    return lax.dot_general(
        left, right, (((1,), (1,)), ((), ())), preferred_element_type=jnp.float32
    )


def matmul_tn(left, right):
    return lax.dot_general(
        left, right, (((0,), (0,)), ((), ())), preferred_element_type=jnp.float32
    )


def inverse_rms(values):
    return lax.rsqrt(jnp.mean(values * values, axis=-1, keepdims=True) + EPS)


def rotary(field, inverse):
    half = HD // 2
    length = field.shape[1]
    places = jnp.arange(length, dtype=jnp.float32)[:, None]
    freqs = 1.0 / THETA ** (jnp.arange(half, dtype=jnp.float32) * 2.0 / HD)
    angle = places * freqs[None, :]
    cosine = jnp.cos(angle)[None, :, None, :]
    sine = jnp.sin(angle)[None, :, None, :]
    if inverse:
        sine = -sine
    first = field[..., :half]
    second = field[..., half:]
    return jnp.concatenate(
        [first * cosine - second * sine, second * cosine + first * sine], axis=-1
    )


def key_mask(lengths, length):
    places = jnp.arange(length, dtype=jnp.int32)
    causal = places[None, :] <= places[:, None]
    live = places[None, :] < lengths[:, None]
    return causal[None, None, :, :] & live[:, None, None, :]


def masked_scores(query, keys, allowed):
    scale = query.shape[-1] ** (-0.5)
    scores = jnp.einsum("cqhd,ckhd->chqk", query, keys, preferred_element_type=jnp.float32) * scale
    return jnp.where(allowed, scores, NEGATIVE)


def attend(query, keys, values, allowed):
    scores = masked_scores(query, keys, allowed)
    top = jnp.max(scores, axis=-1, keepdims=True)
    total = jnp.sum(jnp.exp(scores - top), axis=-1, keepdims=True)
    log_total = top + jnp.log(total)
    probs = jnp.exp(scores - log_total).astype(jnp.bfloat16)
    attended = jnp.einsum("chqk,ckhd->cqhd", probs, values, preferred_element_type=jnp.float32)
    return (attended, log_total)


def attend_back(query, keys, values, allowed, log_total, grad_out):
    scale = query.shape[-1] ** (-0.5)
    probs = jnp.exp(masked_scores(query, keys, allowed) - log_total)
    grad_probs = jnp.einsum("cqhd,ckhd->chqk", grad_out, values, preferred_element_type=jnp.float32)
    centre = jnp.sum(grad_probs * probs, axis=-1, keepdims=True)
    grad_scores = (probs * (grad_probs - centre)).astype(jnp.bfloat16)
    grad_query = (
        jnp.einsum("chqk,ckhd->cqhd", grad_scores, keys, preferred_element_type=jnp.float32) * scale
    )
    grad_key = (
        jnp.einsum("chqk,cqhd->ckhd", grad_scores, query, preferred_element_type=jnp.float32)
        * scale
    )
    grad_value = jnp.einsum(
        "chqk,cqhd->ckhd", probs.astype(jnp.bfloat16), grad_out, preferred_element_type=jnp.float32
    )
    return (
        rotary(grad_query, True).astype(jnp.bfloat16),
        rotary(grad_key, True).astype(jnp.bfloat16),
        grad_value.astype(jnp.bfloat16),
    )


def gather_attention(w_query, w_key, w_value, w_out):
    return (
        lax.all_gather(w_query, "fsdp", axis=0, tiled=True),
        lax.all_gather(w_key, "fsdp", axis=0, tiled=True),
        lax.all_gather(w_value, "fsdp", axis=0, tiled=True),
        lax.all_gather(w_out, "fsdp", axis=0, tiled=True),
    )


def gather_mlp(w_gate, w_up, w_down):
    return (
        lax.all_gather(w_gate, "fsdp", axis=0, tiled=True),
        lax.all_gather(w_up, "fsdp", axis=0, tiled=True),
        lax.all_gather(w_down, "fsdp", axis=0, tiled=True),
    )


def forward(tokens_f, gain_attn, gain_mlp, attn_weights, mlp_weights, lengths):
    w_query, w_key, w_value, w_out = attn_weights
    w_gate, w_up, w_down = mlp_weights
    scale_one = inverse_rms(tokens_f)
    normed_one = tokens_f * scale_one
    rows_one = (normed_one * gain_attn).astype(jnp.bfloat16)
    hidden_one = lax.all_gather(rows_one, "tp", axis=0, tiled=True)
    count = lengths.shape[0]
    group_rows = hidden_one.shape[0]
    length = group_rows // count
    local_heads = w_query.shape[1] // HD

    def heads_of(weight):
        return matmul(hidden_one, weight).reshape(count, length, local_heads, HD)

    query = rotary(heads_of(w_query), False).astype(jnp.bfloat16)
    keys = rotary(heads_of(w_key), False).astype(jnp.bfloat16)
    values = heads_of(w_value).astype(jnp.bfloat16)
    allowed = key_mask(lengths, length)
    attended, log_total = attend(query, keys, values, allowed)
    mixed = attended.astype(jnp.bfloat16).reshape(group_rows, -1)
    attn_out = lax.psum_scatter(matmul_nt(mixed, w_out), "tp", scatter_dimension=0, tiled=True)
    middle = tokens_f + attn_out
    scale_two = inverse_rms(middle)
    normed_two = middle * scale_two
    rows_two = (normed_two * gain_mlp).astype(jnp.bfloat16)
    hidden_two = lax.all_gather(rows_two, "tp", axis=0, tiled=True)
    gate = matmul(hidden_two, w_gate)
    upward = matmul(hidden_two, w_up)
    activated = (jax.nn.silu(gate) * upward).astype(jnp.bfloat16)
    return (
        normed_one,
        scale_one,
        hidden_one,
        query,
        keys,
        values,
        allowed,
        log_total,
        mixed,
        middle,
        normed_two,
        scale_two,
        hidden_two,
        gate,
        upward,
        activated,
    )


def per_device(
    tokens,
    gain_attn,
    gain_mlp,
    w_query,
    w_key,
    w_value,
    w_out,
    w_gate,
    w_up,
    w_down,
    lengths,
    out_grad,
):
    tokens_f = tokens.astype(jnp.float32)
    attn_weights = gather_attention(w_query, w_key, w_value, w_out)
    mlp_weights = gather_mlp(w_gate, w_up, w_down)
    state = forward(tokens_f, gain_attn, gain_mlp, attn_weights, mlp_weights, lengths)
    middle = state[9]
    activated = state[15]
    mlp_out = lax.psum_scatter(
        matmul_nt(activated, mlp_weights[2]).astype(jnp.bfloat16),
        "tp",
        scatter_dimension=0,
        tiled=True,
    ).astype(jnp.float32)
    own_rows = tokens.shape[0]
    count = lengths.shape[0]
    length = own_rows * lax.axis_size("tp") // count
    row_index = lax.axis_index("tp") * own_rows + jnp.arange(own_rows, dtype=jnp.int32)
    slot_index = row_index // length
    slot_length = jnp.sum(
        jnp.where(
            slot_index[:, None] == jnp.arange(count, dtype=jnp.int32)[None, :], lengths[None, :], 0
        ),
        axis=1,
    )
    valid = (row_index % length < slot_length).astype(jnp.float32)[:, None]
    output = (valid * (middle + mlp_out)).astype(jnp.bfloat16)
    held = lax.optimization_barrier(
        (tokens_f, (w_query, w_key, w_value, w_out), (w_gate, w_up, w_down), output)
    )
    attn_weights = gather_attention(*held[1])
    mlp_weights = gather_mlp(*held[2])
    state = forward(held[0], gain_attn, gain_mlp, attn_weights, mlp_weights, lengths)
    (
        normed_one,
        scale_one,
        hidden_one,
        query,
        keys,
        values,
        allowed,
        log_total,
        mixed,
        middle,
        normed_two,
        scale_two,
        hidden_two,
        gate,
        upward,
        activated,
    ) = state
    query_full, key_full, value_full, out_full = attn_weights
    gate_full, up_full, down_full = mlp_weights
    grad_rows = valid * out_grad.astype(jnp.float32)
    grad_mlp = lax.all_gather(grad_rows.astype(jnp.bfloat16), "tp", axis=0, tiled=True)
    grad_hidden = matmul(grad_mlp, down_full)
    down_term = matmul_tn(grad_mlp, activated)
    sigma = jax.nn.sigmoid(gate)
    grad_gate = (grad_hidden * upward * sigma * (1.0 + gate * (1.0 - sigma))).astype(jnp.bfloat16)
    grad_up = (grad_hidden * gate * sigma).astype(jnp.bfloat16)
    gate_term = matmul_tn(hidden_two, grad_gate)
    up_term = matmul_tn(hidden_two, grad_up)
    grad_two = lax.psum_scatter(
        matmul_nt(grad_gate, gate_full) + matmul_nt(grad_up, up_full),
        "tp",
        scatter_dimension=0,
        tiled=True,
    )
    gain_mlp_term = jnp.sum(grad_two * normed_two, axis=0)
    inner_two = grad_two * gain_mlp
    grad_middle = grad_rows + scale_two * (
        inner_two - normed_two * jnp.mean(inner_two * normed_two, axis=-1, keepdims=True)
    )
    grad_attn = lax.all_gather(grad_middle.astype(jnp.bfloat16), "tp", axis=0, tiled=True)
    out_term = matmul_tn(grad_attn, mixed)
    grad_mixed = matmul(grad_attn, out_full).astype(jnp.bfloat16).reshape(query.shape)
    grad_query, grad_key, grad_value = attend_back(
        query, keys, values, allowed, log_total, grad_mixed
    )
    group_rows = hidden_one.shape[0]
    grad_query = grad_query.reshape(group_rows, -1)
    grad_key = grad_key.reshape(group_rows, -1)
    grad_value = grad_value.reshape(group_rows, -1)
    query_term = matmul_tn(hidden_one, grad_query)
    key_term = matmul_tn(hidden_one, grad_key)
    value_term = matmul_tn(hidden_one, grad_value)
    partial_one = (
        matmul_nt(grad_query, query_full)
        + matmul_nt(grad_key, key_full)
        + matmul_nt(grad_value, value_full)
    )
    grad_one = lax.psum_scatter(
        partial_one.astype(jnp.bfloat16), "tp", scatter_dimension=0, tiled=True
    ).astype(jnp.float32)
    gain_attn_term = jnp.sum(grad_one * normed_one, axis=0)
    inner_one = grad_one * gain_attn
    input_grad = (
        grad_middle
        + scale_one
        * (inner_one - normed_one * jnp.mean(inner_one * normed_one, axis=-1, keepdims=True))
    ).astype(jnp.bfloat16)
    attn_grads = (
        lax.psum_scatter(
            query_term.astype(jnp.bfloat16), "fsdp", scatter_dimension=0, tiled=True
        ).astype(jnp.float32),
        lax.psum_scatter(
            key_term.astype(jnp.bfloat16), "fsdp", scatter_dimension=0, tiled=True
        ).astype(jnp.float32),
        lax.psum_scatter(
            value_term.astype(jnp.bfloat16), "fsdp", scatter_dimension=0, tiled=True
        ).astype(jnp.float32),
        lax.psum_scatter(
            out_term.astype(jnp.bfloat16), "fsdp", scatter_dimension=0, tiled=True
        ).astype(jnp.float32),
    )
    mlp_grads = (
        lax.psum_scatter(
            gate_term.astype(jnp.bfloat16), "fsdp", scatter_dimension=0, tiled=True
        ).astype(jnp.float32),
        lax.psum_scatter(
            up_term.astype(jnp.bfloat16), "fsdp", scatter_dimension=0, tiled=True
        ).astype(jnp.float32),
        lax.psum_scatter(
            down_term.astype(jnp.bfloat16), "fsdp", scatter_dimension=0, tiled=True
        ).astype(jnp.float32),
    )
    gain_grads = (
        lax.psum_scatter(gain_attn_term, ("fsdp", "tp"), scatter_dimension=0, tiled=True),
        lax.psum_scatter(gain_mlp_term, ("fsdp", "tp"), scatter_dimension=0, tiled=True),
    )
    return (
        output,
        input_grad,
        gain_grads[0],
        gain_grads[1],
        attn_grads[0],
        attn_grads[1],
        attn_grads[2],
        attn_grads[3],
        mlp_grads[0],
        mlp_grads[1],
        mlp_grads[2],
    )


def solution(mesh):
    placed = (
        P(("fsdp", "tp"), None),
        P(),
        P(),
        P("fsdp", "tp"),
        P("fsdp", "tp"),
        P("fsdp", "tp"),
        P("fsdp", "tp"),
        P("fsdp", "tp"),
        P("fsdp", "tp"),
        P("fsdp", "tp"),
        P("fsdp"),
        P(("fsdp", "tp"), None),
    )
    return jax.shard_map(
        per_device,
        mesh=mesh,
        in_specs=placed,
        out_specs=(
            P(("fsdp", "tp"), None),
            P(("fsdp", "tp"), None),
            P(("fsdp", "tp")),
            P(("fsdp", "tp")),
            P("fsdp", "tp"),
            P("fsdp", "tp"),
            P("fsdp", "tp"),
            P("fsdp", "tp"),
            P("fsdp", "tp"),
            P("fsdp", "tp"),
            P("fsdp", "tp"),
        ),
        check_vma=False,
    )
```

profile of v0, /device:TPU:0, one launch (start us, length us, event | category | flops | bytes accessed | tf_op | source)
XLA Modules:
  0.0 2662.1 jit_solution(6100084873919959131)
XLA Ops:
  18.5 23.0 all-gather.25.cloned.1.call-done
  41.5 89.3 %all-gather.21.cloned.1.call-done = bf16[2048,2048]{1,0:T(8,128)(2,1)} async-done(((bf16[512,2048]{1,0:T(8,128)(2,1)}), bf16[2048,2048]{1,0:T(8,128)(2,1)}) %all-gather.21.cloned.1.call-update) | async-done | bytes 8388624 | tf_op jit(solution)/shard_map/all_gather | solution.py:120
  130.8 10.6 fusion.50
  148.0 13.6 all-gather.27.cloned.1.call-done
  161.6 10.6 fusion.51
  187.7 24.1 fusion
  211.8 22.2 exponential_reduce_fusion.1
  234.1 9.8 convolution_convert_fusion.9
  250.1 28.0 %convert_bitcast_fusion.2 = bf16[2,1024,8,64]{1,3,2,0:T(8,128)(2,1)} fusion(f32[2,8,1024,1024]{2,3,1,0:T(8,128)} %get-tuple-element.71, f32[2,8,1024]{2,1,0:T(8,128)S(1)} %log_add_fusion.1, pred[2,1024,1024]{1,2,0:T(8,128)(4,1)S(1)} %broadcast_and_fusion, bf16[2,1024,8,64]{3,2,1,0:T(8,128)(2,1)} %reshape.263), kind=kOutput, calls=%fused_computation.82 | convolution fusion | flops 2215641088 | bytes 73465856 | tf_op jit(solution)/shard_map/chqk,ckhd->cqhd/dot_general | solution.py:70
  282.5 10.0 fusion.52
  293.3 152.4 %reduce-scatter.13.cloned.1.call-done = f32[512,2048]{1,0:T(8,128)} async-done(((f32[2048,2048]{1,0:T(8,128)}), f32[512,2048]{1,0:T(8,128)}) %reduce-scatter.13.cloned.1.call-update) | async-done | bytes 4194320 | tf_op jit(solution)/shard_map/reduce_scatter | solution.py:135
  452.6 76.8 %all-gather.33.cloned.1.call-done = bf16[2048,2048]{1,0:T(8,128)(2,1)} async-done(((bf16[256,2048]{1,0:T(8,128)(2,1)}), bf16[2048,2048]{1,0:T(8,128)(2,1)}) %all-gather.33.cloned.1.call-update) | async-done | bytes 8388624 | tf_op jit(solution)/shard_map/all_gather | solution.py:108
  529.4 88.4 %all-gather.31.cloned.1.call-done = bf16[2048,2048]{1,0:T(8,128)(2,1)} async-done(((bf16[512,2048]{1,0:T(8,128)(2,1)}), bf16[2048,2048]{1,0:T(8,128)(2,1)}) %all-gather.31.cloned.1.call-update) | async-done | bytes 8388624 | tf_op jit(solution)/shard_map/all_gather | solution.py:140
  617.8 24.2 fusion.53
  642.0 59.5 %all-gather.35.cloned.1.call-done = bf16[2048,2048]{1,0:T(8,128)(2,1)} async-done(((bf16[256,2048]{1,0:T(8,128)(2,1)}), bf16[2048,2048]{1,0:T(8,128)(2,1)}) %all-gather.35.cloned.1.call-update) | async-done | bytes 8388624 | tf_op jit(solution)/shard_map/all_gather | solution.py:109
  701.5 26.1 multiply_convert_fusion.4.clone.4
  727.6 55.9 %all-gather.37.cloned.1.call-done = bf16[2048,2048]{1,0:T(8,128)(2,1)} async-done(((bf16[256,2048]{1,0:T(8,128)(2,1)}), bf16[2048,2048]{1,0:T(8,128)(2,1)}) %all-gather.37.cloned.1.call-update) | async-done | bytes 8388624 | tf_op jit(solution)/shard_map/all_gather | solution.py:110
  783.5 23.9 convolution_convert_fusion.2
  810.2 82.2 %reduce-scatter.15.cloned.1.call-done = bf16[512,2048]{1,0:T(8,128)(2,1)} async-done(((bf16[2048,2048]{1,0:T(8,128)(2,1)}), bf16[512,2048]{1,0:T(8,128)(2,1)}) %reduce-scatter.15.cloned.1.call-update) | async-done | bytes 2097168 | tf_op jit(solution)/shard_map/reduce_scatter | solution.py:184
  892.4 7.3 fusion.15
  906.8 22.3 all-gather.45.cloned.1.call-done
  929.1 89.3 %all-gather.39.cloned.1.call-done = bf16[2048,2048]{1,0:T(8,128)(2,1)} async-done(((bf16[512,2048]{1,0:T(8,128)(2,1)}), bf16[2048,2048]{1,0:T(8,128)(2,1)}) %all-gather.39.cloned.1.call-update) | async-done | bytes 8388624 | tf_op jit(solution)/shard_map/all_gather | solution.py:120
  1018.4 10.7 fusion.55
  1049.0 10.6 fusion.54
  1073.7 24.1 fusion.1
  1097.8 22.0 exponential_reduce_fusion
  1119.8 9.8 convolution_convert_fusion.8
  1141.3 26.0 convert_bitcast_fusion.1
  1171.7 10.5 fusion.56
  1182.9 152.6 %reduce-scatter.17.cloned.1.call-done = f32[512,2048]{1,0:T(8,128)} async-done(((f32[2048,2048]{1,0:T(8,128)}), f32[512,2048]{1,0:T(8,128)}) %reduce-scatter.17.cloned.1.call-update) | async-done | bytes 4194320 | tf_op jit(solution)/shard_map/reduce_scatter | solution.py:135
  1345.5 73.6 %all-gather.55.cloned.1.call-done = bf16[2048,2048]{1,0:T(8,128)(2,1)} async-done(((bf16[256,2048]{1,0:T(8,128)(2,1)}), bf16[2048,2048]{1,0:T(8,128)(2,1)}) %all-gather.55.cloned.1.call-update) | async-done | bytes 8388624 | tf_op jit(solution)/shard_map/all_gather | solution.py:109
  1419.1 88.4 %all-gather.53.cloned.1.call-done = bf16[2048,2048]{1,0:T(8,128)(2,1)} async-done(((bf16[512,2048]{1,0:T(8,128)(2,1)}), bf16[2048,2048]{1,0:T(8,128)(2,1)}) %all-gather.53.cloned.1.call-update) | async-done | bytes 8388624 | tf_op jit(solution)/shard_map/all_gather | solution.py:140
  1507.5 24.2 fusion.57
  1531.7 59.3 %all-gather.57.cloned.1.call-done = bf16[2048,2048]{1,0:T(8,128)(2,1)} async-done(((bf16[256,2048]{1,0:T(8,128)(2,1)}), bf16[2048,2048]{1,0:T(8,128)(2,1)}) %all-gather.57.cloned.1.call-update) | async-done | bytes 8388624 | tf_op jit(solution)/shard_map/all_gather | solution.py:108
  1591.0 24.2 fusion.58
  1615.3 64.2 %all-gather.49.cloned.1.call-done = bf16[2048,2048]{1,0:T(8,128)(2,1)} async-done(((bf16[512,2048]{1,0:T(8,128)(2,1)}), bf16[2048,2048]{1,0:T(8,128)(2,1)}) %all-gather.49.cloned.1.call-update) | async-done | bytes 8388624 | tf_op jit(solution)/shard_map/all_gather | solution.py:230
  1679.4 83.7 %all-gather.51.cloned.1.call-done = bf16[2048,2048]{1,0:T(8,128)(2,1)} async-done(((bf16[256,2048]{1,0:T(8,128)(2,1)}), bf16[2048,2048]{1,0:T(8,128)(2,1)}) %all-gather.51.cloned.1.call-update) | async-done | bytes 8388624 | tf_op jit(solution)/shard_map/all_gather | solution.py:110
  1763.1 32.4 %multiply_convert_fusion.2 = (bf16[2048,2048]{1,0:T(8,128)(2,1)}, bf16[2048,2048]{1,0:T(8,128)(2,1)}) fusion(f32[2048,2048]{1,0:T(8,128)} %fusion.58, f32[2048,2048]{1,0:T(8,128)} %fusion.57, bf16[2048,2048]{1,0:T(8,128)(2,1)} %all-gather.49.cloned.1.call-done, bf16[2048,2048]{1,0:T(8,128)(2,1)} %all-gather.51.cloned.1.call-done), kind=kOutput, calls=%fused_computation.15 | convolution fusion | flops 17234395136 | bytes 67108864 | tf_op jit(solution)/shard_map/dot_general | solution.py:15
  1795.5 24.4 fusion.59
  1819.8 26.5 convolution_add_fusion
  1846.4 152.3 %reduce-scatter.19.cloned.1.call-done = f32[512,2048]{1,0:T(8,128)} async-done(((f32[2048,2048]{1,0:T(8,128)}), f32[512,2048]{1,0:T(8,128)}) %reduce-scatter.19.cloned.1.call-update) | async-done | bytes 4194320 | tf_op jit(solution)/shard_map/reduce_scatter | solution.py:238
  2008.3 26.1 fusion.6
  2034.5 24.2 convolution_convert_fusion
  2058.8 23.8 convolution_convert_fusion.1
  2082.8 13.1 all-gather.59.cloned.1.call-done
  2095.9 8.5 convolution_convert_fusion.7
  2113.5 10.1 convolution_convert_fusion.3
  2123.6 50.7 %multiply_reduce_fusion = (f32[2,8,1024]{2,1,0:T(8,128)S(1)}, f32[2,8,1024,1024]{2,3,1,0:T(8,128)}) fusion(f32[2,8,1024,1024]{2,3,1,0:T(8,128)} %get-tuple-element.73, f32[2,8,1024]{2,1,0:T(8,128)S(1)} %copy-done.19, pred[2,1024,1024]{1,2,0:T(8,128)(4,1)S(1)} %copy-done.3, bf16[2,1024,8,64]{1,3,2,0:T(8,128)(2,1)} %copy.118, bf16[2,1024,8,64]{1,3,2,0:T(8,128)(2,1)} %copy.114), kind=kOutput, calls=%fused_computation.1 | convolution fusion | flops 2231353344 | bytes 140640256 | tf_op jit(solution)/shard_map/cqhd,ckhd->chqk/dot_general | solution.py:77
  2174.4 55.7 %multiply_convert_fusion = bf16[2,8,1024,1024]{2,3,1,0:T(8,128)(2,1)} fusion(f32[2,8,1024,1024]{2,3,1,0:T(8,128)} %get-tuple-element.75, f32[2,8,1024,1024]{2,3,1,0:T(8,128)} %get-tuple-element.73, f32[2,8,1024]{2,1,0:T(8,128)S(1)} %get-tuple-element.74, f32[2,8,1024]{2,1,0:T(8,128)S(1)} %copy-done.19, pred[2,1024,1024]{1,2,0:T(8,128)(4,1)S(1)} %copy-done.3), kind=kLoop, calls=%fused_computation | loop fusion | flops 100663296 | bytes 170000384 | tf_op jit(solution)/shard_map/convert_element_type | solution.py:79
  2230.1 26.7 %convert_bitcast_fusion = bf16[2,1024,8,64]{1,3,2,0:T(8,128)(2,1)} fusion(bf16[2,1024,8,64]{1,3,2,0:T(8,128)(2,1)} %copy.118, f32[2,8,1024,1024]{2,3,1,0:T(8,128)} %get-tuple-element.73, f32[2,8,1024]{2,1,0:T(8,128)S(1)} %copy-done.19, pred[2,1024,1024]{1,2,0:T(8,128)(4,1)S(1)} %copy-done.3), kind=kOutput, calls=%fused_computation.72 | convolution fusion | flops 2215641088 | bytes 73465856 | tf_op jit(solution)/shard_map/chqk,cqhd->ckhd/dot_general | solution.py:87
  2261.2 9.7 convolution_convert_fusion.4
  2270.9 19.4 multiply_bitcast_fusion.1
  2290.5 18.1 multiply_bitcast_fusion
  2318.8 9.6 convolution_convert_fusion.5
  2334.1 9.5 convolution_convert_fusion.6
  2343.8 12.8 fusion.61
  2356.6 8.2 fusion.60
  2364.8 17.2 add_convert_fusion
  2390.5 14.5 reduce-scatter.29.cloned.1.call-done
  2406.8 35.2 %reduce-scatter.27.cloned.1.call-done = bf16[256,512]{1,0:T(8,128)(2,1)} async-done(((bf16[2048,512]{1,0:T(8,128)(2,1)}), bf16[256,512]{1,0:T(8,128)(2,1)}) %reduce-scatter.27.cloned.1.call-update) | async-done | bytes 262160 | tf_op jit(solution)/shard_map/reduce_scatter | solution.py:284
  2443.8 35.1 %reduce-scatter.25.cloned.1.call-done = bf16[256,512]{1,0:T(8,128)(2,1)} async-done(((bf16[2048,512]{1,0:T(8,128)(2,1)}), bf16[256,512]{1,0:T(8,128)(2,1)}) %reduce-scatter.25.cloned.1.call-update) | async-done | bytes 262160 | tf_op jit(solution)/shard_map/reduce_scatter | solution.py:281
  2480.7 35.8 %reduce-scatter.23.cloned.1.call-done = bf16[256,512]{1,0:T(8,128)(2,1)} async-done(((bf16[2048,512]{1,0:T(8,128)(2,1)}), bf16[256,512]{1,0:T(8,128)(2,1)}) %reduce-scatter.23.cloned.1.call-update) | async-done | bytes 262160 | tf_op jit(solution)/shard_map/reduce_scatter | solution.py:278
  2518.3 86.2 %reduce-scatter.21.cloned.1.call-done = bf16[512,2048]{1,0:T(8,128)(2,1)} async-done(((bf16[2048,2048]{1,0:T(8,128)(2,1)}), bf16[512,2048]{1,0:T(8,128)(2,1)}) %reduce-scatter.21.cloned.1.call-update) | async-done | bytes 2097168 | tf_op jit(solution)/shard_map/reduce_scatter | solution.py:267
  2608.7 39.5 %all-reduce.2 = (f32[2048]{0:T(1024)S(1)}, f32[2048]{0:T(1024)S(1)}) all-reduce(f32[2048]{0:T(1024)S(1)} %get-tuple-element.29, f32[2048]{0:T(1024)S(1)} %copy-done.37), channel_id=7, replica_groups=mesh['fsdp'=8,'tp'=4] {'fsdp','tp'}, use_global_device_ids=true, to_apply=%region_18.19.clone | all-reduce | flops 4096 | bytes 32768
  (227 shorter events, 187.9 us)
Async XLA Ops:
  7.2 34.3 %all-gather.25.cloned.1.call-start = ((), (), s32[]{:S(2)}) async-start(), calls=%async_computation.14 | async-start | bytes 2359296 | tf_op jit(solution)/shard_map/all_gather | solution.py:99
  7.9 122.9 %all-gather.21.cloned.1.call-start = ((), (), s32[]{:S(2)}) async-start(), calls=%async_computation.12 | async-start | bytes 10485760 | tf_op jit(solution)/shard_map/all_gather | solution.py:120
  10.0 7.0 copy-start.42
  13.5 148.1 %all-gather.27.cloned.1.call-start = ((), (), s32[]{:S(2)}) async-start(), calls=%async_computation.15 | async-start | bytes 2359296 | tf_op jit(solution)/shard_map/all_gather | solution.py:100
  14.3 219.8 %all-gather.23.cloned.1.call-start = ((), (), s32[]{:S(2)}) async-start(), calls=%async_computation.13 | async-start | bytes 2359296 | tf_op jit(solution)/shard_map/all_gather | solution.py:101
  14.9 267.6 %all-gather.29.cloned.1.call-start = ((), (), s32[]{:S(2)}) async-start(), calls=%async_computation.16 | async-start | bytes 2359296 | tf_op jit(solution)/shard_map/all_gather | solution.py:102
  15.4 430.3 %reduce-scatter.13.cloned.1.call-start = ((), (), s32[]{:S(2)}) async-start(), calls=%async_computation.17 | async-start | bytes 20971520 | tf_op jit(solution)/shard_map/reduce_scatter | solution.py:135
  17.0 167.4 %copy-start.20 = (f32[1024,32]{0,1:T(8,128)}, f32[1024,32]{0,1:T(8,128)S(1)}, u32[]{:S(2)}) copy-start(f32[1024,32]{0,1:T(8,128)S(1)} %get-tuple-element.69) | copy-start | bytes 393220
  17.0 167.4 %copy-start.27 = (f32[1024,32]{0,1:T(8,128)}, f32[1024,32]{0,1:T(8,128)S(1)}, u32[]{:S(2)}) copy-start(f32[1024,32]{0,1:T(8,128)S(1)} %get-tuple-element.68) | copy-start | bytes 393220
  18.5 231.6 %copy-start.1 = (pred[2,1024,1024]{1,2,0:T(8,128)(4,1)}, pred[2,1024,1024]{1,2,0:T(8,128)(4,1)S(1)}, u32[]{:S(2)}) copy-start(pred[2,1024,1024]{1,2,0:T(8,128)(4,1)S(1)} %broadcast_and_fusion) | copy-start | bytes 6291460
  292.5 153.3 %copy-start.4 = (bf16[512,2048]{1,0:T(8,128)(2,1)S(1)}, bf16[512,2048]{1,0:T(8,128)(2,1)}, u32[]{:S(2)}) copy-start(bf16[512,2048]{1,0:T(8,128)(2,1)} %param.12) | copy-start | bytes 6291460
  292.5 156.2 %copy-start.32 = (f32[2048]{0:T(1024)S(1)}, f32[2048]{0:T(1024)}, u32[]{:S(2)}) copy-start(f32[2048]{0:T(1024)} %param.14) | copy-start | bytes 24580
  292.5 236.9 %all-gather.33.cloned.1.call-start = ((), (), s32[]{:S(2)}) async-start(), calls=%async_computation.19 | async-start | bytes 9437184 | tf_op jit(solution)/shard_map/all_gather | solution.py:108
  293.2 324.6 %all-gather.31.cloned.1.call-start = ((), (), s32[]{:S(2)}) async-start(), calls=%async_computation.18 | async-start | bytes 10485760 | tf_op jit(solution)/shard_map/all_gather | solution.py:140
  451.3 250.2 %all-gather.35.cloned.1.call-start = ((), (), s32[]{:S(2)}) async-start(), calls=%async_computation.20 | async-start | bytes 9437184 | tf_op jit(solution)/shard_map/all_gather | solution.py:109
  452.0 331.5 %all-gather.37.cloned.1.call-start = ((), (), s32[]{:S(2)}) async-start(), calls=%async_computation.21 | async-start | bytes 9437184 | tf_op jit(solution)/shard_map/all_gather | solution.py:110
  452.6 439.8 %reduce-scatter.15.cloned.1.call-start = ((), (), s32[]{:S(2)}) async-start(), calls=%async_computation.22 | async-start | bytes 10485760 | tf_op jit(solution)/shard_map/reduce_scatter | solution.py:184
  807.5 121.6 %all-gather.45.cloned.1.call-start = ((), (), s32[]{:S(2)}) async-start(), calls=%async_computation.26 | async-start | bytes 2359296 | tf_op jit(solution)/shard_map/all_gather | solution.py:100
  810.2 89.6 %copy-start.40 = (f32[512]{0:T(512)}, f32[512]{0:T(512)S(1)}, u32[]{:S(2)}) copy-start(f32[512]{0:T(512)S(1)} %fusion.33) | copy-start | bytes 6148
  899.8 118.6 %all-gather.39.cloned.1.call-start = ((), (), s32[]{:S(2)}) async-start(), calls=%async_computation.23 | async-start | bytes 10485760 | tf_op jit(solution)/shard_map/all_gather | solution.py:120
  905.0 144.0 %all-gather.43.cloned.1.call-start = ((), (), s32[]{:S(2)}) async-start(), calls=%async_computation.25 | async-start | bytes 2359296 | tf_op jit(solution)/shard_map/all_gather | solution.py:99
  905.6 214.2 %all-gather.41.cloned.1.call-start = ((), (), s32[]{:S(2)}) async-start(), calls=%async_computation.24 | async-start | bytes 2359296 | tf_op jit(solution)/shard_map/all_gather | solution.py:101
  906.2 265.5 %all-gather.47.cloned.1.call-start = ((), (), s32[]{:S(2)}) async-start(), calls=%async_computation.27 | async-start | bytes 2359296 | tf_op jit(solution)/shard_map/all_gather | solution.py:102
  906.8 428.8 %reduce-scatter.17.cloned.1.call-start = ((), (), s32[]{:S(2)}) async-start(), calls=%async_computation.28 | async-start | bytes 20971520 | tf_op jit(solution)/shard_map/reduce_scatter | solution.py:135
  1066.4 3.9 copy-start.11
  1073.6 24.2 copy-start.13
  1073.6 24.2 copy-start.15
  1073.6 24.2 copy-start.16
  1073.6 24.2 copy-start.17
  1141.3 26.0 copy-start.18
  1171.7 10.6 copy-start.23
  1182.3 236.8 %all-gather.55.cloned.1.call-start = ((), (), s32[]{:S(2)}) async-start(), calls=%async_computation.32 | async-start | bytes 9437184 | tf_op jit(solution)/shard_map/all_gather | solution.py:109
  1182.9 158.8 %copy-start.33 = (f32[2048]{0:T(1024)S(1)}, f32[2048]{0:T(1024)}, u32[]{:S(2)}) copy-start(f32[2048]{0:T(1024)} %param.14) | copy-start | bytes 24580
  1182.9 324.6 %all-gather.53.cloned.1.call-start = ((), (), s32[]{:S(2)}) async-start(), calls=%async_computation.31 | async-start | bytes 10485760 | tf_op jit(solution)/shard_map/all_gather | solution.py:140
  1343.4 247.6 %all-gather.57.cloned.1.call-start = ((), (), s32[]{:S(2)}) async-start(), calls=%async_computation.33 | async-start | bytes 9437184 | tf_op jit(solution)/shard_map/all_gather | solution.py:108
  1344.0 335.5 %all-gather.49.cloned.1.call-start = ((), (), s32[]{:S(2)}) async-start(), calls=%async_computation.29 | async-start | bytes 10485760 | tf_op jit(solution)/shard_map/all_gather | solution.py:230
  1344.7 418.4 %all-gather.51.cloned.1.call-start = ((), (), s32[]{:S(2)}) async-start(), calls=%async_computation.30 | async-start | bytes 9437184 | tf_op jit(solution)/shard_map/all_gather | solution.py:110
  1345.5 653.3 %reduce-scatter.19.cloned.1.call-start = ((), (), s32[]{:S(2)}) async-start(), calls=%async_computation.34 | async-start | bytes 20971520 | tf_op jit(solution)/shard_map/reduce_scatter | solution.py:238
  1846.3 152.4 %copy-start.34 = (f32[2048]{0:T(1024)S(1)}, f32[2048]{0:T(1024)}, u32[]{:S(2)}) copy-start(f32[2048]{0:T(1024)} %param.14) | copy-start | bytes 24580
  1846.3 152.4 %copy-start.39 = (f32[512]{0:T(512)S(1)}, f32[512]{0:T(512)}, u32[]{:S(2)}) copy-start(f32[512]{0:T(512)} %copy-done.38) | copy-start | bytes 6148
  1846.3 157.6 %copy-start.9 = (bf16[512,2048]{1,0:T(8,128)(2,1)S(1)}, bf16[512,2048]{1,0:T(8,128)(2,1)}, u32[]{:S(2)}) copy-start(bf16[512,2048]{1,0:T(8,128)(2,1)} %param.23) | copy-start | bytes 6291460
  1846.4 157.6 %copy-start.41 = (f32[512]{0:T(512)S(1)}, f32[512]{0:T(512)}, u32[]{:S(2)}) copy-start(f32[512]{0:T(512)} %copy-done.40) | copy-start | bytes 6148
  1846.4 249.6 %all-gather.59.cloned.1.call-start = ((), (), s32[]{:S(2)}) async-start(), calls=%async_computation.35 | async-start | bytes 10485760 | tf_op jit(solution)/shard_map/all_gather | solution.py:249
  1998.7 5.2 copy-start.6
  1998.7 5.9 copy-start.8
  2008.3 373.8 %reduce-scatter.35.cloned.1.call-start = ((), (), s32[]{:S(2)}) async-start(), calls=%async_computation.43 | async-start | bytes 9437184 | tf_op jit(solution)/shard_map/reduce_scatter | solution.py:298
  2034.5 350.4 %reduce-scatter.33.cloned.1.call-start = ((), (), s32[]{:S(2)}) async-start(), calls=%async_computation.42 | async-start | bytes 9437184 | tf_op jit(solution)/shard_map/reduce_scatter | solution.py:295
  2058.7 328.9 %reduce-scatter.31.cloned.1.call-start = ((), (), s32[]{:S(2)}) async-start(), calls=%async_computation.41 | async-start | bytes 9437184 | tf_op jit(solution)/shard_map/reduce_scatter | solution.py:292
  2082.6 322.3 %reduce-scatter.29.cloned.1.call-start = ((), (), s32[]{:S(2)}) async-start(), calls=%async_computation.40 | async-start | bytes 2359296 | tf_op jit(solution)/shard_map/reduce_scatter | solution.py:287
  2113.5 10.2 copy-start.3
  2113.5 10.2 copy-start.19
  2174.3 267.6 %reduce-scatter.27.cloned.1.call-start = ((), (), s32[]{:S(2)}) async-start(), calls=%async_computation.39 | async-start | bytes 2359296 | tf_op jit(solution)/shard_map/reduce_scatter | solution.py:284
  2270.9 19.6 copy-start.14
  2290.4 18.2 copy-start.22
  2290.4 18.2 copy-start.29
  2290.4 188.5 %reduce-scatter.25.cloned.1.call-start = ((), (), s32[]{:S(2)}) async-start(), calls=%async_computation.38 | async-start | bytes 2359296 | tf_op jit(solution)/shard_map/reduce_scatter | solution.py:281
  2328.4 188.1 %reduce-scatter.23.cloned.1.call-start = ((), (), s32[]{:S(2)}) async-start(), calls=%async_computation.37 | async-start | bytes 2359296 | tf_op jit(solution)/shard_map/reduce_scatter | solution.py:278
  2343.7 260.8 %reduce-scatter.21.cloned.1.call-start = ((), (), s32[]{:S(2)}) async-start(), calls=%async_computation.36 | async-start | bytes 10485760 | tf_op jit(solution)/shard_map/reduce_scatter | solution.py:267
  2343.8 12.8 copy-start.26
  2343.8 12.8 copy-start.44
  2384.9 219.6 %copy-start.31 = (f32[2048]{0:T(1024)S(1)}, f32[2048]{0:T(1024)}, u32[]{:S(2)}) copy-start(f32[2048]{0:T(1024)} %param.13) | copy-start | bytes 24580
  2384.9 219.6 %copy-start.36 = (f32[512]{0:T(512)S(1)}, f32[512]{0:T(512)}, u32[]{:S(2)}) copy-start(f32[512]{0:T(512)} %copy-done.35) | copy-start | bytes 6148
  2406.8 201.9 %copy-start.37 = (f32[2048]{0:T(1024)S(1)}, f32[2048]{0:T(1024)}, u32[]{:S(2)}) copy-start(f32[2048]{0:T(1024)} %get-tuple-element.27) | copy-start | bytes 24580
  2604.5 44.8 %copy-start.10 = (bf16[512,2048]{1,0:T(8,128)(2,1)S(1)}, bf16[512,2048]{1,0:T(8,128)(2,1)}, u32[]{:S(2)}) copy-start(bf16[512,2048]{1,0:T(8,128)(2,1)} %reduce-scatter.21.cloned.1.call-done) | copy-start | bytes 6291460
  (13 other events, 35.1 us)
Sparse Core Ops, SparseCore 0:
  9.6 31.8 all-gather.24
  43.9 86.8 all-gather.20
  132.4 29.1 all-gather.26
  163.1 28.5 all-gather.22
  193.1 28.5 all-gather.28
  292.6 153.0 reduce-scatter.12
  447.3 82.0 all-gather.32
  531.8 85.9 all-gather.30
  619.4 82.0 all-gather.34
  702.9 80.5 all-gather.36
  807.6 84.7 reduce-scatter.14
  899.9 29.1 all-gather.44
  931.5 86.8 all-gather.38
  1019.9 29.1 all-gather.42
  1050.5 28.5 all-gather.40
  1080.5 28.5 all-gather.46
  1182.4 153.0 reduce-scatter.16
  1337.0 82.0 all-gather.54
  1421.5 85.9 all-gather.52
  1508.9 82.0 all-gather.56
  1593.4 85.9 all-gather.48
  1681.0 82.0 all-gather.50
  1846.5 152.1 reduce-scatter.18
  2008.4 87.4 all-gather.58
  2098.2 89.5 reduce-scatter.34
  2189.9 87.9 reduce-scatter.32
  2280.1 88.0 reduce-scatter.30
  2370.4 34.5 reduce-scatter.28
  2407.3 34.6 reduce-scatter.26
  2444.1 34.7 reduce-scatter.24
  2481.7 34.6 reduce-scatter.22
  2519.5 84.9 reduce-scatter.20
where the time goes:
time: 2670 us; the launch traced here: 2660 us
  waiting for transfers between devices  1660 us (62%)
  matrix products  666 us (25%)
  other arithmetic  182 us (7%)
  local copies, waits for them, and re-layouts  95.9 us (4%)
  blocking collectives  39.5 us (1%)
    reduce_scatter x2, waiting for transfers between devices, forward(): lax.psum_scatter(matmul_nt(mixed, w_out), 'tp', scatter_dimension=0, tile...  305 us
    dot_general x12, matrix products, matmul(): return jnp.dot(left, right, preferred_element_type=jnp.float32)  202 us
    all_gather x2, waiting for transfers between devices, forward(): hidden_one = lax.all_gather(rows_one, 'tp', axis=0, tiled=True)  179 us
    all_gather x2, waiting for transfers between devices, forward(): hidden_two = lax.all_gather(rows_two, 'tp', axis=0, tiled=True)  177 us
    reduce_scatter x1, waiting for transfers between devices, per_device(): lax.psum_scatter(matmul_nt(grad_gate, gate_full) + matmul_nt(grad_up, up_...  152 us
    all_gather x2, waiting for transfers between devices, gather_mlp(): lax.all_gather(w_down, 'fsdp', axis=0, tiled=True)  140 us
    all_gather x2, waiting for transfers between devices, gather_mlp(): lax.all_gather(w_gate, 'fsdp', axis=0, tiled=True)  136 us
    dot_general x8, matrix products, matmul_nt(): lax.dot_general(left, right, (((1,), (1,)), ((), ())), preferred_element_...  134 us
  transfers between devices with their start and end apart: 32, of which 25 were waited for; matrix products, arithmetic and copies ran while one was open for 29% of the time, Pallas kernels for 0%

commit v1 on v0

v1 whole, which is shorter than its diff:
```python
import functools

import jax
import jax.numpy as jnp
from jax import lax
from jax.experimental import pallas as pl
from jax.experimental.pallas import tpu as pltpu
from jax.sharding import PartitionSpec as P

HD = 64
EPS = 1e-05
THETA = 130000.0
NEGATIVE = -1e30
QB = 256
LANES = 128
BF16 = jnp.bfloat16
F32 = jnp.float32


def matmul(left, right):
    return jnp.dot(left, right, preferred_element_type=F32)


def matmul_nt(left, right):
    return lax.dot_general(left, right, (((1,), (1,)), ((), ())), preferred_element_type=F32)


def matmul_tn(left, right):
    return lax.dot_general(left, right, (((0,), (0,)), ((), ())), preferred_element_type=F32)


def inverse_rms(values):
    return lax.rsqrt(jnp.mean(values * values, axis=-1, keepdims=True) + EPS)


def rotary_tables(length):
    half = HD // 2
    places = jnp.arange(length, dtype=F32)[:, None]
    freqs = 1.0 / THETA ** (jnp.arange(half, dtype=F32) * 2.0 / HD)
    angle = places * freqs[None, :]
    cosine, sine = jnp.cos(angle), jnp.sin(angle)
    return (
        jnp.concatenate([cosine] * 4, axis=1),
        jnp.concatenate([-sine, sine, -sine, sine], axis=1),
    )


def turn(field, cosine, sine):
    lane = lax.broadcasted_iota(jnp.int32, field.shape, 1)
    swapped = jnp.where(lane % HD < HD // 2, pltpu.roll(field, LANES - HD // 2, 1), pltpu.roll(field, HD // 2, 1))
    return field * cosine + swapped * sine


def head_lanes(rows, head):
    lane = lax.broadcasted_iota(jnp.int32, (rows, LANES), 1)
    return (lane // HD) == head


def only(values, keep):
    return jnp.where(keep, values, jnp.zeros_like(values))


def place_of(block, own, flip):
    piece, rest = divmod(block * QB, own)
    return pl.multiple_of((piece ^ flip) * own + rest, QB)


def diag_mask(block, live):
    row = lax.broadcasted_iota(jnp.int32, (QB, QB), 0)
    col = lax.broadcasted_iota(jnp.int32, (QB, QB), 1)
    return (col <= row) & (col + block * QB < live)


def attend_kernel(own, info, q_ref, k_ref, v_ref, cos_ref, sin_ref, qo, ko, vo, ao, qs, ks, vs):
    length = q_ref.shape[0]
    live, flip = info[0], info[1]
    for b in range(length // QB):
        rows = pl.ds(place_of(b, own, flip), QB)
        here = pl.ds(b * QB, QB)
        cosine, sine = cos_ref[here, :], sin_ref[here, :]
        query = (turn(q_ref[rows, :], cosine, sine) * HD ** (-0.5)).astype(BF16)
        key = turn(k_ref[rows, :], cosine, sine).astype(BF16)
        value = v_ref[rows, :].astype(BF16)
        qo[rows, :] = query
        ko[rows, :] = key
        vo[rows, :] = value
        qs[here, :] = query
        ks[here, :] = key
        vs[here, :] = value
    for b in range(length // QB):
        rows = pl.ds(place_of(b, own, flip), QB)

        @pl.when(b * QB < live)
        def _():
            allowed = diag_mask(b, live)
            outs = []
            for head in range(2):
                query = only(qs[pl.ds(b * QB, QB), :], head_lanes(QB, head))
                diag = matmul_nt(query, ks[pl.ds(b * QB, QB), :])
                diag = jnp.where(allowed, diag, NEGATIVE)
                top = jnp.max(diag, axis=1, keepdims=True)
                if b:
                    past = matmul_nt(query, ks[pl.ds(0, b * QB), :])
                    top = jnp.maximum(top, jnp.max(past, axis=1, keepdims=True))
                diag = jnp.exp(diag - top)
                total = jnp.sum(diag, axis=1, keepdims=True)
                mixed = matmul(diag.astype(BF16), vs[pl.ds(b * QB, QB), :])
                if b:
                    past = jnp.exp(past - top)
                    total = total + jnp.sum(past, axis=1, keepdims=True)
                    mixed = mixed + matmul(past.astype(BF16), vs[pl.ds(0, b * QB), :])
                outs.append(mixed / total)
            ao[rows, :] = jnp.where(head_lanes(QB, 0), outs[0], outs[1]).astype(BF16)

        @pl.when(b * QB >= live)
        def _():
            ao[rows, :] = jnp.zeros((QB, LANES), BF16)


def attend(qkv, slot, info, cosine, sine, own, length):
    width = qkv.shape[1] // 3
    pairs = width // LANES
    wide = jax.ShapeDtypeStruct((length, width), BF16)

    def column(third):
        return pl.BlockSpec((length, LANES), lambda i, s: (slot, third * pairs + i))

    whole = pl.BlockSpec((length, LANES), lambda i, s: (0, 0))
    out = pl.BlockSpec((length, LANES), lambda i, s: (0, i))
    return pl.pallas_call(
        functools.partial(attend_kernel, own),
        out_shape=[wide] * 4,
        grid_spec=pltpu.PrefetchScalarGridSpec(
            num_scalar_prefetch=1,
            grid=(pairs,),
            in_specs=[column(0), column(1), column(2), whole, whole],
            out_specs=[out] * 4,
            scratch_shapes=[pltpu.VMEM((length, LANES), BF16)] * 3,
        ),
        compiler_params=pltpu.CompilerParams(dimension_semantics=("arbitrary",)),
        cost_estimate=pl.CostEstimate(
            flops=8 * length * length * width, bytes_accessed=20 * length * width, transcendentals=0
        ),
        name="attend",
    )(info, qkv, qkv, qkv, cosine, sine)


def attend_back_kernel(own, info, q_ref, k_ref, v_ref, g_ref, cos_ref, sin_ref, out, qs, ks, vs, gs, dq, dk, dv):
    length = q_ref.shape[0]
    width = out.shape[1] // 3
    live, flip = info[0], info[1]
    pair = pl.program_id(0)
    for b in range(length // QB):
        rows = pl.ds(place_of(b, own, flip), QB)
        here = pl.ds(b * QB, QB)
        qs[here, :] = q_ref[rows, :]
        ks[here, :] = k_ref[rows, :]
        vs[here, :] = v_ref[rows, :]
        gs[here, :] = g_ref[rows, :]
    dq[...] = jnp.zeros_like(dq)
    dk[...] = jnp.zeros_like(dk)
    dv[...] = jnp.zeros_like(dv)
    for b in range(length // QB):

        @pl.when(b * QB < live)
        def _():
            here = pl.ds(b * QB, QB)
            allowed = diag_mask(b, live)
            for head in range(2):
                keep = head_lanes(QB, head)
                query = only(qs[here, :], keep)
                grad = only(gs[here, :], keep)
                diag = jnp.where(allowed, matmul_nt(query, ks[here, :]), NEGATIVE)
                top = jnp.max(diag, axis=1, keepdims=True)
                if b:
                    before = pl.ds(0, b * QB)
                    past = matmul_nt(query, ks[before, :])
                    top = jnp.maximum(top, jnp.max(past, axis=1, keepdims=True))
                diag = jnp.exp(diag - top)
                total = jnp.sum(diag, axis=1, keepdims=True)
                if b:
                    past = jnp.exp(past - top)
                    total = total + jnp.sum(past, axis=1, keepdims=True)
                scale = 1.0 / total
                diag = diag * scale
                diag_dp = matmul_nt(grad, vs[here, :])
                centre = jnp.sum(diag * diag_dp, axis=1, keepdims=True)
                if b:
                    past = past * scale
                    past_dp = matmul_nt(grad, vs[before, :])
                    centre = centre + jnp.sum(past * past_dp, axis=1, keepdims=True)
                diag_ds = (diag * (diag_dp - centre)).astype(BF16)
                dq_b = matmul(diag_ds, only(ks[here, :], keep))
                dk[here, :] += matmul_tn(diag_ds, query)
                dv[here, :] += matmul_tn(diag.astype(BF16), grad)
                if b:
                    past_ds = (past * (past_dp - centre)).astype(BF16)
                    dq_b = dq_b + matmul(past_ds, only(ks[before, :], head_lanes(b * QB, head)))
                    dk[before, :] += matmul_tn(past_ds, query)
                    dv[before, :] += matmul_tn(past.astype(BF16), grad)
                dq[here, :] += dq_b

    for b in range(length // QB):
        rows = pl.ds(place_of(b, own, flip), QB)
        here = pl.ds(b * QB, QB)
        cosine, sine = cos_ref[here, :], -sin_ref[here, :]

        def columns(third):
            return pl.ds(pl.multiple_of(third * width + pair * LANES, LANES), LANES)

        out[rows, columns(0)] = turn(dq[here, :] * HD ** (-0.5), cosine, sine).astype(BF16)
        out[rows, columns(1)] = turn(dk[here, :], cosine, sine).astype(BF16)
        out[rows, columns(2)] = dv[here, :].astype(BF16)


def attend_back(query, keys, values, grad, slot, info, cosine, sine, own, length):
    width = query.shape[1]
    pairs = width // LANES
    block = pl.BlockSpec((length, LANES), lambda i, s: (0, i))
    block_grad = pl.BlockSpec((length, LANES), lambda i, s: (slot, i))
    whole = pl.BlockSpec((length, LANES), lambda i, s: (0, 0))
    return pl.pallas_call(
        functools.partial(attend_back_kernel, own),
        out_shape=jax.ShapeDtypeStruct((length, 3 * width), BF16),
        grid_spec=pltpu.PrefetchScalarGridSpec(
            num_scalar_prefetch=1,
            grid=(pairs,),
            in_specs=[block, block, block, block_grad, whole, whole],
            out_specs=pl.BlockSpec((length, 3 * width), lambda i, s: (0, 0)),
            scratch_shapes=[pltpu.VMEM((length, LANES), BF16)] * 4 + [pltpu.VMEM((length, LANES), F32)] * 3,
        ),
        compiler_params=pltpu.CompilerParams(dimension_semantics=("arbitrary",)),
        cost_estimate=pl.CostEstimate(
            flops=20 * length * length * width, bytes_accessed=20 * length * width, transcendentals=0
        ),
        name="attend_back",
    )(info, query, keys, values, grad, cosine, sine)


def gate_up_kernel(h_ref, g_ref, u_ref, hid_ref, gate_slope, up_slope):
    gate = matmul(h_ref[...], g_ref[...])
    upward = matmul(h_ref[...], u_ref[...])
    sigma = 1.0 / (1.0 + jnp.exp(-gate))
    silu = gate * sigma
    hid_ref[...] = (silu * upward).astype(BF16)
    gate_slope[...] = (upward * sigma * (1.0 + gate * (1.0 - sigma))).astype(BF16)
    up_slope[...] = silu.astype(BF16)


def tile(extent, most):
    return min(extent, most)


def gate_up(hidden, w_gate, w_up):
    rows, depth = hidden.shape
    width = w_gate.shape[1]
    bm, bn = tile(rows, 512), tile(width, 512)
    weight = pl.BlockSpec((depth, bn), lambda j, i: (0, j))
    out = pl.BlockSpec((bm, bn), lambda j, i: (i, j))
    return pl.pallas_call(
        gate_up_kernel,
        out_shape=[jax.ShapeDtypeStruct((rows, width), BF16)] * 3,
        grid=(width // bn, rows // bm),
        in_specs=[pl.BlockSpec((bm, depth), lambda j, i: (i, 0)), weight, weight],
        out_specs=[out] * 3,
        cost_estimate=pl.CostEstimate(
            flops=4 * rows * depth * width, bytes_accessed=2 * (rows * depth + 2 * depth * width + 3 * rows * width), transcendentals=0
        ),
        name="gate_up",
    )(hidden, w_gate, w_up)


def hidden_back_kernel(g_ref, w_ref, gate_slope, up_slope, gate_out, up_out):
    grad = matmul(g_ref[...], w_ref[...])
    gate_out[...] = (grad * gate_slope[...].astype(F32)).astype(BF16)
    up_out[...] = (grad * up_slope[...].astype(F32)).astype(BF16)


def hidden_back(grad, w_down, gate_slope, up_slope):
    rows, depth = grad.shape
    width = w_down.shape[1]
    bm, bn = tile(rows, 512), tile(width, 512)
    out = pl.BlockSpec((bm, bn), lambda j, i: (i, j))
    return pl.pallas_call(
        hidden_back_kernel,
        out_shape=[jax.ShapeDtypeStruct((rows, width), BF16)] * 2,
        grid=(width // bn, rows // bm),
        in_specs=[
            pl.BlockSpec((bm, depth), lambda j, i: (i, 0)),
            pl.BlockSpec((depth, bn), lambda j, i: (0, j)),
            out,
            out,
        ],
        out_specs=[out] * 2,
        cost_estimate=pl.CostEstimate(
            flops=2 * rows * depth * width, bytes_accessed=2 * (rows * depth + depth * width + 4 * rows * width), transcendentals=0
        ),
        name="hidden_back",
    )(grad, w_down, gate_slope, up_slope)


def two_nt_kernel(a_ref, b_ref, wa_ref, wb_ref, out_ref):
    out_ref[...] = (matmul_nt(a_ref[...], wa_ref[...]) + matmul_nt(b_ref[...], wb_ref[...])).astype(BF16)


def two_nt(first, second, w_first, w_second, start, rows):
    depth = first.shape[1]
    width = w_first.shape[0]
    bm, bn = tile(rows, 512), tile(width, 512)
    left = pl.BlockSpec((bm, depth), lambda j, i: (start // bm + i, 0))
    weight = pl.BlockSpec((bn, depth), lambda j, i: (j, 0))
    return pl.pallas_call(
        two_nt_kernel,
        out_shape=jax.ShapeDtypeStruct((rows, width), BF16),
        grid=(width // bn, rows // bm),
        in_specs=[left, left, weight, weight],
        out_specs=pl.BlockSpec((bm, bn), lambda j, i: (i, j)),
        cost_estimate=pl.CostEstimate(
            flops=4 * rows * depth * width, bytes_accessed=2 * (2 * rows * depth + 2 * depth * width + rows * width), transcendentals=0
        ),
        name="two_nt",
    )(first, second, w_first, w_second)


def hop(value, bit, size):
    return lax.ppermute(value, "tp", [(i, i ^ bit) for i in range(size)])


def bit_orders(size):
    bits = []
    bit = 1
    while bit < size:
        bits.append(bit)
        bit *= 2
    return (bits, bits[::-1])


def gather_tp(halves, size):
    got = []
    for half, order in zip(halves, bit_orders(size)):
        have = {0: half}
        for bit in order:
            for r in sorted(have):
                have[r ^ bit] = hop(have[r], bit, size)
        got.append(have)
    return jnp.concatenate([got[h][r] for r in range(size) for h in range(2)], axis=0)


def scatter_tp(piece, size):
    out = []
    parts = [piece(r) for r in range(size)]
    own = parts[0].shape[0]
    for h, order in enumerate(bit_orders(size)):
        have = {r: parts[r][h * (own // 2) : (h + 1) * (own // 2)] for r in range(size)}
        for step, bit in enumerate(order[::-1]):
            last = step == len(order) - 1
            for r in sorted(have, reverse=True):
                if r & bit:
                    came = hop(have.pop(r), bit, size).astype(F32)
                    total = have[r ^ bit].astype(F32) + came
                    have[r ^ bit] = total if last else total.astype(BF16)
        out.append(have[0].astype(F32))
    return out


def split_halves(rows):
    middle = rows.shape[0] // 2
    return [rows[:middle], rows[middle:]]


def per_device(
    tokens, gain_attn, gain_mlp, w_query, w_key, w_value, w_out, w_gate, w_up, w_down, lengths, out_grad
):
    size = lax.axis_size("tp")
    me = lax.axis_index("tp")
    own = tokens.shape[0]
    count = lengths.shape[0]
    group = own * size
    length = group // count
    per_slot = length // own
    my_slot = me // per_slot
    flip = me % per_slot
    head_width = w_query.shape[1]

    def along_fsdp(weight):
        return lax.all_gather(weight, "fsdp", axis=0, tiled=True)

    qkv_full = along_fsdp(jnp.concatenate([w_query, w_key, w_value], axis=1))
    out_full = along_fsdp(w_out)
    gate_full = along_fsdp(w_gate)
    up_full = along_fsdp(w_up)
    down_full = along_fsdp(w_down)

    own_length = lax.dynamic_index_in_dim(lengths, my_slot, keepdims=False)
    places = flip * own + jnp.arange(own, dtype=jnp.int32)
    valid = split_halves((places < own_length).astype(F32)[:, None])
    infos = [
        jnp.stack([lax.dynamic_index_in_dim(lengths, my_slot ^ s, keepdims=False), flip]).astype(jnp.int32)
        for s in range(count)
    ]
    cosine, sine = rotary_tables(length)
    x = [half.astype(F32) for half in split_halves(tokens)]
    scale_one = [inverse_rms(v) for v in x]
    normed_one = [v * s for v, s in zip(x, scale_one)]
    h1 = gather_tp([(n * gain_attn).astype(BF16) for n in normed_one], size)
    grad_rows = [m * g.astype(F32) for m, g in zip(valid, split_halves(out_grad))]
    dm = gather_tp([g.astype(BF16) for g in grad_rows], size)

    qkv = matmul(h1, qkv_full)
    saved = {}
    partial = {}
    for s in reversed(range(count)):
        saved[s] = attend(qkv, s, infos[s], cosine, sine, own, length)
        partial[s] = matmul_nt(saved[s][3], out_full).astype(BF16)

    def attn_piece(r):
        s, inside = divmod(r, per_slot)
        return partial[s][inside * own : (inside + 1) * own]

    attn_out = scatter_tp(attn_piece, size)
    middle = [v + a for v, a in zip(x, attn_out)]
    scale_two = [inverse_rms(v) for v in middle]
    normed_two = [v * s for v, s in zip(middle, scale_two)]
    h2 = gather_tp([(n * gain_mlp).astype(BF16) for n in normed_two], size)

    hid, gate_slope, up_slope = gate_up(h2, gate_full, up_full)
    down_term = matmul_tn(dm, hid).astype(BF16)
    grad_gate, grad_up = hidden_back(dm, down_full, gate_slope, up_slope)
    gate_term = matmul_tn(h2, grad_gate).astype(BF16)
    up_term = matmul_tn(h2, grad_up).astype(BF16)
    half_group = group // 2
    two = [two_nt(grad_gate, grad_up, gate_full, up_full, half_group * i, half_group) for i in range(2)]

    def two_piece(r):
        i, inside = divmod(r, size // 2)
        return two[i][inside * own : (inside + 1) * own]

    grad_two = scatter_tp(two_piece, size)
    mlp = matmul_nt(hid, down_full).astype(BF16)
    mlp_out = scatter_tp(lambda r: mlp[r * own : (r + 1) * own], size)
    output = jnp.concatenate(
        [(m * (v + o)).astype(BF16) for m, v, o in zip(valid, middle, mlp_out)], axis=0
    )
    gain_mlp_term = sum(jnp.sum(g * n, axis=0) for g, n in zip(grad_two, normed_two))
    inner_two = [g * gain_mlp for g in grad_two]
    grad_middle = [
        g + s * (i - n * jnp.mean(i * n, axis=-1, keepdims=True))
        for g, s, i, n in zip(grad_rows, scale_two, inner_two, normed_two)
    ]
    grad_attn = gather_tp([g.astype(BF16) for g in grad_middle], size)

    mixed = jnp.concatenate([saved[s][3] for s in range(count)], axis=0)
    out_term = matmul_tn(grad_attn, mixed).astype(BF16)
    grad_mixed = matmul(grad_attn, out_full).astype(BF16)
    grad_qkv = {}
    partial_one = {}
    for s in reversed(range(count)):
        query, keys, values, _ = saved[s]
        grad_qkv[s] = attend_back(query, keys, values, grad_mixed, s, infos[s], cosine, sine, own, length)
        partial_one[s] = matmul_nt(grad_qkv[s], qkv_full).astype(BF16)
    qkv_term = matmul_tn(h1, jnp.concatenate([grad_qkv[s] for s in range(count)], axis=0)).astype(BF16)

    def one_piece(r):
        s, inside = divmod(r, per_slot)
        return partial_one[s][inside * own : (inside + 1) * own]

    grad_one = scatter_tp(one_piece, size)
    gain_attn_term = sum(jnp.sum(g * n, axis=0) for g, n in zip(grad_one, normed_one))
    inner_one = [g * gain_attn for g in grad_one]
    input_grad = jnp.concatenate(
        [
            (m + s * (i - n * jnp.mean(i * n, axis=-1, keepdims=True))).astype(BF16)
            for m, s, i, n in zip(grad_middle, scale_one, inner_one, normed_one)
        ],
        axis=0,
    )

    def back_fsdp(term):
        return lax.psum_scatter(term, "fsdp", scatter_dimension=0, tiled=True).astype(F32)

    down_grad = back_fsdp(down_term)
    gate_grad = back_fsdp(gate_term)
    up_grad = back_fsdp(up_term)
    out_proj_grad = back_fsdp(out_term)
    qkv_grad = back_fsdp(qkv_term)
    gains = [
        lax.psum_scatter(term, ("fsdp", "tp"), scatter_dimension=0, tiled=True)
        for term in (gain_attn_term, gain_mlp_term)
    ]
    return (
        output,
        input_grad,
        gains[0],
        gains[1],
        qkv_grad[:, :head_width],
        qkv_grad[:, head_width : 2 * head_width],
        qkv_grad[:, 2 * head_width :],
        out_proj_grad,
        gate_grad,
        up_grad,
        down_grad,
    )


def solution(mesh):
    rows = P(("fsdp", "tp"), None)
    weight = P("fsdp", "tp")
    vector = P(("fsdp", "tp"))
    return jax.shard_map(
        per_device,
        mesh=mesh,
        in_specs=(rows, P(), P()) + (weight,) * 7 + (P("fsdp"), rows),
        out_specs=(rows, rows, vector, vector) + (weight,) * 7,
        check_vma=False,
    )
```

time: 2670 us -> 1110 us (0.42)
  waiting for transfers between devices: 1660 us -> 450 us
  matrix products: 666 us -> 174 us
  Pallas kernels: 0 us -> 202 us
  other arithmetic: 182 us -> 70.2 us
  starting transfers between devices: 1.67 us -> 53.8 us
  blocking collectives: 39.5 us -> 85.3 us
  local copies, waits for them, and re-layouts: 95.9 us -> 52 us
    all_gather x20 -> x5, waiting for transfers between devices: 907 us -> 0.01 us  [along_fsdp(): return lax.all_gather(weight, 'fsdp', axis=0, tiled=True)]
    reduce_scatter x12 -> x5, waiting for transfers between devices: 746 us -> 74.2 us  [back_fsdp(): lax.psum_scatter(term, 'fsdp', scatter_dimension=0, tiled=True).astype(F32)]
    dot_general x20 -> x2, matrix products: 419 us -> 28.9 us  [matmul(): return jnp.dot(left, right, preferred_element_type=F32)]
    ppermute x0 -> x48, waiting for transfers between devices: none -> 374 us  [hop(): return lax.ppermute(value, 'tp', [(i, i ^ bit) for i in range(size)])]
    pallas_call x0 -> x8, Pallas kernels: none -> 202 us  [the longest x2 55.6 us: two_nt(): pl.pallas_call(two_nt_kernel, out_shape=jax.ShapeDtypeStruct((rows, width...]
    dot_general x8 -> x5, matrix products: 134 us -> 47.8 us  [matmul_nt(): lax.dot_general(left, right, (((1,), (1,)), ((), ())), preferred_element_...]
    convert_element_type x17 -> x14, other arithmetic: 99.7 us -> 31.4 us  [the longest x7 11.6 us: scatter_tp(): have[r ^ bit] = total if last else total.astype(BF16)]
    ppermute x0 -> x48, starting transfers between devices: none -> 53.4 us  [hop(): return lax.ppermute(value, 'tp', [(i, i ^ bit) for i in range(size)])]
  transfers between devices with their start and end apart: 32 -> 58, of which waited for: 25 -> 27; matrix products, arithmetic and copies ran while one was open for 29% -> 22% of each run, Pallas kernels for 0% -> 18%
where the time goes in v1:
time: 1110 us; the launch traced here: 1100 us
  waiting for transfers between devices  450 us (41%)
  Pallas kernels  202 us (18%)
  matrix products  174 us (16%)
  blocking collectives  85.3 us (8%)
  other arithmetic  70.2 us (6%)
  starting transfers between devices  53.8 us (5%)
  local copies, waits for them, and re-layouts  52 us (5%)
  between operations  15.4 us (1%)
    ppermute x48, waiting for transfers between devices, hop(): return lax.ppermute(value, 'tp', [(i, i ^ bit) for i in range(size)])  374 us
    dot_general x5, matrix products, matmul_tn(): lax.dot_general(left, right, (((0,), (0,)), ((), ())), preferred_element_...  97 us
    unnamed x1, blocking collectives  85.3 us
    reduce_scatter x5, waiting for transfers between devices, back_fsdp(): lax.psum_scatter(term, 'fsdp', scatter_dimension=0, tiled=True).astype(F32)  74.2 us
    pallas_call x2, Pallas kernels, two_nt(): pl.pallas_call(two_nt_kernel, out_shape=jax.ShapeDtypeStruct((rows, width...  55.6 us
    ppermute x48, starting transfers between devices, hop(): return lax.ppermute(value, 'tp', [(i, i ^ bit) for i in range(size)])  53.4 us
    pallas_call x1, Pallas kernels, gate_up(): pl.pallas_call(gate_up_kernel, out_shape=[jax.ShapeDtypeStruct((rows, wid...  48.3 us
    dot_general x5, matrix products, matmul_nt(): lax.dot_general(left, right, (((1,), (1,)), ((), ())), preferred_element_...  47.8 us
  transfers between devices with their start and end apart: 58, of which 27 were waited for; matrix products, arithmetic and copies ran while one was open for 22% of the time, Pallas kernels for 18%

profile of v1, /device:TPU:0, one launch (start us, length us, event | category | flops | bytes accessed | tf_op | source)
XLA Modules:
  0.0 1102.8 jit_solution(16750789362215190294)
XLA Ops:
  13.8 3.0 collective-permute-start
  22.3 2.8 constant_dynamic-update-slice_fusion.23
  31.0 10.0 collective-permute-done
  45.0 20.6 %collective-permute-done.3 = bf16[256,2048]{1,0:T(8,128)(2,1)} collective-permute-done((bf16[256,2048]{1,0:T(8,128)(2,1)}, bf16[256,2048]{1,0:T(8,128)(2,1)}, u32[]{:S(2)}, u32[]{:S(2)}) %collective-permute-start.3) | collective-permute-done | bytes 1048608 | tf_op jit(solution)/shard_map/ppermute | solution.py:326
  73.8 12.8 %collective-permute-done.4 = bf16[256,2048]{1,0:T(8,128)(2,1)S(1)} collective-permute-done((bf16[256,2048]{1,0:T(8,128)(2,1)S(1)}, bf16[256,2048]{1,0:T(8,128)(2,1)S(1)}, u32[]{:S(2)}, u32[]{:S(2)}) %collective-permute-start.4) | collective-permute-done | bytes 1048608 | tf_op jit(solution)/shard_map/ppermute | solution.py:326
  87.6 20.0 %collective-permute-done.5 = bf16[256,2048]{1,0:T(8,128)(2,1)S(1)} collective-permute-done((bf16[256,2048]{1,0:T(8,128)(2,1)}, bf16[256,2048]{1,0:T(8,128)(2,1)S(1)}, u32[]{:S(2)}, u32[]{:S(2)}) %collective-permute-start.5) | collective-permute-done | bytes 1048608 | tf_op jit(solution)/shard_map/ppermute | solution.py:326
  108.6 19.6 %fusion.53.q_ref.k_ref.v_ref = f32[2048,1536]{1,0:T(8,128)} fusion(bf16[2048,2048]{1,0:T(8,128)(2,1)} %constant_dynamic-update-slice_fusion, bf16[2048,1536]{1,0:T(8,128)(2,1)} %all-gather.6.cloned.1.call-done), kind=kOutput, calls=%fused_computation.150 | convolution fusion | flops 12884901888 | bytes 27262976 | tf_op jit(solution)/shard_map/dot_general | solution.py:21
  128.2 12.2 %attend.3 = (bf16[1024,512]{1,0:T(8,128)(2,1)}, bf16[1024,512]{1,0:T(8,128)(2,1)}, bf16[1024,512]{1,0:T(8,128)(2,1)}, bf16[1024,512]{1,0:T(8,128)(2,1)}) custom-call(s32[2]{0:T(128)} %get-tuple-element.106.info, f32[2048,1536]{1,0:T(8,128)} %fusion.53.q_ref.k_ref.v_ref, f32[2048,1536]{1,0:T(8,128)} %fusion.53.q_ref.k_ref.v_ref, ...), custom_call_target="tpu_custom_call" | custom-call | flops 4294967296 | bytes 10485760 | tf_op jit(solution)/shard_map/attend/pallas_call | solution.py:130
  140.4 4.3 convolution_convert_fusion.7
  153.2 12.6 %attend.2 = (bf16[1024,512]{1,0:T(8,128)(2,1)}, bf16[1024,512]{1,0:T(8,128)(2,1)}, bf16[1024,512]{1,0:T(8,128)(2,1)}, bf16[1024,512]{1,0:T(8,128)(2,1)}) custom-call(s32[2]{0:T(128)} %get-tuple-element.105.info, f32[2048,1536]{1,0:T(8,128)} %fusion.53.q_ref.k_ref.v_ref, f32[2048,1536]{1,0:T(8,128)} %fusion.53.q_ref.k_ref.v_ref, ...), custom_call_target="tpu_custom_call" | custom-call | flops 4294967296 | bytes 10485760 | tf_op jit(solution)/shard_map/attend/pallas_call | solution.py:130
  165.9 4.3 convolution_convert_fusion.8
  171.4 2.5 collective-permute-start.6
  175.5 18.8 %collective-permute-done.7 = bf16[256,2048]{1,0:T(8,128)(2,1)} collective-permute-done((bf16[256,2048]{1,0:T(8,128)(2,1)}, bf16[256,2048]{1,0:T(8,128)(2,1)}, u32[]{:S(2)}, u32[]{:S(2)}) %collective-permute-start.7) | collective-permute-done | bytes 1048608 | tf_op jit(solution)/shard_map/ppermute | solution.py:326
  194.3 2.5 collective-permute-start.11
  199.1 2.6 constant_dynamic-update-slice_fusion.21
  203.2 13.5 %collective-permute-done.6 = bf16[256,2048]{1,0:T(8,128)(2,1)S(1)} collective-permute-done((bf16[256,2048]{1,0:T(8,128)(2,1)S(1)}, bf16[256,2048]{1,0:T(8,128)(2,1)S(1)}, u32[]{:S(2)}, u32[]{:S(2)}) %collective-permute-start.6) | collective-permute-done | bytes 1048608 | tf_op jit(solution)/shard_map/ppermute | solution.py:326
  216.7 2.5 collective-permute-start.28
  219.2 20.0 %collective-permute-done.11 = bf16[256,2048]{1,0:T(8,128)(2,1)S(1)} collective-permute-done((bf16[256,2048]{1,0:T(8,128)(2,1)S(1)}, bf16[256,2048]{1,0:T(8,128)(2,1)S(1)}, u32[]{:S(2)}, u32[]{:S(2)}) %collective-permute-start.11) | collective-permute-done | bytes 1048608 | tf_op jit(solution)/shard_map/ppermute | solution.py:326
  245.7 2.5 collective-permute-start.15
  249.3 12.4 %collective-permute-done.26 = bf16[256,2048]{1,0:T(8,128)(2,1)S(1)} collective-permute-done((bf16[256,2048]{1,0:T(8,128)(2,1)}, bf16[256,2048]{1,0:T(8,128)(2,1)S(1)}, u32[]{:S(2)}, u32[]{:S(2)}) %collective-permute-start.26) | collective-permute-done | bytes 1048608 | tf_op jit(solution)/shard_map/ppermute | solution.py:326
  263.3 20.9 %collective-permute-done.28 = bf16[256,2048]{1,0:T(8,128)(2,1)S(1)} collective-permute-done((bf16[256,2048]{1,0:T(8,128)(2,1)}, bf16[256,2048]{1,0:T(8,128)(2,1)S(1)}, u32[]{:S(2)}, u32[]{:S(2)}) %collective-permute-start.28) | collective-permute-done | bytes 1048608 | tf_op jit(solution)/shard_map/ppermute | solution.py:326
  291.2 15.4 %collective-permute-done.15 = bf16[256,2048]{1,0:T(8,128)(2,1)S(1)} collective-permute-done((bf16[256,2048]{1,0:T(8,128)(2,1)S(1)}, bf16[256,2048]{1,0:T(8,128)(2,1)S(1)}, u32[]{:S(2)}, u32[]{:S(2)}) %collective-permute-start.15) | collective-permute-done | bytes 1048608 | tf_op jit(solution)/shard_map/ppermute | solution.py:326
  309.2 19.9 %collective-permute-done.14 = bf16[256,2048]{1,0:T(8,128)(2,1)S(1)} collective-permute-done((bf16[256,2048]{1,0:T(8,128)(2,1)S(1)}, bf16[256,2048]{1,0:T(8,128)(2,1)S(1)}, u32[]{:S(2)}, u32[]{:S(2)}) %collective-permute-start.14) | collective-permute-done | bytes 1048608 | tf_op jit(solution)/shard_map/ppermute | solution.py:326
  331.2 20.3 %collective-permute-done.16 = bf16[256,2048]{1,0:T(8,128)(2,1)S(1)} collective-permute-done((bf16[256,2048]{1,0:T(8,128)(2,1)S(1)}, bf16[256,2048]{1,0:T(8,128)(2,1)S(1)}, u32[]{:S(2)}, u32[]{:S(2)}) %collective-permute-start.16) | collective-permute-done | bytes 1048608 | tf_op jit(solution)/shard_map/ppermute | solution.py:326
  353.6 48.3 %gate_up.1 = (bf16[2048,2048]{1,0:T(8,128)(2,1)}, bf16[2048,2048]{1,0:T(8,128)(2,1)}, bf16[2048,2048]{1,0:T(8,128)(2,1)}) custom-call(bf16[2048,2048]{1,0:T(8,128)(2,1)} %constant_dynamic-update-slice_fusion.8.h_ref, bf16[2048,2048]{1,0:T(8,128)(2,1)} %all-gather.10.cloned.1.call-done.g_ref.wa_ref, bf16[2048,2048]{1,0:T(8,128)(2,1)} %all-gather.12.cloned.1.call-done.u_ref.wb_ref), custom_call_target="tpu_custom_call" | custom-call | flops 34359738368 | bytes 50331648 | tf_op jit(solution)/shard_map/gate_up/pallas_call | solution.py:260
  401.9 22.3 %convolution_convert_fusion.3 = bf16[2048,2048]{1,0:T(8,128)(2,1)S(1)} fusion(bf16[2048,2048]{1,0:T(8,128)(2,1)} %get-tuple-element.26, bf16[2048,2048]{1,0:T(8,128)(2,1)} %all-gather.14.cloned.1.call-done.w_ref), kind=kOutput, calls=%fused_computation.3 | convolution fusion | flops 17184063488 | bytes 25165824 | tf_op jit(solution)/shard_map/dot_general | solution.py:25
  428.8 2.5 collective-permute-start.19
  431.8 34.1 %hidden_back.1 = (bf16[2048,2048]{1,0:T(8,128)(2,1)}, bf16[2048,2048]{1,0:T(8,128)(2,1)}) custom-call(bf16[2048,2048]{1,0:T(8,128)(2,1)} %constant_dynamic-update-slice_fusion.16.g_ref, bf16[2048,2048]{1,0:T(8,128)(2,1)} %all-gather.14.cloned.1.call-done.w_ref, bf16[2048,2048]{1,0:T(8,128)(2,1)} %get-tuple-element.27.gate_slope, ...), custom_call_target="tpu_custom_call" | custom-call | flops 17179869184 | bytes 50331648 | tf_op jit(solution)/shard_map/hidden_back/pallas_call | solution.py:284
  465.9 27.7 %two_nt.3 = bf16[1024,2048]{1,0:T(8,128)(2,1)} custom-call(bf16[2048,2048]{1,0:T(8,128)(2,1)} %get-tuple-element.29.a_ref, bf16[2048,2048]{1,0:T(8,128)(2,1)} %get-tuple-element.30.b_ref, bf16[2048,2048]{1,0:T(8,128)(2,1)} %all-gather.10.cloned.1.call-done.g_ref.wa_ref, bf16[2048,2048]{1,0:T(8,128)(2,1)} %all-gather.12.cloned.1.call-done.u_ref.wb_ref), custom_call_target="tpu_custom_call" | custom-call | flops 17179869184 | bytes 29360128 | tf_op jit(solution)/shard_map/two_nt/pallas_call | solution.py:312
  493.6 3.6 fusion.48
  500.9 27.9 %two_nt.2 = bf16[1024,2048]{1,0:T(8,128)(2,1)} custom-call(bf16[2048,2048]{1,0:T(8,128)(2,1)} %get-tuple-element.29.a_ref, bf16[2048,2048]{1,0:T(8,128)(2,1)} %get-tuple-element.30.b_ref, bf16[2048,2048]{1,0:T(8,128)(2,1)} %all-gather.10.cloned.1.call-done.g_ref.wa_ref, bf16[2048,2048]{1,0:T(8,128)(2,1)} %all-gather.12.cloned.1.call-done.u_ref.wb_ref), custom_call_target="tpu_custom_call" | custom-call | flops 17179869184 | bytes 29360128 | tf_op jit(solution)/shard_map/two_nt/pallas_call | solution.py:312
  540.4 36.1 %collective-permute-done.20 = bf16[256,2048]{1,0:T(8,128)(2,1)S(1)} collective-permute-done((bf16[256,2048]{1,0:T(8,128)(2,1)S(1)}, bf16[256,2048]{1,0:T(8,128)(2,1)S(1)}, u32[]{:S(2)}, u32[]{:S(2)}) %collective-permute-start.20) | collective-permute-done | bytes 1048608 | tf_op jit(solution)/shard_map/ppermute | solution.py:326
  576.9 3.8 multiply_convert_fusion.1
  580.7 18.2 %collective-permute-done.21 = bf16[256,2048]{1,0:T(8,128)(2,1)S(1)} collective-permute-done((bf16[256,2048]{1,0:T(8,128)(2,1)S(1)}, bf16[256,2048]{1,0:T(8,128)(2,1)S(1)}, u32[]{:S(2)}, u32[]{:S(2)}) %collective-permute-start.21) | collective-permute-done | bytes 1048608 | tf_op jit(solution)/shard_map/ppermute | solution.py:326
  599.0 22.5 %collective-permute-done.32 = bf16[256,2048]{1,0:T(8,128)(2,1)S(1)} collective-permute-done((bf16[256,2048]{1,0:T(8,128)(2,1)S(1)}, bf16[256,2048]{1,0:T(8,128)(2,1)S(1)}, u32[]{:S(2)}, u32[]{:S(2)}) %collective-permute-start.32) | collective-permute-done | bytes 1048608 | tf_op jit(solution)/shard_map/ppermute | solution.py:326
  621.5 5.1 multiply_reduce_fusion.1
  635.2 18.6 %collective-permute-done.36 = bf16[256,2048]{1,0:T(8,128)(2,1)S(1)} collective-permute-done((bf16[256,2048]{1,0:T(8,128)(2,1)S(1)}, bf16[256,2048]{1,0:T(8,128)(2,1)S(1)}, u32[]{:S(2)}, u32[]{:S(2)}) %collective-permute-start.36) | collective-permute-done | bytes 1048608 | tf_op jit(solution)/shard_map/ppermute | solution.py:326
  653.9 3.0 collective-permute-done.39
  658.6 17.8 %collective-permute-done.37 = bf16[256,2048]{1,0:T(8,128)(2,1)S(1)} collective-permute-done((bf16[256,2048]{1,0:T(8,128)(2,1)S(1)}, bf16[256,2048]{1,0:T(8,128)(2,1)S(1)}, u32[]{:S(2)}, u32[]{:S(2)}) %collective-permute-start.37) | collective-permute-done | bytes 1048608 | tf_op jit(solution)/shard_map/ppermute | solution.py:326
  676.4 2.9 collective-permute-done.38
  679.5 22.3 %collective-permute-done.40 = bf16[256,2048]{1,0:T(8,128)(2,1)S(1)} collective-permute-done((bf16[256,2048]{1,0:T(8,128)(2,1)S(1)}, bf16[256,2048]{1,0:T(8,128)(2,1)S(1)}, u32[]{:S(2)}, u32[]{:S(2)}) %collective-permute-start.40) | collective-permute-done | bytes 1048608 | tf_op jit(solution)/shard_map/ppermute | solution.py:326
  702.0 3.3 copy-done.20
  705.3 6.4 convolution_convert_fusion.9
  711.7 24.2 %convolution_convert_fusion.1 = bf16[2048,2048]{1,0:T(8,128)(2,1)} fusion(bf16[2048,2048]{1,0:T(8,128)(2,1)} %constant_dynamic-update-slice_fusion.8.h_ref, bf16[2048,2048]{1,0:T(8,128)(2,1)} %get-tuple-element.30.b_ref), kind=kOutput, calls=%fused_computation.1 | convolution fusion | flops 17184063488 | bytes 25165824 | tf_op jit(solution)/shard_map/dot_general | solution.py:29
  736.0 23.9 %convolution_convert_fusion.2 = bf16[2048,2048]{1,0:T(8,128)(2,1)} fusion(bf16[2048,2048]{1,0:T(8,128)(2,1)} %constant_dynamic-update-slice_fusion.8.h_ref, bf16[2048,2048]{1,0:T(8,128)(2,1)} %get-tuple-element.29.a_ref), kind=kOutput, calls=%fused_computation.2 | convolution fusion | flops 17184063488 | bytes 25165824 | tf_op jit(solution)/shard_map/dot_general | solution.py:29
  760.0 23.8 %convolution_convert_fusion = bf16[2048,2048]{1,0:T(8,128)(2,1)} fusion(bf16[2048,2048]{1,0:T(8,128)(2,1)} %constant_dynamic-update-slice_fusion.16.g_ref, bf16[2048,2048]{1,0:T(8,128)(2,1)} %get-tuple-element.26), kind=kOutput, calls=%fused_computation | convolution fusion | flops 17184063488 | bytes 25165824 | tf_op jit(solution)/shard_map/dot_general | solution.py:29
  785.4 9.3 convolution_convert_fusion.10.g_ref
  794.7 19.3 %attend_back.2 = bf16[1024,1536]{1,0:T(8,128)(2,1)} custom-call(s32[2]{0:T(128)} %get-tuple-element.105.info, bf16[1024,512]{1,0:T(8,128)(2,1)} %get-tuple-element.31.q_ref, bf16[1024,512]{1,0:T(8,128)(2,1)} %get-tuple-element.32.k_ref, bf16[1024,512]{1,0:T(8,128)(2,1)} %get-tuple-element.33.v_ref, bf16[2048,512]{1,0:T(8,128)(2,1)} %convolution_convert_fusion.10.g_ref, ...), custom_call_target="tpu_custom_call" | custom-call | flops 10737418240 | bytes 10485760 | tf_op jit(solution)/shard_map/attend_back/pallas_call | solution.py:222
  814.0 19.6 %attend_back.3 = bf16[1024,1536]{1,0:T(8,128)(2,1)} custom-call(s32[2]{0:T(128)} %get-tuple-element.106.info, bf16[1024,512]{1,0:T(8,128)(2,1)} %get-tuple-element.34.q_ref, bf16[1024,512]{1,0:T(8,128)(2,1)} %get-tuple-element.35.k_ref, bf16[1024,512]{1,0:T(8,128)(2,1)} %get-tuple-element.36.v_ref, bf16[2048,512]{1,0:T(8,128)(2,1)} %convolution_convert_fusion.10.g_ref, ...), custom_call_target="tpu_custom_call" | custom-call | flops 10737418240 | bytes 10485760 | tf_op jit(solution)/shard_map/attend_back/pallas_call | solution.py:222
  833.6 18.8 %convolution_convert_fusion.4 = bf16[2048,1536]{1,0:T(8,128)(2,1)} fusion(bf16[2048,2048]{1,0:T(8,128)(2,1)} %constant_dynamic-update-slice_fusion, bf16[1024,1536]{1,0:T(8,128)(2,1)} %attend_back.3, bf16[1024,1536]{1,0:T(8,128)(2,1)S(1)} %copy-done.39), kind=kOutput, calls=%fused_computation.4 | convolution fusion | flops 12900630528 | bytes 20971520 | tf_op jit(solution)/shard_map/dot_general | solution.py:29
  852.5 9.9 convolution_convert_fusion.5
  865.4 6.9 convolution_convert_fusion.6
  875.9 2.7 collective-permute-done.46
  883.1 2.9 pad_maximum_fusion
  886.0 3.9 collective-permute-done.45
  891.5 19.9 %collective-permute-done.47 = bf16[256,2048]{1,0:T(8,128)(2,1)} collective-permute-done((bf16[256,2048]{1,0:T(8,128)(2,1)}, bf16[256,2048]{1,0:T(8,128)(2,1)}, u32[]{:S(2)}, u32[]{:S(2)}) %collective-permute-start.47) | collective-permute-done | bytes 1048608 | tf_op jit(solution)/shard_map/ppermute | solution.py:326
  911.4 4.0 fusion.17
  915.5 85.3 %all-reduce.2 = (f32[2048]{0:T(1024)S(1)}, f32[2048]{0:T(1024)S(1)}) all-reduce(f32[2048]{0:T(1024)S(1)} %add.208, f32[2048]{0:T(1024)S(1)} %add.209), channel_id=2, replica_groups=mesh['fsdp'=8,'tp'=4] {'fsdp','tp'}, use_global_device_ids=true, to_apply=%region_10.11.clone | all-reduce | flops 4096 | bytes 32768
  1002.0 5.2 fusion.16
  1010.5 2.8 convert_element_type.385
  1013.3 2.8 convert_element_type.383
  1016.1 6.6 reduce-scatter.14.cloned.1.call-done
  1022.7 2.8 convert_element_type.387
  1025.5 67.6 %reduce-scatter.6.cloned.1.call-done = bf16[256,1536]{1,0:T(8,128)(2,1)} async-done(((bf16[2048,1536]{1,0:T(8,128)(2,1)}), bf16[256,1536]{1,0:T(8,128)(2,1)}) %reduce-scatter.6.cloned.1.call-update) | async-done | bytes 786448 | tf_op jit(solution)/shard_map/reduce_scatter | solution.py:479
  (248 shorter events, 122.7 us)
Async XLA Ops:
  7.2 101.4 %all-gather.6.cloned.1.call-start = ((), (), s32[]{:S(2)}) async-start(), calls=%async_computation.5 | async-start | bytes 7077888 | tf_op jit(solution)/shard_map/all_gather | solution.py:386
  9.4 131.0 %all-gather.8.cloned.1.call-start = ((), (), s32[]{:S(2)}) async-start(), calls=%async_computation.6 | async-start | bytes 2359296 | tf_op jit(solution)/shard_map/all_gather | solution.py:386
  10.2 343.4 %all-gather.10.cloned.1.call-start = ((), (), s32[]{:S(2)}) async-start(), calls=%async_computation.7 | async-start | bytes 9437184 | tf_op jit(solution)/shard_map/all_gather | solution.py:386
  10.9 342.7 %all-gather.12.cloned.1.call-start = ((), (), s32[]{:S(2)}) async-start(), calls=%async_computation.8 | async-start | bytes 9437184 | tf_op jit(solution)/shard_map/all_gather | solution.py:386
  11.5 390.4 %all-gather.14.cloned.1.call-start = ((), (), s32[]{:S(2)}) async-start(), calls=%async_computation.9 | async-start | bytes 9437184 | tf_op jit(solution)/shard_map/all_gather | solution.py:386
  13.8 27.2 %collective-permute-start = (bf16[256,2048]{1,0:T(8,128)(2,1)}, bf16[256,2048]{1,0:T(8,128)(2,1)S(1)}, u32[]{:S(2)}, u32[]{:S(2)}) collective-permute-start(bf16[256,2048]{1,0:T(8,128)(2,1)} %get-tuple-element.74), channel_id=1, source_target_pairs={{0,1},{1,0},{2,3},{3,2},{4,5},{5,4},{6,7},{7,6},{8,9},{9,8},{10,11... | collective-permute-start | bytes 3145736 | tf_op jit(solution)/shard_map/ppermute | solution.py:326
  16.8 52.3 %collective-permute-start.2 = (bf16[256,2048]{1,0:T(8,128)(2,1)}, bf16[256,2048]{1,0:T(8,128)(2,1)}, u32[]{:S(2)}, u32[]{:S(2)}) collective-permute-start(bf16[256,2048]{1,0:T(8,128)(2,1)} %get-tuple-element.74), channel_id=1, source_target_pairs={{0,2},{1,3},{2,0},{3,1},{4,6},{5,7},{6,4},{7,5},{8,10},{9,11},{10,... | collective-permute-start | bytes 3145736 | tf_op jit(solution)/shard_map/ppermute | solution.py:326
  20.0 46.8 %collective-permute-start.1 = (bf16[256,2048]{1,0:T(8,128)(2,1)}, bf16[256,2048]{1,0:T(8,128)(2,1)}, u32[]{:S(2)}, u32[]{:S(2)}) collective-permute-start(bf16[256,2048]{1,0:T(8,128)(2,1)} %get-tuple-element.72), channel_id=1, source_target_pairs={{0,1},{1,0},{2,3},{3,2},{4,5},{5,4},{6,7},{7,6},{8,9},{9,8},{10,11... | collective-permute-start | bytes 3145736 | tf_op jit(solution)/shard_map/ppermute | solution.py:326
  20.5 45.1 %collective-permute-start.3 = (bf16[256,2048]{1,0:T(8,128)(2,1)}, bf16[256,2048]{1,0:T(8,128)(2,1)}, u32[]{:S(2)}, u32[]{:S(2)}) collective-permute-start(bf16[256,2048]{1,0:T(8,128)(2,1)} %get-tuple-element.72), channel_id=1, source_target_pairs={{0,2},{1,3},{2,0},{3,1},{4,6},{5,7},{6,4},{7,5},{8,10},{9,11},{10,... | collective-permute-start | bytes 3145736 | tf_op jit(solution)/shard_map/ppermute | solution.py:326
  21.8 127.8 %copy-start.27 = (f32[256]{0:T(256)}, f32[256]{0:T(256)S(1)}, u32[]{:S(2)}) copy-start(f32[256]{0:T(256)S(1)} %get-tuple-element.99) | copy-start | bytes 3076
  25.1 173.4 %collective-permute-start.24 = (bf16[256,2048]{1,0:T(8,128)(2,1)}, bf16[256,2048]{1,0:T(8,128)(2,1)}, u32[]{:S(2)}, u32[]{:S(2)}) collective-permute-start(bf16[256,2048]{1,0:T(8,128)(2,1)} %get-tuple-element.62), channel_id=1, source_target_pairs={{0,1},{1,0},{2,3},{3,2},{4,5},{5,4},{6,7},{7,6},{8,9},{9,8},{10,11... | collective-permute-start | bytes 3145736 | tf_op jit(solution)/shard_map/ppermute | solution.py:326
  27.1 981.6 %reduce-scatter.8.cloned.1.call-start = ((), (), s32[]{:S(2)}) async-start(), calls=%async_computation.11 | async-start | bytes 2359296 | tf_op jit(solution)/shard_map/reduce_scatter | solution.py:479
  41.0 45.6 %collective-permute-start.4 = (bf16[256,2048]{1,0:T(8,128)(2,1)S(1)}, bf16[256,2048]{1,0:T(8,128)(2,1)S(1)}, u32[]{:S(2)}, u32[]{:S(2)}) collective-permute-start(bf16[256,2048]{1,0:T(8,128)(2,1)S(1)} %collective-permute-done), channel_id=1, source_target_pairs={{0,2},{1,3},{2,0},{3,1},{4,6},{5,7},{6,4},{7,5},{8,10},{9,11},{10,... | collective-permute-start | bytes 3145736 | tf_op jit(solution)/shard_map/ppermute | solution.py:326
  65.6 42.0 %collective-permute-start.5 = (bf16[256,2048]{1,0:T(8,128)(2,1)}, bf16[256,2048]{1,0:T(8,128)(2,1)S(1)}, u32[]{:S(2)}, u32[]{:S(2)}) collective-permute-start(bf16[256,2048]{1,0:T(8,128)(2,1)} %collective-permute-done.3), channel_id=1, source_target_pairs={{0,1},{1,0},{2,3},{3,2},{4,5},{5,4},{6,7},{7,6},{8,9},{9,8},{10,11... | collective-permute-start | bytes 3145736 | tf_op jit(solution)/shard_map/ppermute | solution.py:326
  147.9 22.8 %collective-permute-start.10 = (bf16[256,2048]{1,0:T(8,128)(2,1)}, bf16[256,2048]{1,0:T(8,128)(2,1)S(1)}, u32[]{:S(2)}, u32[]{:S(2)}) collective-permute-start(bf16[256,2048]{1,0:T(8,128)(2,1)} %get-tuple-element.92), channel_id=1, source_target_pairs={{0,1},{1,0},{2,3},{3,2},{4,5},{5,4},{6,7},{7,6},{8,9},{9,8},{10,11... | collective-permute-start | bytes 3145736 | tf_op jit(solution)/shard_map/ppermute | solution.py:326
  151.2 50.5 %collective-permute-start.27 = (bf16[256,2048]{1,0:T(8,128)(2,1)}, bf16[256,2048]{1,0:T(8,128)(2,1)}, u32[]{:S(2)}, u32[]{:S(2)}) collective-permute-start(bf16[256,2048]{1,0:T(8,128)(2,1)} %get-tuple-element.60), channel_id=1, source_target_pairs={{0,2},{1,3},{2,0},{3,1},{4,6},{5,7},{6,4},{7,5},{8,10},{9,11},{10,... | collective-permute-start | bytes 3145736 | tf_op jit(solution)/shard_map/ppermute | solution.py:326
  152.7 41.6 %collective-permute-start.7 = (bf16[256,2048]{1,0:T(8,128)(2,1)}, bf16[256,2048]{1,0:T(8,128)(2,1)}, u32[]{:S(2)}, u32[]{:S(2)}) collective-permute-start(bf16[256,2048]{1,0:T(8,128)(2,1)} %get-tuple-element.93), channel_id=1, source_target_pairs={{0,2},{1,3},{2,0},{3,1},{4,6},{5,7},{6,4},{7,5},{8,10},{9,11},{10,... | collective-permute-start | bytes 3145736 | tf_op jit(solution)/shard_map/ppermute | solution.py:326
  170.3 32.9 %collective-permute-start.9 = (bf16[256,2048]{1,0:T(8,128)(2,1)S(1)}, bf16[256,2048]{1,0:T(8,128)(2,1)S(1)}, u32[]{:S(2)}, u32[]{:S(2)}) collective-permute-start(bf16[256,2048]{1,0:T(8,128)(2,1)S(1)} %slice.219), channel_id=1, source_target_pairs={{0,1},{1,0},{2,3},{3,2},{4,5},{5,4},{6,7},{7,6},{8,9},{9,8},{10,11... | collective-permute-start | bytes 3145736 | tf_op jit(solution)/shard_map/ppermute | solution.py:326
  171.4 45.3 %collective-permute-start.6 = (bf16[256,2048]{1,0:T(8,128)(2,1)S(1)}, bf16[256,2048]{1,0:T(8,128)(2,1)S(1)}, u32[]{:S(2)}, u32[]{:S(2)}) collective-permute-start(bf16[256,2048]{1,0:T(8,128)(2,1)S(1)} %copy-done.14), channel_id=1, source_target_pairs={{0,2},{1,3},{2,0},{3,1},{4,6},{5,7},{6,4},{7,5},{8,10},{9,11},{10,... | collective-permute-start | bytes 3145736 | tf_op jit(solution)/shard_map/ppermute | solution.py:326
  194.3 44.8 %collective-permute-start.11 = (bf16[256,2048]{1,0:T(8,128)(2,1)S(1)}, bf16[256,2048]{1,0:T(8,128)(2,1)S(1)}, u32[]{:S(2)}, u32[]{:S(2)}) collective-permute-start(bf16[256,2048]{1,0:T(8,128)(2,1)S(1)} %add_convert_fusion.12), channel_id=1, source_target_pairs={{0,2},{1,3},{2,0},{3,1},{4,6},{5,7},{6,4},{7,5},{8,10},{9,11},{10,... | collective-permute-start | bytes 3145736 | tf_op jit(solution)/shard_map/ppermute | solution.py:326
  198.5 41.1 %collective-permute-start.8 = (bf16[256,2048]{1,0:T(8,128)(2,1)S(1)}, bf16[256,2048]{1,0:T(8,128)(2,1)S(1)}, u32[]{:S(2)}, u32[]{:S(2)}) collective-permute-start(bf16[256,2048]{1,0:T(8,128)(2,1)S(1)} %add_convert_fusion.14), channel_id=1, source_target_pairs={{0,1},{1,0},{2,3},{3,2},{4,5},{5,4},{6,7},{7,6},{8,9},{9,8},{10,11... | collective-permute-start | bytes 3145736 | tf_op jit(solution)/shard_map/ppermute | solution.py:326
  201.7 44.0 %collective-permute-start.25 = (bf16[256,2048]{1,0:T(8,128)(2,1)}, bf16[256,2048]{1,0:T(8,128)(2,1)S(1)}, u32[]{:S(2)}, u32[]{:S(2)}) collective-permute-start(bf16[256,2048]{1,0:T(8,128)(2,1)} %get-tuple-element.60), channel_id=1, source_target_pairs={{0,1},{1,0},{2,3},{3,2},{4,5},{5,4},{6,7},{7,6},{8,9},{9,8},{10,11... | collective-permute-start | bytes 3145736 | tf_op jit(solution)/shard_map/ppermute | solution.py:326
  203.2 58.5 %collective-permute-start.26 = (bf16[256,2048]{1,0:T(8,128)(2,1)}, bf16[256,2048]{1,0:T(8,128)(2,1)S(1)}, u32[]{:S(2)}, u32[]{:S(2)}) collective-permute-start(bf16[256,2048]{1,0:T(8,128)(2,1)} %get-tuple-element.62), channel_id=1, source_target_pairs={{0,2},{1,3},{2,0},{3,1},{4,6},{5,7},{6,4},{7,5},{8,10},{9,11},{10,... | collective-permute-start | bytes 3145736 | tf_op jit(solution)/shard_map/ppermute | solution.py:326
  216.7 67.5 %collective-permute-start.28 = (bf16[256,2048]{1,0:T(8,128)(2,1)}, bf16[256,2048]{1,0:T(8,128)(2,1)S(1)}, u32[]{:S(2)}, u32[]{:S(2)}) collective-permute-start(bf16[256,2048]{1,0:T(8,128)(2,1)} %collective-permute-done.24), channel_id=1, source_target_pairs={{0,2},{1,3},{2,0},{3,1},{4,6},{5,7},{6,4},{7,5},{8,10},{9,11},{10,... | collective-permute-start | bytes 3145736 | tf_op jit(solution)/shard_map/ppermute | solution.py:326
  239.1 50.9 %collective-permute-start.29 = (bf16[256,2048]{1,0:T(8,128)(2,1)}, bf16[256,2048]{1,0:T(8,128)(2,1)S(1)}, u32[]{:S(2)}, u32[]{:S(2)}) collective-permute-start(bf16[256,2048]{1,0:T(8,128)(2,1)} %collective-permute-done.27), channel_id=1, source_target_pairs={{0,1},{1,0},{2,3},{3,2},{4,5},{5,4},{6,7},{7,6},{8,9},{9,8},{10,11... | collective-permute-start | bytes 3145736 | tf_op jit(solution)/shard_map/ppermute | solution.py:326
  242.9 47.1 %collective-permute-start.12 = (bf16[256,2048]{1,0:T(8,128)(2,1)S(1)}, bf16[256,2048]{1,0:T(8,128)(2,1)S(1)}, u32[]{:S(2)}, u32[]{:S(2)}) collective-permute-start(bf16[256,2048]{1,0:T(8,128)(2,1)S(1)} %get-tuple-element.68), channel_id=1, source_target_pairs={{0,1},{1,0},{2,3},{3,2},{4,5},{5,4},{6,7},{7,6},{8,9},{9,8},{10,11... | collective-permute-start | bytes 3145736 | tf_op jit(solution)/shard_map/ppermute | solution.py:326
  245.7 60.8 %collective-permute-start.15 = (bf16[256,2048]{1,0:T(8,128)(2,1)S(1)}, bf16[256,2048]{1,0:T(8,128)(2,1)S(1)}, u32[]{:S(2)}, u32[]{:S(2)}) collective-permute-start(bf16[256,2048]{1,0:T(8,128)(2,1)S(1)} %get-tuple-element.64), channel_id=1, source_target_pairs={{0,2},{1,3},{2,0},{3,1},{4,6},{5,7},{6,4},{7,5},{8,10},{9,11},{10,... | collective-permute-start | bytes 3145736 | tf_op jit(solution)/shard_map/ppermute | solution.py:326
  261.7 46.4 %collective-permute-start.13 = (bf16[256,2048]{1,0:T(8,128)(2,1)S(1)}, bf16[256,2048]{1,0:T(8,128)(2,1)S(1)}, u32[]{:S(2)}, u32[]{:S(2)}) collective-permute-start(bf16[256,2048]{1,0:T(8,128)(2,1)S(1)} %get-tuple-element.64), channel_id=1, source_target_pairs={{0,1},{1,0},{2,3},{3,2},{4,5},{5,4},{6,7},{7,6},{8,9},{9,8},{10,11... | collective-permute-start | bytes 3145736 | tf_op jit(solution)/shard_map/ppermute | solution.py:326
  284.2 44.8 %collective-permute-start.14 = (bf16[256,2048]{1,0:T(8,128)(2,1)S(1)}, bf16[256,2048]{1,0:T(8,128)(2,1)S(1)}, u32[]{:S(2)}, u32[]{:S(2)}) collective-permute-start(bf16[256,2048]{1,0:T(8,128)(2,1)S(1)} %get-tuple-element.68), channel_id=1, source_target_pairs={{0,2},{1,3},{2,0},{3,1},{4,6},{5,7},{6,4},{7,5},{8,10},{9,11},{10,... | collective-permute-start | bytes 3145736 | tf_op jit(solution)/shard_map/ppermute | solution.py:326
  290.1 61.4 %collective-permute-start.16 = (bf16[256,2048]{1,0:T(8,128)(2,1)S(1)}, bf16[256,2048]{1,0:T(8,128)(2,1)S(1)}, u32[]{:S(2)}, u32[]{:S(2)}) collective-permute-start(bf16[256,2048]{1,0:T(8,128)(2,1)S(1)} %collective-permute-done.12), channel_id=1, source_target_pairs={{0,2},{1,3},{2,0},{3,1},{4,6},{5,7},{6,4},{7,5},{8,10},{9,11},{10,... | collective-permute-start | bytes 3145736 | tf_op jit(solution)/shard_map/ppermute | solution.py:326
  306.6 46.0 %collective-permute-start.17 = (bf16[256,2048]{1,0:T(8,128)(2,1)S(1)}, bf16[256,2048]{1,0:T(8,128)(2,1)S(1)}, u32[]{:S(2)}, u32[]{:S(2)}) collective-permute-start(bf16[256,2048]{1,0:T(8,128)(2,1)S(1)} %collective-permute-done.15), channel_id=1, source_target_pairs={{0,1},{1,0},{2,3},{3,2},{4,5},{5,4},{6,7},{7,6},{8,9},{9,8},{10,11... | collective-permute-start | bytes 3145736 | tf_op jit(solution)/shard_map/ppermute | solution.py:326
  428.8 101.2 %collective-permute-start.19 = (bf16[256,2048]{1,0:T(8,128)(2,1)}, bf16[256,2048]{1,0:T(8,128)(2,1)S(1)}, u32[]{:S(2)}, u32[]{:S(2)}) collective-permute-start(bf16[256,2048]{1,0:T(8,128)(2,1)} %get-tuple-element.80), channel_id=1, source_target_pairs={{0,2},{1,3},{2,0},{3,1},{4,6},{5,7},{6,4},{7,5},{8,10},{9,11},{10,... | collective-permute-start | bytes 3145736 | tf_op jit(solution)/shard_map/ppermute | solution.py:326
  431.3 106.6 %collective-permute-start.18 = (bf16[256,2048]{1,0:T(8,128)(2,1)}, bf16[256,2048]{1,0:T(8,128)(2,1)S(1)}, u32[]{:S(2)}, u32[]{:S(2)}) collective-permute-start(bf16[256,2048]{1,0:T(8,128)(2,1)} %get-tuple-element.77), channel_id=1, source_target_pairs={{0,2},{1,3},{2,0},{3,1},{4,6},{5,7},{6,4},{7,5},{8,10},{9,11},{10,... | collective-permute-start | bytes 3145736 | tf_op jit(solution)/shard_map/ppermute | solution.py:326
  431.4 107.2 %collective-permute-start.22 = (bf16[256,2048]{1,0:T(8,128)(2,1)}, bf16[256,2048]{1,0:T(8,128)(2,1)S(1)}, u32[]{:S(2)}, u32[]{:S(2)}) collective-permute-start(bf16[256,2048]{1,0:T(8,128)(2,1)} %get-tuple-element.78), channel_id=1, source_target_pairs={{0,1},{1,0},{2,3},{3,2},{4,5},{5,4},{6,7},{7,6},{8,9},{9,8},{10,11... | collective-permute-start | bytes 3145736 | tf_op jit(solution)/shard_map/ppermute | solution.py:326
  497.3 35.1 %collective-permute-start.34 = (bf16[256,2048]{1,0:T(8,128)(2,1)}, bf16[256,2048]{1,0:T(8,128)(2,1)}, u32[]{:S(2)}, u32[]{:S(2)}) collective-permute-start(bf16[256,2048]{1,0:T(8,128)(2,1)} %get-tuple-element.88), channel_id=1, source_target_pairs={{0,1},{1,0},{2,3},{3,2},{4,5},{5,4},{6,7},{7,6},{8,9},{9,8},{10,11... | collective-permute-start | bytes 3145736 | tf_op jit(solution)/shard_map/ppermute | solution.py:326
  498.8 37.2 %collective-permute-start.31 = (bf16[256,2048]{1,0:T(8,128)(2,1)}, bf16[256,2048]{1,0:T(8,128)(2,1)}, u32[]{:S(2)}, u32[]{:S(2)}) collective-permute-start(bf16[256,2048]{1,0:T(8,128)(2,1)} %get-tuple-element.89), channel_id=1, source_target_pairs={{0,2},{1,3},{2,0},{3,1},{4,6},{5,7},{6,4},{7,5},{8,10},{9,11},{10,... | collective-permute-start | bytes 3145736 | tf_op jit(solution)/shard_map/ppermute | solution.py:326
  530.1 50.6 %collective-permute-start.33 = (bf16[256,2048]{1,0:T(8,128)(2,1)S(1)}, bf16[256,2048]{1,0:T(8,128)(2,1)S(1)}, u32[]{:S(2)}, u32[]{:S(2)}) collective-permute-start(bf16[256,2048]{1,0:T(8,128)(2,1)S(1)} %slice.235), channel_id=1, source_target_pairs={{0,1},{1,0},{2,3},{3,2},{4,5},{5,4},{6,7},{7,6},{8,9},{9,8},{10,11... | collective-permute-start | bytes 3145736 | tf_op jit(solution)/shard_map/ppermute | solution.py:326
  532.4 44.1 %collective-permute-start.20 = (bf16[256,2048]{1,0:T(8,128)(2,1)S(1)}, bf16[256,2048]{1,0:T(8,128)(2,1)S(1)}, u32[]{:S(2)}, u32[]{:S(2)}) collective-permute-start(bf16[256,2048]{1,0:T(8,128)(2,1)S(1)} %add_convert_fusion.10), channel_id=1, source_target_pairs={{0,1},{1,0},{2,3},{3,2},{4,5},{5,4},{6,7},{7,6},{8,9},{9,8},{10,11... | collective-permute-start | bytes 3145736 | tf_op jit(solution)/shard_map/ppermute | solution.py:326
  536.0 44.7 %collective-permute-start.30 = (bf16[256,2048]{1,0:T(8,128)(2,1)S(1)}, bf16[256,2048]{1,0:T(8,128)(2,1)S(1)}, u32[]{:S(2)}, u32[]{:S(2)}) collective-permute-start(bf16[256,2048]{1,0:T(8,128)(2,1)S(1)} %copy-done.13), channel_id=1, source_target_pairs={{0,2},{1,3},{2,0},{3,1},{4,6},{5,7},{6,4},{7,5},{8,10},{9,11},{10,... | collective-permute-start | bytes 3145736 | tf_op jit(solution)/shard_map/ppermute | solution.py:326
  537.9 83.5 %copy-start.5 = (f32[256,2048]{1,0:T(8,128)S(1)}, f32[256,2048]{1,0:T(8,128)}, u32[]{:S(2)}) copy-start(f32[256,2048]{1,0:T(8,128)} %copy-done.4) | copy-start | bytes 6291460
  537.9 83.5 %copy-start.17 = (f32[2048]{0:T(1024)S(1)}, f32[2048]{0:T(1024)}, u32[]{:S(2)}) copy-start(f32[2048]{0:T(1024)} %param.14) | copy-start | bytes 24580
  537.9 83.5 %copy-start.24 = (f32[256]{0:T(256)S(1)}, f32[256]{0:T(256)}, u32[]{:S(2)}) copy-start(f32[256]{0:T(256)} %copy-done.23) | copy-start | bytes 3076
  537.9 83.5 %copy-start.26 = (f32[256]{0:T(256)S(1)}, f32[256]{0:T(256)}, u32[]{:S(2)}) copy-start(f32[256]{0:T(256)} %copy-done.25) | copy-start | bytes 3076
  538.0 83.5 %copy-start.28 = (f32[256]{0:T(256)S(1)}, f32[256]{0:T(256)}, u32[]{:S(2)}) copy-start(f32[256]{0:T(256)} %copy-done.27) | copy-start | bytes 3076
  538.0 61.0 %collective-permute-start.21 = (bf16[256,2048]{1,0:T(8,128)(2,1)S(1)}, bf16[256,2048]{1,0:T(8,128)(2,1)S(1)}, u32[]{:S(2)}, u32[]{:S(2)}) collective-permute-start(bf16[256,2048]{1,0:T(8,128)(2,1)S(1)} %copy-done.15), channel_id=1, source_target_pairs={{0,1},{1,0},{2,3},{3,2},{4,5},{5,4},{6,7},{7,6},{8,9},{9,8},{10,11... | collective-permute-start | bytes 3145736 | tf_op jit(solution)/shard_map/ppermute | solution.py:326
  538.5 60.5 %collective-permute-start.35 = (bf16[256,2048]{1,0:T(8,128)(2,1)S(1)}, bf16[256,2048]{1,0:T(8,128)(2,1)S(1)}, u32[]{:S(2)}, u32[]{:S(2)}) collective-permute-start(bf16[256,2048]{1,0:T(8,128)(2,1)S(1)} %add_convert_fusion.4), channel_id=1, source_target_pairs={{0,2},{1,3},{2,0},{3,1},{4,6},{5,7},{6,4},{7,5},{8,10},{9,11},{10,... | collective-permute-start | bytes 3145736 | tf_op jit(solution)/shard_map/ppermute | solution.py:326
  576.5 44.9 %collective-permute-start.32 = (bf16[256,2048]{1,0:T(8,128)(2,1)S(1)}, bf16[256,2048]{1,0:T(8,128)(2,1)S(1)}, u32[]{:S(2)}, u32[]{:S(2)}) collective-permute-start(bf16[256,2048]{1,0:T(8,128)(2,1)S(1)} %add_convert_fusion.6), channel_id=1, source_target_pairs={{0,1},{1,0},{2,3},{3,2},{4,5},{5,4},{6,7},{7,6},{8,9},{9,8},{10,11... | collective-permute-start | bytes 3145736 | tf_op jit(solution)/shard_map/ppermute | solution.py:326
  580.7 40.7 %collective-permute-start.23 = (bf16[256,2048]{1,0:T(8,128)(2,1)S(1)}, bf16[256,2048]{1,0:T(8,128)(2,1)S(1)}, u32[]{:S(2)}, u32[]{:S(2)}) collective-permute-start(bf16[256,2048]{1,0:T(8,128)(2,1)S(1)} %get-tuple-element.76), channel_id=1, source_target_pairs={{0,2},{1,3},{2,0},{3,1},{4,6},{5,7},{6,4},{7,5},{8,10},{9,11},{10,... | collective-permute-start | bytes 3145736 | tf_op jit(solution)/shard_map/ppermute | solution.py:326
  628.9 25.0 %collective-permute-start.36 = (bf16[256,2048]{1,0:T(8,128)(2,1)S(1)}, bf16[256,2048]{1,0:T(8,128)(2,1)S(1)}, u32[]{:S(2)}, u32[]{:S(2)}) collective-permute-start(bf16[256,2048]{1,0:T(8,128)(2,1)S(1)} %get-tuple-element.57), channel_id=1, source_target_pairs={{0,1},{1,0},{2,3},{3,2},{4,5},{5,4},{6,7},{7,6},{8,9},{9,8},{10,11... | collective-permute-start | bytes 3145736 | tf_op jit(solution)/shard_map/ppermute | solution.py:326
  631.6 25.2 %collective-permute-start.39 = (bf16[256,2048]{1,0:T(8,128)(2,1)S(1)}, bf16[256,2048]{1,0:T(8,128)(2,1)S(1)}, u32[]{:S(2)}, u32[]{:S(2)}) collective-permute-start(bf16[256,2048]{1,0:T(8,128)(2,1)S(1)} %get-tuple-element.54), channel_id=1, source_target_pairs={{0,2},{1,3},{2,0},{3,1},{4,6},{5,7},{6,4},{7,5},{8,10},{9,11},{10,... | collective-permute-start | bytes 3145736 | tf_op jit(solution)/shard_map/ppermute | solution.py:326
  631.6 44.7 %collective-permute-start.37 = (bf16[256,2048]{1,0:T(8,128)(2,1)S(1)}, bf16[256,2048]{1,0:T(8,128)(2,1)S(1)}, u32[]{:S(2)}, u32[]{:S(2)}) collective-permute-start(bf16[256,2048]{1,0:T(8,128)(2,1)S(1)} %get-tuple-element.54), channel_id=1, source_target_pairs={{0,1},{1,0},{2,3},{3,2},{4,5},{5,4},{6,7},{7,6},{8,9},{9,8},{10,11... | collective-permute-start | bytes 3145736 | tf_op jit(solution)/shard_map/ppermute | solution.py:326
  633.2 46.1 %collective-permute-start.38 = (bf16[256,2048]{1,0:T(8,128)(2,1)S(1)}, bf16[256,2048]{1,0:T(8,128)(2,1)S(1)}, u32[]{:S(2)}, u32[]{:S(2)}) collective-permute-start(bf16[256,2048]{1,0:T(8,128)(2,1)S(1)} %get-tuple-element.57), channel_id=1, source_target_pairs={{0,2},{1,3},{2,0},{3,1},{4,6},{5,7},{6,4},{7,5},{8,10},{9,11},{10,... | collective-permute-start | bytes 3145736 | tf_op jit(solution)/shard_map/ppermute | solution.py:326
  653.9 47.9 %collective-permute-start.40 = (bf16[256,2048]{1,0:T(8,128)(2,1)S(1)}, bf16[256,2048]{1,0:T(8,128)(2,1)S(1)}, u32[]{:S(2)}, u32[]{:S(2)}) collective-permute-start(bf16[256,2048]{1,0:T(8,128)(2,1)S(1)} %collective-permute-done.36), channel_id=1, source_target_pairs={{0,2},{1,3},{2,0},{3,1},{4,6},{5,7},{6,4},{7,5},{8,10},{9,11},{10,... | collective-permute-start | bytes 3145736 | tf_op jit(solution)/shard_map/ppermute | solution.py:326
  656.9 45.0 %collective-permute-start.41 = (bf16[256,2048]{1,0:T(8,128)(2,1)S(1)}, bf16[256,2048]{1,0:T(8,128)(2,1)S(1)}, u32[]{:S(2)}, u32[]{:S(2)}) collective-permute-start(bf16[256,2048]{1,0:T(8,128)(2,1)S(1)} %collective-permute-done.39), channel_id=1, source_target_pairs={{0,1},{1,0},{2,3},{3,2},{4,5},{5,4},{6,7},{7,6},{8,9},{9,8},{10,11... | collective-permute-start | bytes 3145736 | tf_op jit(solution)/shard_map/ppermute | solution.py:326
  711.7 298.8 %reduce-scatter.12.cloned.1.call-start = ((), (), s32[]{:S(2)}) async-start(), calls=%async_computation.13 | async-start | bytes 9437184 | tf_op jit(solution)/shard_map/reduce_scatter | solution.py:479
  735.9 277.4 %reduce-scatter.10.cloned.1.call-start = ((), (), s32[]{:S(2)}) async-start(), calls=%async_computation.12 | async-start | bytes 9437184 | tf_op jit(solution)/shard_map/reduce_scatter | solution.py:479
  759.9 262.8 %reduce-scatter.14.cloned.1.call-start = ((), (), s32[]{:S(2)}) async-start(), calls=%async_computation.14 | async-start | bytes 9437184 | tf_op jit(solution)/shard_map/reduce_scatter | solution.py:479
  783.8 309.4 %reduce-scatter.6.cloned.1.call-start = ((), (), s32[]{:S(2)}) async-start(), calls=%async_computation.10 | async-start | bytes 7077888 | tf_op jit(solution)/shard_map/reduce_scatter | solution.py:479
  863.8 14.8 %collective-permute-start.46 = (bf16[256,2048]{1,0:T(8,128)(2,1)S(1)}, bf16[256,2048]{1,0:T(8,128)(2,1)S(1)}, u32[]{:S(2)}, u32[]{:S(2)}) collective-permute-start(bf16[256,2048]{1,0:T(8,128)(2,1)S(1)} %get-tuple-element.86), channel_id=1, source_target_pairs={{0,1},{1,0},{2,3},{3,2},{4,5},{5,4},{6,7},{7,6},{8,9},{9,8},{10,11... | collective-permute-start | bytes 3145736 | tf_op jit(solution)/shard_map/ppermute | solution.py:326
  865.4 14.8 %collective-permute-start.43 = (bf16[256,2048]{1,0:T(8,128)(2,1)S(1)}, bf16[256,2048]{1,0:T(8,128)(2,1)S(1)}, u32[]{:S(2)}, u32[]{:S(2)}) collective-permute-start(bf16[256,2048]{1,0:T(8,128)(2,1)S(1)} %get-tuple-element.87), channel_id=1, source_target_pairs={{0,2},{1,3},{2,0},{3,1},{4,6},{5,7},{6,4},{7,5},{8,10},{9,11},{10,... | collective-permute-start | bytes 3145736 | tf_op jit(solution)/shard_map/ppermute | solution.py:326
  873.5 16.4 %collective-permute-start.45 = (bf16[256,2048]{1,0:T(8,128)(2,1)}, bf16[256,2048]{1,0:T(8,128)(2,1)}, u32[]{:S(2)}, u32[]{:S(2)}) collective-permute-start(bf16[256,2048]{1,0:T(8,128)(2,1)} %slice.243), channel_id=1, source_target_pairs={{0,1},{1,0},{2,3},{3,2},{4,5},{5,4},{6,7},{7,6},{8,9},{9,8},{10,11... | collective-permute-start | bytes 3145736 | tf_op jit(solution)/shard_map/ppermute | solution.py:326
  874.4 17.1 %collective-permute-start.42 = (bf16[256,2048]{1,0:T(8,128)(2,1)}, bf16[256,2048]{1,0:T(8,128)(2,1)}, u32[]{:S(2)}, u32[]{:S(2)}) collective-permute-start(bf16[256,2048]{1,0:T(8,128)(2,1)} %get-tuple-element.85), channel_id=1, source_target_pairs={{0,2},{1,3},{2,0},{3,1},{4,6},{5,7},{6,4},{7,5},{8,10},{9,11},{10,... | collective-permute-start | bytes 3145736 | tf_op jit(solution)/shard_map/ppermute | solution.py:326
  879.9 31.5 %collective-permute-start.47 = (bf16[256,2048]{1,0:T(8,128)(2,1)}, bf16[256,2048]{1,0:T(8,128)(2,1)}, u32[]{:S(2)}, u32[]{:S(2)}) collective-permute-start(bf16[256,2048]{1,0:T(8,128)(2,1)} %add_convert_fusion), channel_id=1, source_target_pairs={{0,2},{1,3},{2,0},{3,1},{4,6},{5,7},{6,4},{7,5},{8,10},{9,11},{10,... | collective-permute-start | bytes 3145736 | tf_op jit(solution)/shard_map/ppermute | solution.py:326
  881.6 29.8 %collective-permute-start.44 = (bf16[256,2048]{1,0:T(8,128)(2,1)}, bf16[256,2048]{1,0:T(8,128)(2,1)}, u32[]{:S(2)}, u32[]{:S(2)}) collective-permute-start(bf16[256,2048]{1,0:T(8,128)(2,1)} %add_convert_fusion.2), channel_id=1, source_target_pairs={{0,1},{1,0},{2,3},{3,2},{4,5},{5,4},{6,7},{7,6},{8,9},{9,8},{10,11... | collective-permute-start | bytes 3145736 | tf_op jit(solution)/shard_map/ppermute | solution.py:326
  (37 other events, 458.6 us)
Sparse Core Ops, SparseCore 0:
  10.2 67.4 all-gather.5
  79.3 27.8 all-gather.7
  108.7 81.4 all-gather.9
  191.6 80.5 all-gather.11
  273.6 80.5 all-gather.13
  711.8 38.7 reduce-scatter.7
  752.9 88.0 reduce-scatter.11
  843.3 88.0 reduce-scatter.9
  933.7 89.0 reduce-scatter.13
  1024.9 68.1 reduce-scatter.5

commit v2 on v1

--- a/solution.py
+++ b/solution.py
@@ -6,6 +6,7 @@
 from jax.experimental import pallas as pl
 from jax.experimental.pallas import tpu as pltpu
 from jax.sharding import PartitionSpec as P
+
 
 HD = 64
 EPS = 1e-05
@@ -363,6 +364,25 @@
     return out
 
 
+def after(value, *others):
+    return lax.optimization_barrier((value,) + others)[0]
+
+
+def scatter_vectors(values):
+    axes = ("fsdp", "tp")
+    devices = lax.axis_size("fsdp") * lax.axis_size("tp")
+    index = lax.axis_index("fsdp") * lax.axis_size("tp") + lax.axis_index("tp")
+    bit = devices // 2
+    while bit:
+        pair = values.reshape(values.shape[0], 2, values.shape[1] // 2)
+        mine = (index // bit) % 2
+        kept = lax.dynamic_index_in_dim(pair, mine, axis=1, keepdims=False)
+        sent = lax.dynamic_index_in_dim(pair, 1 - mine, axis=1, keepdims=False)
+        values = kept + lax.ppermute(sent, axes, [(i, i ^ bit) for i in range(devices)])
+        bit //= 2
+    return values
+
+
 def split_halves(rows):
     middle = rows.shape[0] // 2
     return [rows[:middle], rows[middle:]]
@@ -404,7 +424,7 @@
     normed_one = [v * s for v, s in zip(x, scale_one)]
     h1 = gather_tp([(n * gain_attn).astype(BF16) for n in normed_one], size)
     grad_rows = [m * g.astype(F32) for m, g in zip(valid, split_halves(out_grad))]
-    dm = gather_tp([g.astype(BF16) for g in grad_rows], size)
+    dm = gather_tp([after(g.astype(BF16), h1) for g in grad_rows], size)
 
     qkv = matmul(h1, qkv_full)
     saved = {}
@@ -425,40 +445,49 @@
 
     hid, gate_slope, up_slope = gate_up(h2, gate_full, up_full)
     down_term = matmul_tn(dm, hid).astype(BF16)
-    grad_gate, grad_up = hidden_back(dm, down_full, gate_slope, up_slope)
-    gate_term = matmul_tn(h2, grad_gate).astype(BF16)
-    up_term = matmul_tn(h2, grad_up).astype(BF16)
+    grad_gate, grad_up = hidden_back(dm, down_full, after(gate_slope, down_term), up_slope)
     half_group = group // 2
-    two = [two_nt(grad_gate, grad_up, gate_full, up_full, half_group * i, half_group) for i in range(2)]
+    two = {}
+    two[1] = two_nt(grad_gate, grad_up, gate_full, up_full, half_group, half_group)
+    two[0] = two_nt(after(grad_gate, two[1]), grad_up, gate_full, up_full, 0, half_group)
+    gate_term = matmul_tn(h2, after(grad_gate, two[0])).astype(BF16)
+    up_term = matmul_tn(h2, after(grad_up, gate_term)).astype(BF16)
+    mlp = matmul_nt(after(hid, up_term), down_full).astype(BF16)
 
     def two_piece(r):
         i, inside = divmod(r, size // 2)
         return two[i][inside * own : (inside + 1) * own]
 
     grad_two = scatter_tp(two_piece, size)
-    mlp = matmul_nt(hid, down_full).astype(BF16)
-    mlp_out = scatter_tp(lambda r: mlp[r * own : (r + 1) * own], size)
-    output = jnp.concatenate(
-        [(m * (v + o)).astype(BF16) for m, v, o in zip(valid, middle, mlp_out)], axis=0
-    )
     gain_mlp_term = sum(jnp.sum(g * n, axis=0) for g, n in zip(grad_two, normed_two))
     inner_two = [g * gain_mlp for g in grad_two]
     grad_middle = [
         g + s * (i - n * jnp.mean(i * n, axis=-1, keepdims=True))
         for g, s, i, n in zip(grad_rows, scale_two, inner_two, normed_two)
     ]
-    grad_attn = gather_tp([g.astype(BF16) for g in grad_middle], size)
-
-    mixed = jnp.concatenate([saved[s][3] for s in range(count)], axis=0)
-    out_term = matmul_tn(grad_attn, mixed).astype(BF16)
+    grad_attn = gather_tp([after(g.astype(BF16), gate_term, up_term) for g in grad_middle], size)
+    mlp, grad_attn = lax.optimization_barrier((mlp, grad_attn))
+    mlp_out = scatter_tp(lambda r: mlp[r * own : (r + 1) * own], size)
+    output = jnp.concatenate(
+        [(m * (v + o)).astype(BF16) for m, v, o in zip(valid, middle, mlp_out)], axis=0
+    )
+
     grad_mixed = matmul(grad_attn, out_full).astype(BF16)
     grad_qkv = {}
     partial_one = {}
+    last = None
     for s in reversed(range(count)):
         query, keys, values, _ = saved[s]
+        if last is not None:
+            query = after(query, last)
         grad_qkv[s] = attend_back(query, keys, values, grad_mixed, s, infos[s], cosine, sine, own, length)
-        partial_one[s] = matmul_nt(grad_qkv[s], qkv_full).astype(BF16)
+        if s:
+            last = partial_one[s] = matmul_nt(grad_qkv[s], qkv_full).astype(BF16)
+        if s == count - 1:
+            mixed = after(jnp.concatenate([saved[i][3] for i in range(count)], axis=0), last)
+            last = out_term = matmul_tn(grad_attn, mixed).astype(BF16)
     qkv_term = matmul_tn(h1, jnp.concatenate([grad_qkv[s] for s in range(count)], axis=0)).astype(BF16)
+    partial_one[0] = matmul_nt(after(grad_qkv[0], qkv_term), qkv_full).astype(BF16)
 
     def one_piece(r):
         s, inside = divmod(r, per_slot)
@@ -483,10 +512,7 @@
     up_grad = back_fsdp(up_term)
     out_proj_grad = back_fsdp(out_term)
     qkv_grad = back_fsdp(qkv_term)
-    gains = [
-        lax.psum_scatter(term, ("fsdp", "tp"), scatter_dimension=0, tiled=True)
-        for term in (gain_attn_term, gain_mlp_term)
-    ]
+    gains = scatter_vectors(jnp.stack([gain_attn_term, gain_mlp_term]))
     return (
         output,
         input_grad,

time: 1110 us -> 1110 us (level)
  blocking collectives: 85.3 us -> 0 us
  waiting for transfers between devices: 450 us -> 497 us
  Pallas kernels: 202 us -> 240 us
  starting transfers between devices: 53.8 us -> 68.5 us
    unnamed x1 -> x0, blocking collectives: 85.3 us -> none
    reduce_scatter x5, waiting for transfers between devices: 74.2 us -> 144 us  [back_fsdp(): lax.psum_scatter(term, 'fsdp', scatter_dimension=0, tiled=True).astype(F32)]
    ppermute x48, waiting for transfers between devices: 374 us -> 328 us  [hop(): return lax.ppermute(value, 'tp', [(i, i ^ bit) for i in range(size)])]
    pallas_call x2, Pallas kernels: 38.9 us -> 64.9 us  [attend_back(): pl.pallas_call(functools.partial(attend_back_kernel, own), out_shape=jax....]
    ppermute x0 -> x5, waiting for transfers between devices: none -> 20.5 us  [scatter_vectors(): lax.ppermute(sent, axes, [(i, i ^ bit) for i in range(devices)])]
    ppermute x0 -> x5, starting transfers between devices: none -> 19.4 us  [scatter_vectors(): lax.ppermute(sent, axes, [(i, i ^ bit) for i in range(devices)])]
    pallas_call x2, Pallas kernels: 24.9 us -> 37 us  [attend(): pl.pallas_call(functools.partial(attend_kernel, own), out_shape=[wide] *...]
    unnamed x108 -> x126, local copies, waits for them, and re-layouts: 34.4 us -> 23.8 us
  transfers between devices with their start and end apart: 58 -> 63, of which waited for: 27 -> 29; matrix products, arithmetic and copies ran while one was open for 22% -> 22% of each run, Pallas kernels for 18% -> 10%
where the time goes in v2:
time: 1110 us
  waiting for transfers between devices  497 us (45%)
  Pallas kernels  240 us (22%)
  matrix products  172 us (15%)
  other arithmetic  73.4 us (7%)
  starting transfers between devices  68.5 us (6%)
  local copies, waits for them, and re-layouts  41.6 us (4%)
  between operations  15.2 us (1%)
    ppermute x48, waiting for transfers between devices, hop(): return lax.ppermute(value, 'tp', [(i, i ^ bit) for i in range(size)])  328 us
    reduce_scatter x5, waiting for transfers between devices, back_fsdp(): lax.psum_scatter(term, 'fsdp', scatter_dimension=0, tiled=True).astype(F32)  144 us
    dot_general x5, matrix products, matmul_tn(): lax.dot_general(left, right, (((0,), (0,)), ((), ())), preferred_element_...  96 us
    pallas_call x2, Pallas kernels, attend_back(): pl.pallas_call(functools.partial(attend_back_kernel, own), out_shape=jax....  64.9 us
    pallas_call x2, Pallas kernels, two_nt(): pl.pallas_call(two_nt_kernel, out_shape=jax.ShapeDtypeStruct((rows, width...  55.5 us
    dot_general x5, matrix products, matmul_nt(): lax.dot_general(left, right, (((1,), (1,)), ((), ())), preferred_element_...  51.2 us
    ppermute x48, starting transfers between devices, hop(): return lax.ppermute(value, 'tp', [(i, i ^ bit) for i in range(size)])  48.8 us
    pallas_call x1, Pallas kernels, gate_up(): pl.pallas_call(gate_up_kernel, out_shape=[jax.ShapeDtypeStruct((rows, wid...  48.4 us
  transfers between devices with their start and end apart: 63, of which 29 were waited for; matrix products, arithmetic and copies ran while one was open for 22% of the time, Pallas kernels for 10%

profile of v2, /device:TPU:0, one launch (start us, length us, event | category | flops | bytes accessed | tf_op | source)
XLA Modules:
  0.0 1107.7 jit_solution(13529304079435187837)
XLA Ops:
  13.8 3.0 collective-permute-start
  25.6 15.3 %collective-permute-done = bf16[256,2048]{1,0:T(8,128)(2,1)S(1)} collective-permute-done((bf16[256,2048]{1,0:T(8,128)(2,1)}, bf16[256,2048]{1,0:T(8,128)(2,1)S(1)}, u32[]{:S(2)}, u32[]{:S(2)}) %collective-permute-start) | collective-permute-done | bytes 1048608 | tf_op jit(solution)/shard_map/ppermute | solution.py:327
  47.5 16.1 %collective-permute-done.1 = bf16[256,2048]{1,0:T(8,128)(2,1)} collective-permute-done((bf16[256,2048]{1,0:T(8,128)(2,1)}, bf16[256,2048]{1,0:T(8,128)(2,1)}, u32[]{:S(2)}, u32[]{:S(2)}) %collective-permute-start.1) | collective-permute-done | bytes 1048608 | tf_op jit(solution)/shard_map/ppermute | solution.py:327
  63.6 2.3 constant_dynamic-update-slice_fusion.4
  67.2 2.4 constant_dynamic-update-slice_fusion.3
  69.6 2.3 constant_dynamic-update-slice_fusion.2
  71.9 16.3 %collective-permute-done.4 = bf16[256,2048]{1,0:T(8,128)(2,1)S(1)} collective-permute-done((bf16[256,2048]{1,0:T(8,128)(2,1)S(1)}, bf16[256,2048]{1,0:T(8,128)(2,1)S(1)}, u32[]{:S(2)}, u32[]{:S(2)}) %collective-permute-start.4) | collective-permute-done | bytes 1048608 | tf_op jit(solution)/shard_map/ppermute | solution.py:327
  90.3 19.6 %fusion.53.q_ref.k_ref.v_ref = f32[2048,1536]{1,0:T(8,128)} fusion(bf16[2048,2048]{1,0:T(8,128)(2,1)} %constant_dynamic-update-slice_fusion, bf16[2048,1536]{1,0:T(8,128)(2,1)} %all-gather.6.cloned.1.call-done), kind=kOutput, calls=%fused_computation.173 | convolution fusion | flops 12884901888 | bytes 27262976 | tf_op jit(solution)/shard_map/dot_general | solution.py:22
  109.9 20.4 %attend.3 = (bf16[1024,512]{1,0:T(8,128)(2,1)}, bf16[1024,512]{1,0:T(8,128)(2,1)}, bf16[1024,512]{1,0:T(8,128)(2,1)}, bf16[1024,512]{1,0:T(8,128)(2,1)}) custom-call(s32[2]{0:T(128)} %get-tuple-element.139.info, f32[2048,1536]{1,0:T(8,128)} %fusion.53.q_ref.k_ref.v_ref, f32[2048,1536]{1,0:T(8,128)} %fusion.53.q_ref.k_ref.v_ref, ...), custom_call_target="tpu_custom_call" | custom-call | flops 4294967296 | bytes 10485760 | tf_op jit(solution)/shard_map/attend/pallas_call | solution.py:131
  130.2 4.3 convolution_convert_fusion.7
  143.3 16.6 %attend.2 = (bf16[1024,512]{1,0:T(8,128)(2,1)}, bf16[1024,512]{1,0:T(8,128)(2,1)}, bf16[1024,512]{1,0:T(8,128)(2,1)}, bf16[1024,512]{1,0:T(8,128)(2,1)}) custom-call(s32[2]{0:T(128)} %get-tuple-element.138.info, f32[2048,1536]{1,0:T(8,128)} %fusion.53.q_ref.k_ref.v_ref, f32[2048,1536]{1,0:T(8,128)} %fusion.53.q_ref.k_ref.v_ref, ...), custom_call_target="tpu_custom_call" | custom-call | flops 4294967296 | bytes 10485760 | tf_op jit(solution)/shard_map/attend/pallas_call | solution.py:131
  159.9 4.3 convolution_convert_fusion.8
  168.2 18.8 %collective-permute-done.7 = bf16[256,2048]{1,0:T(8,128)(2,1)} collective-permute-done((bf16[256,2048]{1,0:T(8,128)(2,1)}, bf16[256,2048]{1,0:T(8,128)(2,1)}, u32[]{:S(2)}, u32[]{:S(2)}) %collective-permute-start.7) | collective-permute-done | bytes 1048608 | tf_op jit(solution)/shard_map/ppermute | solution.py:327
  190.2 18.8 %collective-permute-done.18 = bf16[256,2048]{1,0:T(8,128)(2,1)} collective-permute-done((bf16[256,2048]{1,0:T(8,128)(2,1)S(1)}, bf16[256,2048]{1,0:T(8,128)(2,1)}, u32[]{:S(2)}, u32[]{:S(2)}) %collective-permute-start.18) | collective-permute-done | bytes 1048608 | tf_op jit(solution)/shard_map/ppermute | solution.py:327
  215.4 15.9 %collective-permute-done.9 = bf16[256,2048]{1,0:T(8,128)(2,1)S(1)} collective-permute-done((bf16[256,2048]{1,0:T(8,128)(2,1)S(1)}, bf16[256,2048]{1,0:T(8,128)(2,1)S(1)}, u32[]{:S(2)}, u32[]{:S(2)}) %collective-permute-start.9) | collective-permute-done | bytes 1048608 | tf_op jit(solution)/shard_map/ppermute | solution.py:327
  231.6 3.3 collective-permute-done.11
  235.0 18.8 %collective-permute-done.8 = bf16[256,2048]{1,0:T(8,128)(2,1)S(1)} collective-permute-done((bf16[256,2048]{1,0:T(8,128)(2,1)S(1)}, bf16[256,2048]{1,0:T(8,128)(2,1)S(1)}, u32[]{:S(2)}, u32[]{:S(2)}) %collective-permute-start.8) | collective-permute-done | bytes 1048608 | tf_op jit(solution)/shard_map/ppermute | solution.py:327
  261.9 18.1 %collective-permute-done.22 = bf16[256,2048]{1,0:T(8,128)(2,1)S(1)} collective-permute-done((bf16[256,2048]{1,0:T(8,128)(2,1)}, bf16[256,2048]{1,0:T(8,128)(2,1)S(1)}, u32[]{:S(2)}, u32[]{:S(2)}) %collective-permute-start.22) | collective-permute-done | bytes 1048608 | tf_op jit(solution)/shard_map/ppermute | solution.py:327
  281.4 17.3 %collective-permute-done.12 = bf16[256,2048]{1,0:T(8,128)(2,1)S(1)} collective-permute-done((bf16[256,2048]{1,0:T(8,128)(2,1)S(1)}, bf16[256,2048]{1,0:T(8,128)(2,1)S(1)}, u32[]{:S(2)}, u32[]{:S(2)}) %collective-permute-start.12) | collective-permute-done | bytes 1048608 | tf_op jit(solution)/shard_map/ppermute | solution.py:327
  304.1 17.1 %collective-permute-done.13 = bf16[256,2048]{1,0:T(8,128)(2,1)S(1)} collective-permute-done((bf16[256,2048]{1,0:T(8,128)(2,1)S(1)}, bf16[256,2048]{1,0:T(8,128)(2,1)S(1)}, u32[]{:S(2)}, u32[]{:S(2)}) %collective-permute-start.13) | collective-permute-done | bytes 1048608 | tf_op jit(solution)/shard_map/ppermute | solution.py:327
  322.3 2.5 collective-permute-done.14
  327.1 18.4 %collective-permute-done.16 = bf16[256,2048]{1,0:T(8,128)(2,1)S(1)} collective-permute-done((bf16[256,2048]{1,0:T(8,128)(2,1)S(1)}, bf16[256,2048]{1,0:T(8,128)(2,1)S(1)}, u32[]{:S(2)}, u32[]{:S(2)}) %collective-permute-start.16) | collective-permute-done | bytes 1048608 | tf_op jit(solution)/shard_map/ppermute | solution.py:327
  347.6 48.4 %gate_up.1 = (bf16[2048,2048]{1,0:T(8,128)(2,1)}, bf16[2048,2048]{1,0:T(8,128)(2,1)}, bf16[2048,2048]{1,0:T(8,128)(2,1)}) custom-call(bf16[2048,2048]{1,0:T(8,128)(2,1)} %constant_dynamic-update-slice_fusion.8.h_ref, bf16[2048,2048]{1,0:T(8,128)(2,1)} %all-gather.10.cloned.1.call-done.g_ref.wa_ref, bf16[2048,2048]{1,0:T(8,128)(2,1)} %all-gather.12.cloned.1.call-done.u_ref.wb_ref), custom_call_target="tpu_custom_call" | custom-call | flops 34359738368 | bytes 50331648 | tf_op jit(solution)/shard_map/gate_up/pallas_call | solution.py:261
  396.0 23.8 %convolution_convert_fusion.3 = bf16[2048,2048]{1,0:T(8,128)(2,1)} fusion(bf16[2048,2048]{1,0:T(8,128)(2,1)} %copy-done.24, bf16[2048,2048]{1,0:T(8,128)(2,1)} %get-tuple-element.51), kind=kOutput, calls=%fused_computation.3 | convolution fusion | flops 17184063488 | bytes 25165824 | tf_op jit(solution)/shard_map/dot_general | solution.py:30
  419.8 34.1 %hidden_back.1 = (bf16[2048,2048]{1,0:T(8,128)(2,1)}, bf16[2048,2048]{1,0:T(8,128)(2,1)}) custom-call(bf16[2048,2048]{1,0:T(8,128)(2,1)} %copy-done.24, bf16[2048,2048]{1,0:T(8,128)(2,1)} %all-gather.14.cloned.1.call-done.w_ref, bf16[2048,2048]{1,0:T(8,128)(2,1)} %get-tuple-element.44.gate_slope, bf16[2048,2048]{1,0:T(8,128)(2,1)} %get-tuple-element.45.up_slope), custom_call_target="tpu_custom_call" | custom-call | flops 17179869184 | bytes 50331648 | tf_op jit(solution)/shard_map/hidden_back/pallas_call | solution.py:285
  453.9 27.7 %two_nt.2 = bf16[1024,2048]{1,0:T(8,128)(2,1)} custom-call(bf16[2048,2048]{1,0:T(8,128)(2,1)} %get-tuple-element.49.a_ref, bf16[2048,2048]{1,0:T(8,128)(2,1)} %get-tuple-element.50.b_ref, bf16[2048,2048]{1,0:T(8,128)(2,1)} %all-gather.10.cloned.1.call-done.g_ref.wa_ref, bf16[2048,2048]{1,0:T(8,128)(2,1)} %all-gather.12.cloned.1.call-done.u_ref.wb_ref), custom_call_target="tpu_custom_call" | custom-call | flops 17179869184 | bytes 29360128 | tf_op jit(solution)/shard_map/two_nt/pallas_call | solution.py:313
  481.6 3.6 fusion.48
  485.2 27.8 %two_nt.3 = bf16[1024,2048]{1,0:T(8,128)(2,1)} custom-call(bf16[2048,2048]{1,0:T(8,128)(2,1)} %get-tuple-element.49.a_ref, bf16[2048,2048]{1,0:T(8,128)(2,1)} %get-tuple-element.50.b_ref, bf16[2048,2048]{1,0:T(8,128)(2,1)} %all-gather.10.cloned.1.call-done.g_ref.wa_ref, bf16[2048,2048]{1,0:T(8,128)(2,1)} %all-gather.12.cloned.1.call-done.u_ref.wb_ref), custom_call_target="tpu_custom_call" | custom-call | flops 17179869184 | bytes 29360128 | tf_op jit(solution)/shard_map/two_nt/pallas_call | solution.py:313
  513.0 2.3 slice.235
  519.3 24.1 %convolution_convert_fusion.2 = bf16[2048,2048]{1,0:T(8,128)(2,1)} fusion(bf16[2048,2048]{1,0:T(8,128)(2,1)} %constant_dynamic-update-slice_fusion.8.h_ref, bf16[2048,2048]{1,0:T(8,128)(2,1)} %get-tuple-element.49.a_ref), kind=kOutput, calls=%fused_computation.2 | convolution fusion | flops 17184063488 | bytes 25165824 | tf_op jit(solution)/shard_map/dot_general | solution.py:30
  543.4 2.6 add_convert_fusion.8
  547.7 2.6 add_convert_fusion.10
  551.2 23.8 %convolution_convert_fusion.1 = bf16[2048,2048]{1,0:T(8,128)(2,1)} fusion(bf16[2048,2048]{1,0:T(8,128)(2,1)} %constant_dynamic-update-slice_fusion.8.h_ref, bf16[2048,2048]{1,0:T(8,128)(2,1)} %get-tuple-element.50.b_ref), kind=kOutput, calls=%fused_computation.1 | convolution fusion | flops 17184063488 | bytes 25165824 | tf_op jit(solution)/shard_map/dot_general | solution.py:30
  575.0 9.6 collective-permute-done.29
  584.7 4.7 multiply_reduce_fusion.1
  589.4 5.4 fusion.42
  599.0 21.6 %convolution_convert_fusion = bf16[2048,2048]{1,0:T(8,128)(2,1)} fusion(bf16[2048,2048]{1,0:T(8,128)(2,1)} %get-tuple-element.51, bf16[2048,2048]{1,0:T(8,128)(2,1)S(1)} %bitcast.64), kind=kOutput, calls=%fused_computation | convolution fusion | flops 17184063488 | bytes 25165824 | tf_op jit(solution)/shard_map/dot_general | solution.py:26
  622.8 22.1 %collective-permute-done.33 = bf16[256,2048]{1,0:T(8,128)(2,1)S(1)} collective-permute-done((bf16[256,2048]{1,0:T(8,128)(2,1)S(1)}, bf16[256,2048]{1,0:T(8,128)(2,1)S(1)}, u32[]{:S(2)}, u32[]{:S(2)}) %collective-permute-start.33) | collective-permute-done | bytes 1048608 | tf_op jit(solution)/shard_map/ppermute | solution.py:327
  645.9 17.9 %collective-permute-done.34 = bf16[256,2048]{1,0:T(8,128)(2,1)S(1)} collective-permute-done((bf16[256,2048]{1,0:T(8,128)(2,1)S(1)}, bf16[256,2048]{1,0:T(8,128)(2,1)S(1)}, u32[]{:S(2)}, u32[]{:S(2)}) %collective-permute-start.34) | collective-permute-done | bytes 1048608 | tf_op jit(solution)/shard_map/ppermute | solution.py:327
  664.0 5.6 convolution_convert_fusion.10.g_ref
  669.7 36.9 %attend_back.2 = bf16[1024,1536]{1,0:T(8,128)(2,1)} custom-call(s32[2]{0:T(128)} %get-tuple-element.139.info, bf16[1024,512]{1,0:T(8,128)(2,1)} %get-tuple-element.57.q_ref, bf16[1024,512]{1,0:T(8,128)(2,1)} %get-tuple-element.58.k_ref, bf16[1024,512]{1,0:T(8,128)(2,1)} %get-tuple-element.59.v_ref, bf16[2048,512]{1,0:T(8,128)(2,1)} %convolution_convert_fusion.10.g_ref, ...), custom_call_target="tpu_custom_call" | custom-call | flops 10737418240 | bytes 10485760 | tf_op jit(solution)/shard_map/attend_back/pallas_call | solution.py:223
  706.6 11.3 %convolution_convert_fusion.6 = bf16[1024,2048]{1,0:T(8,128)(2,1)} fusion(bf16[1024,1536]{1,0:T(8,128)(2,1)} %attend_back.2, bf16[2048,1536]{1,0:T(8,128)(2,1)} %all-gather.6.cloned.1.call-done), kind=kOutput, calls=%fused_computation.9 | convolution fusion | flops 6444548096 | bytes 13631488 | tf_op jit(solution)/shard_map/dot_general | solution.py:26
  717.9 5.8 convolution_convert_fusion.9
  725.2 28.0 %attend_back.3 = bf16[1024,1536]{1,0:T(8,128)(2,1)} custom-call(s32[2]{0:T(128)} %get-tuple-element.138.info, bf16[1024,512]{1,0:T(8,128)(2,1)} %get-tuple-element.61.q_ref, bf16[1024,512]{1,0:T(8,128)(2,1)} %get-tuple-element.62.k_ref, bf16[1024,512]{1,0:T(8,128)(2,1)} %get-tuple-element.63.v_ref, bf16[2048,512]{1,0:T(8,128)(2,1)} %convolution_convert_fusion.10.g_ref, ...), custom_call_target="tpu_custom_call" | custom-call | flops 10737418240 | bytes 10485760 | tf_op jit(solution)/shard_map/attend_back/pallas_call | solution.py:223
  753.2 18.6 %convolution_convert_fusion.4 = bf16[2048,1536]{1,0:T(8,128)(2,1)} fusion(bf16[2048,2048]{1,0:T(8,128)(2,1)} %constant_dynamic-update-slice_fusion, bf16[1024,1536]{1,0:T(8,128)(2,1)S(1)} %copy-done.43, bf16[1024,1536]{1,0:T(8,128)(2,1)} %attend_back.3), kind=kOutput, calls=%fused_computation.4 | convolution fusion | flops 12900630528 | bytes 20971520 | tf_op jit(solution)/shard_map/dot_general | solution.py:30
  772.4 2.3 fusion.47
  777.0 9.7 convolution_convert_fusion.5
  792.2 3.9 collective-permute-done.46
  801.2 40.6 %collective-permute-done.37 = bf16[256,2048]{1,0:T(8,128)(2,1)S(1)} collective-permute-done((bf16[256,2048]{1,0:T(8,128)(2,1)S(1)}, bf16[256,2048]{1,0:T(8,128)(2,1)S(1)}, u32[]{:S(2)}, u32[]{:S(2)}) %collective-permute-start.37) | collective-permute-done | bytes 1048608 | tf_op jit(solution)/shard_map/ppermute | solution.py:327
  846.7 17.6 %collective-permute-done.47 = bf16[256,2048]{1,0:T(8,128)(2,1)S(1)} collective-permute-done((bf16[256,2048]{1,0:T(8,128)(2,1)S(1)}, bf16[256,2048]{1,0:T(8,128)(2,1)S(1)}, u32[]{:S(2)}, u32[]{:S(2)}) %collective-permute-start.47) | collective-permute-done | bytes 1048608 | tf_op jit(solution)/shard_map/ppermute | solution.py:327
  866.7 4.1 fusion.17
  870.9 15.9 %collective-permute-done.36 = bf16[256,2048]{1,0:T(8,128)(2,1)} collective-permute-done((bf16[256,2048]{1,0:T(8,128)(2,1)}, bf16[256,2048]{1,0:T(8,128)(2,1)}, u32[]{:S(2)}, u32[]{:S(2)}) %collective-permute-start.36) | collective-permute-done | bytes 1048608 | tf_op jit(solution)/shard_map/ppermute | solution.py:327
  886.9 4.7 multiply_convert_fusion.1
  891.7 7.1 collective-permute-start.49
  900.7 9.4 collective-permute-start.50
  912.2 5.8 fusion.16
  918.0 17.5 %collective-permute-done.51 = f32[2,128]{1,0:T(2,128)S(1)} collective-permute-done((f32[2,128]{1,0:T(2,128)S(1)}, f32[2,128]{1,0:T(2,128)S(1)}, u32[]{:S(2)}, u32[]{:S(2)}) %collective-permute-start.51) | collective-permute-done | bytes 1056 | tf_op jit(solution)/shard_map/ppermute | solution.py:381
  939.8 2.6 multiply_convert_fusion
  945.8 2.8 convert_element_type.386
  948.6 2.8 convert_element_type.385
  951.4 56.4 %reduce-scatter.6.cloned.1.call-done = bf16[256,1536]{1,0:T(8,128)(2,1)} async-done(((bf16[2048,1536]{1,0:T(8,128)(2,1)}), bf16[256,1536]{1,0:T(8,128)(2,1)}) %reduce-scatter.6.cloned.1.call-update) | async-done | bytes 786448 | tf_op jit(solution)/shard_map/reduce_scatter | solution.py:508
  1007.8 2.3 fusion.50
  1010.1 87.8 %reduce-scatter.14.cloned.1.call-done = bf16[256,2048]{1,0:T(8,128)(2,1)} async-done(((bf16[2048,2048]{1,0:T(8,128)(2,1)}), bf16[256,2048]{1,0:T(8,128)(2,1)}) %reduce-scatter.14.cloned.1.call-update) | async-done | bytes 1048592 | tf_op jit(solution)/shard_map/reduce_scatter | solution.py:508
  1097.9 2.8 convert_element_type.387
  (293 shorter events, 116.3 us)
Async XLA Ops:
  7.2 83.1 %all-gather.6.cloned.1.call-start = ((), (), s32[]{:S(2)}) async-start(), calls=%async_computation.5 | async-start | bytes 7077888 | tf_op jit(solution)/shard_map/all_gather | solution.py:406
  9.4 120.8 %all-gather.8.cloned.1.call-start = ((), (), s32[]{:S(2)}) async-start(), calls=%async_computation.6 | async-start | bytes 2359296 | tf_op jit(solution)/shard_map/all_gather | solution.py:406
  10.2 337.4 %all-gather.10.cloned.1.call-start = ((), (), s32[]{:S(2)}) async-start(), calls=%async_computation.7 | async-start | bytes 9437184 | tf_op jit(solution)/shard_map/all_gather | solution.py:406
  10.9 336.7 %all-gather.12.cloned.1.call-start = ((), (), s32[]{:S(2)}) async-start(), calls=%async_computation.8 | async-start | bytes 9437184 | tf_op jit(solution)/shard_map/all_gather | solution.py:406
  11.5 408.2 %all-gather.14.cloned.1.call-start = ((), (), s32[]{:S(2)}) async-start(), calls=%async_computation.9 | async-start | bytes 9437184 | tf_op jit(solution)/shard_map/all_gather | solution.py:406
  13.8 27.2 %collective-permute-start = (bf16[256,2048]{1,0:T(8,128)(2,1)}, bf16[256,2048]{1,0:T(8,128)(2,1)S(1)}, u32[]{:S(2)}, u32[]{:S(2)}) collective-permute-start(bf16[256,2048]{1,0:T(8,128)(2,1)} %get-tuple-element.94), channel_id=1, source_target_pairs={{0,1},{1,0},{2,3},{3,2},{4,5},{5,4},{6,7},{7,6},{8,9},{9,8},{10,11... | collective-permute-start | bytes 3145736 | tf_op jit(solution)/shard_map/ppermute | solution.py:327
  18.4 26.6 %collective-permute-start.3 = (bf16[256,2048]{1,0:T(8,128)(2,1)}, bf16[256,2048]{1,0:T(8,128)(2,1)}, u32[]{:S(2)}, u32[]{:S(2)}) collective-permute-start(bf16[256,2048]{1,0:T(8,128)(2,1)} %get-tuple-element.92), channel_id=1, source_target_pairs={{0,2},{1,3},{2,0},{3,1},{4,6},{5,7},{6,4},{7,5},{8,10},{9,11},{10,... | collective-permute-start | bytes 3145736 | tf_op jit(solution)/shard_map/ppermute | solution.py:327
  19.9 43.7 %collective-permute-start.1 = (bf16[256,2048]{1,0:T(8,128)(2,1)}, bf16[256,2048]{1,0:T(8,128)(2,1)}, u32[]{:S(2)}, u32[]{:S(2)}) collective-permute-start(bf16[256,2048]{1,0:T(8,128)(2,1)} %get-tuple-element.92), channel_id=1, source_target_pairs={{0,1},{1,0},{2,3},{3,2},{4,5},{5,4},{6,7},{7,6},{8,9},{9,8},{10,11... | collective-permute-start | bytes 3145736 | tf_op jit(solution)/shard_map/ppermute | solution.py:327
  20.4 46.8 %collective-permute-start.2 = (bf16[256,2048]{1,0:T(8,128)(2,1)}, bf16[256,2048]{1,0:T(8,128)(2,1)}, u32[]{:S(2)}, u32[]{:S(2)}) collective-permute-start(bf16[256,2048]{1,0:T(8,128)(2,1)} %get-tuple-element.94), channel_id=1, source_target_pairs={{0,2},{1,3},{2,0},{3,1},{4,6},{5,7},{6,4},{7,5},{8,10},{9,11},{10,... | collective-permute-start | bytes 3145736 | tf_op jit(solution)/shard_map/ppermute | solution.py:327
  20.5 923.5 %reduce-scatter.8.cloned.1.call-start = ((), (), s32[]{:S(2)}) async-start(), calls=%async_computation.11 | async-start | bytes 2359296 | tf_op jit(solution)/shard_map/reduce_scatter | solution.py:508
  25.6 112.4 %copy-start.34 = (f32[256]{0:T(256)}, f32[256]{0:T(256)S(1)}, u32[]{:S(2)}) copy-start(f32[256]{0:T(256)S(1)} %get-tuple-element.129) | copy-start | bytes 3076
  41.0 47.2 %collective-permute-start.4 = (bf16[256,2048]{1,0:T(8,128)(2,1)S(1)}, bf16[256,2048]{1,0:T(8,128)(2,1)S(1)}, u32[]{:S(2)}, u32[]{:S(2)}) collective-permute-start(bf16[256,2048]{1,0:T(8,128)(2,1)S(1)} %collective-permute-done), channel_id=1, source_target_pairs={{0,2},{1,3},{2,0},{3,1},{4,6},{5,7},{6,4},{7,5},{8,10},{9,11},{10,... | collective-permute-start | bytes 3145736 | tf_op jit(solution)/shard_map/ppermute | solution.py:327
  45.0 44.2 %collective-permute-start.5 = (bf16[256,2048]{1,0:T(8,128)(2,1)}, bf16[256,2048]{1,0:T(8,128)(2,1)S(1)}, u32[]{:S(2)}, u32[]{:S(2)}) collective-permute-start(bf16[256,2048]{1,0:T(8,128)(2,1)} %collective-permute-done.3), channel_id=1, source_target_pairs={{0,1},{1,0},{2,3},{3,2},{4,5},{5,4},{6,7},{7,6},{8,9},{9,8},{10,11... | collective-permute-start | bytes 3145736 | tf_op jit(solution)/shard_map/ppermute | solution.py:327
  137.7 26.7 %collective-permute-start.10 = (bf16[256,2048]{1,0:T(8,128)(2,1)}, bf16[256,2048]{1,0:T(8,128)(2,1)}, u32[]{:S(2)}, u32[]{:S(2)}) collective-permute-start(bf16[256,2048]{1,0:T(8,128)(2,1)} %get-tuple-element.114), channel_id=1, source_target_pairs={{0,1},{1,0},{2,3},{3,2},{4,5},{5,4},{6,7},{7,6},{8,9},{9,8},{10,11... | collective-permute-start | bytes 3145736 | tf_op jit(solution)/shard_map/ppermute | solution.py:327
  139.3 69.7 %collective-permute-start.19 = (bf16[256,2048]{1,0:T(8,128)(2,1)}, bf16[256,2048]{1,0:T(8,128)(2,1)}, u32[]{:S(2)}, u32[]{:S(2)}) collective-permute-start(bf16[256,2048]{1,0:T(8,128)(2,1)} %get-tuple-element.42), channel_id=1, source_target_pairs={{0,1},{1,0},{2,3},{3,2},{4,5},{5,4},{6,7},{7,6},{8,9},{9,8},{10,11... | collective-permute-start | bytes 3145736 | tf_op jit(solution)/shard_map/ppermute | solution.py:327
  141.0 72.4 %collective-permute-start.21 = (bf16[256,2048]{1,0:T(8,128)(2,1)}, bf16[256,2048]{1,0:T(8,128)(2,1)}, u32[]{:S(2)}, u32[]{:S(2)}) collective-permute-start(bf16[256,2048]{1,0:T(8,128)(2,1)} %get-tuple-element.42), channel_id=1, source_target_pairs={{0,2},{1,3},{2,0},{3,1},{4,6},{5,7},{6,4},{7,5},{8,10},{9,11},{10,... | collective-permute-start | bytes 3145736 | tf_op jit(solution)/shard_map/ppermute | solution.py:327
  141.0 68.0 %collective-permute-start.18 = (bf16[256,2048]{1,0:T(8,128)(2,1)S(1)}, bf16[256,2048]{1,0:T(8,128)(2,1)}, u32[]{:S(2)}, u32[]{:S(2)}) collective-permute-start(bf16[256,2048]{1,0:T(8,128)(2,1)S(1)} %get-tuple-element.41), channel_id=1, source_target_pairs={{0,1},{1,0},{2,3},{3,2},{4,5},{5,4},{6,7},{7,6},{8,9},{9,8},{10,11... | collective-permute-start | bytes 3145736 | tf_op jit(solution)/shard_map/ppermute | solution.py:327
  141.3 45.7 %collective-permute-start.7 = (bf16[256,2048]{1,0:T(8,128)(2,1)}, bf16[256,2048]{1,0:T(8,128)(2,1)}, u32[]{:S(2)}, u32[]{:S(2)}) collective-permute-start(bf16[256,2048]{1,0:T(8,128)(2,1)} %get-tuple-element.115), channel_id=1, source_target_pairs={{0,2},{1,3},{2,0},{3,1},{4,6},{5,7},{6,4},{7,5},{8,10},{9,11},{10,... | collective-permute-start | bytes 3145736 | tf_op jit(solution)/shard_map/ppermute | solution.py:327
  164.4 66.9 %collective-permute-start.9 = (bf16[256,2048]{1,0:T(8,128)(2,1)S(1)}, bf16[256,2048]{1,0:T(8,128)(2,1)S(1)}, u32[]{:S(2)}, u32[]{:S(2)}) collective-permute-start(bf16[256,2048]{1,0:T(8,128)(2,1)S(1)} %slice.227), channel_id=1, source_target_pairs={{0,1},{1,0},{2,3},{3,2},{4,5},{5,4},{6,7},{7,6},{8,9},{9,8},{10,11... | collective-permute-start | bytes 3145736 | tf_op jit(solution)/shard_map/ppermute | solution.py:327
  187.0 44.3 %collective-permute-start.6 = (bf16[256,2048]{1,0:T(8,128)(2,1)S(1)}, bf16[256,2048]{1,0:T(8,128)(2,1)S(1)}, u32[]{:S(2)}, u32[]{:S(2)}) collective-permute-start(bf16[256,2048]{1,0:T(8,128)(2,1)S(1)} %copy-done.17), channel_id=1, source_target_pairs={{0,2},{1,3},{2,0},{3,1},{4,6},{5,7},{6,4},{7,5},{8,10},{9,11},{10,... | collective-permute-start | bytes 3145736 | tf_op jit(solution)/shard_map/ppermute | solution.py:327
  209.0 26.0 %collective-permute-start.11 = (bf16[256,2048]{1,0:T(8,128)(2,1)S(1)}, bf16[256,2048]{1,0:T(8,128)(2,1)S(1)}, u32[]{:S(2)}, u32[]{:S(2)}) collective-permute-start(bf16[256,2048]{1,0:T(8,128)(2,1)S(1)} %add_convert_fusion.12), channel_id=1, source_target_pairs={{0,2},{1,3},{2,0},{3,1},{4,6},{5,7},{6,4},{7,5},{8,10},{9,11},{10,... | collective-permute-start | bytes 3145736 | tf_op jit(solution)/shard_map/ppermute | solution.py:327
  209.0 44.8 %collective-permute-start.8 = (bf16[256,2048]{1,0:T(8,128)(2,1)S(1)}, bf16[256,2048]{1,0:T(8,128)(2,1)S(1)}, u32[]{:S(2)}, u32[]{:S(2)}) collective-permute-start(bf16[256,2048]{1,0:T(8,128)(2,1)S(1)} %add_convert_fusion.14), channel_id=1, source_target_pairs={{0,1},{1,0},{2,3},{3,2},{4,5},{5,4},{6,7},{7,6},{8,9},{9,8},{10,11... | collective-permute-start | bytes 3145736 | tf_op jit(solution)/shard_map/ppermute | solution.py:327
  213.4 45.6 %collective-permute-start.20 = (bf16[256,2048]{1,0:T(8,128)(2,1)S(1)}, bf16[256,2048]{1,0:T(8,128)(2,1)S(1)}, u32[]{:S(2)}, u32[]{:S(2)}) collective-permute-start(bf16[256,2048]{1,0:T(8,128)(2,1)S(1)} %get-tuple-element.41), channel_id=1, source_target_pairs={{0,2},{1,3},{2,0},{3,1},{4,6},{5,7},{6,4},{7,5},{8,10},{9,11},{10,... | collective-permute-start | bytes 3145736 | tf_op jit(solution)/shard_map/ppermute | solution.py:327
  231.3 48.6 %collective-permute-start.22 = (bf16[256,2048]{1,0:T(8,128)(2,1)}, bf16[256,2048]{1,0:T(8,128)(2,1)S(1)}, u32[]{:S(2)}, u32[]{:S(2)}) collective-permute-start(bf16[256,2048]{1,0:T(8,128)(2,1)} %collective-permute-done.18), channel_id=1, source_target_pairs={{0,2},{1,3},{2,0},{3,1},{4,6},{5,7},{6,4},{7,5},{8,10},{9,11},{10,... | collective-permute-start | bytes 3145736 | tf_op jit(solution)/shard_map/ppermute | solution.py:327
  231.3 50.0 %collective-permute-start.23 = (bf16[256,2048]{1,0:T(8,128)(2,1)}, bf16[256,2048]{1,0:T(8,128)(2,1)S(1)}, u32[]{:S(2)}, u32[]{:S(2)}) collective-permute-start(bf16[256,2048]{1,0:T(8,128)(2,1)} %collective-permute-done.21), channel_id=1, source_target_pairs={{0,1},{1,0},{2,3},{3,2},{4,5},{5,4},{6,7},{7,6},{8,9},{9,8},{10,11... | collective-permute-start | bytes 3145736 | tf_op jit(solution)/shard_map/ppermute | solution.py:327
  257.1 41.7 %collective-permute-start.12 = (bf16[256,2048]{1,0:T(8,128)(2,1)S(1)}, bf16[256,2048]{1,0:T(8,128)(2,1)S(1)}, u32[]{:S(2)}, u32[]{:S(2)}) collective-permute-start(bf16[256,2048]{1,0:T(8,128)(2,1)S(1)} %get-tuple-element.88), channel_id=1, source_target_pairs={{0,1},{1,0},{2,3},{3,2},{4,5},{5,4},{6,7},{7,6},{8,9},{9,8},{10,11... | collective-permute-start | bytes 3145736 | tf_op jit(solution)/shard_map/ppermute | solution.py:327
  259.0 43.4 %collective-permute-start.15 = (bf16[256,2048]{1,0:T(8,128)(2,1)S(1)}, bf16[256,2048]{1,0:T(8,128)(2,1)S(1)}, u32[]{:S(2)}, u32[]{:S(2)}) collective-permute-start(bf16[256,2048]{1,0:T(8,128)(2,1)S(1)} %get-tuple-element.84), channel_id=1, source_target_pairs={{0,2},{1,3},{2,0},{3,1},{4,6},{5,7},{6,4},{7,5},{8,10},{9,11},{10,... | collective-permute-start | bytes 3145736 | tf_op jit(solution)/shard_map/ppermute | solution.py:327
  259.1 62.1 %collective-permute-start.13 = (bf16[256,2048]{1,0:T(8,128)(2,1)S(1)}, bf16[256,2048]{1,0:T(8,128)(2,1)S(1)}, u32[]{:S(2)}, u32[]{:S(2)}) collective-permute-start(bf16[256,2048]{1,0:T(8,128)(2,1)S(1)} %get-tuple-element.84), channel_id=1, source_target_pairs={{0,1},{1,0},{2,3},{3,2},{4,5},{5,4},{6,7},{7,6},{8,9},{9,8},{10,11... | collective-permute-start | bytes 3145736 | tf_op jit(solution)/shard_map/ppermute | solution.py:327
  279.9 44.9 %collective-permute-start.14 = (bf16[256,2048]{1,0:T(8,128)(2,1)S(1)}, bf16[256,2048]{1,0:T(8,128)(2,1)S(1)}, u32[]{:S(2)}, u32[]{:S(2)}) collective-permute-start(bf16[256,2048]{1,0:T(8,128)(2,1)S(1)} %get-tuple-element.88), channel_id=1, source_target_pairs={{0,2},{1,3},{2,0},{3,1},{4,6},{5,7},{6,4},{7,5},{8,10},{9,11},{10,... | collective-permute-start | bytes 3145736 | tf_op jit(solution)/shard_map/ppermute | solution.py:327
  298.7 46.7 %collective-permute-start.16 = (bf16[256,2048]{1,0:T(8,128)(2,1)S(1)}, bf16[256,2048]{1,0:T(8,128)(2,1)S(1)}, u32[]{:S(2)}, u32[]{:S(2)}) collective-permute-start(bf16[256,2048]{1,0:T(8,128)(2,1)S(1)} %collective-permute-done.12), channel_id=1, source_target_pairs={{0,2},{1,3},{2,0},{3,1},{4,6},{5,7},{6,4},{7,5},{8,10},{9,11},{10,... | collective-permute-start | bytes 3145736 | tf_op jit(solution)/shard_map/ppermute | solution.py:327
  302.4 44.1 %collective-permute-start.17 = (bf16[256,2048]{1,0:T(8,128)(2,1)S(1)}, bf16[256,2048]{1,0:T(8,128)(2,1)S(1)}, u32[]{:S(2)}, u32[]{:S(2)}) collective-permute-start(bf16[256,2048]{1,0:T(8,128)(2,1)S(1)} %collective-permute-done.15), channel_id=1, source_target_pairs={{0,1},{1,0},{2,3},{3,2},{4,5},{5,4},{6,7},{7,6},{8,9},{9,8},{10,11... | collective-permute-start | bytes 3145736 | tf_op jit(solution)/shard_map/ppermute | solution.py:327
  515.3 28.2 %collective-permute-start.28 = (bf16[256,2048]{1,0:T(8,128)(2,1)}, bf16[256,2048]{1,0:T(8,128)(2,1)S(1)}, u32[]{:S(2)}, u32[]{:S(2)}) collective-permute-start(bf16[256,2048]{1,0:T(8,128)(2,1)} %get-tuple-element.110), channel_id=1, source_target_pairs={{0,1},{1,0},{2,3},{3,2},{4,5},{5,4},{6,7},{7,6},{8,9},{9,8},{10,11... | collective-permute-start | bytes 3145736 | tf_op jit(solution)/shard_map/ppermute | solution.py:327
  516.1 31.6 %collective-permute-start.25 = (bf16[256,2048]{1,0:T(8,128)(2,1)}, bf16[256,2048]{1,0:T(8,128)(2,1)S(1)}, u32[]{:S(2)}, u32[]{:S(2)}) collective-permute-start(bf16[256,2048]{1,0:T(8,128)(2,1)} %get-tuple-element.111), channel_id=1, source_target_pairs={{0,2},{1,3},{2,0},{3,1},{4,6},{5,7},{6,4},{7,5},{8,10},{9,11},{10,... | collective-permute-start | bytes 3145736 | tf_op jit(solution)/shard_map/ppermute | solution.py:327
  517.8 57.2 %collective-permute-start.27 = (bf16[256,2048]{1,0:T(8,128)(2,1)}, bf16[256,2048]{1,0:T(8,128)(2,1)S(1)}, u32[]{:S(2)}, u32[]{:S(2)}) collective-permute-start(bf16[256,2048]{1,0:T(8,128)(2,1)} %slice.235), channel_id=1, source_target_pairs={{0,1},{1,0},{2,3},{3,2},{4,5},{5,4},{6,7},{7,6},{8,9},{9,8},{10,11... | collective-permute-start | bytes 3145736 | tf_op jit(solution)/shard_map/ppermute | solution.py:327
  519.0 56.0 %collective-permute-start.24 = (bf16[256,2048]{1,0:T(8,128)(2,1)}, bf16[256,2048]{1,0:T(8,128)(2,1)}, u32[]{:S(2)}, u32[]{:S(2)}) collective-permute-start(bf16[256,2048]{1,0:T(8,128)(2,1)} %get-tuple-element.112), channel_id=1, source_target_pairs={{0,2},{1,3},{2,0},{3,1},{4,6},{5,7},{6,4},{7,5},{8,10},{9,11},{10,... | collective-permute-start | bytes 3145736 | tf_op jit(solution)/shard_map/ppermute | solution.py:327
  546.0 38.6 %collective-permute-start.29 = (bf16[256,2048]{1,0:T(8,128)(2,1)}, bf16[256,2048]{1,0:T(8,128)(2,1)}, u32[]{:S(2)}, u32[]{:S(2)}) collective-permute-start(bf16[256,2048]{1,0:T(8,128)(2,1)} %add_convert_fusion.8), channel_id=1, source_target_pairs={{0,2},{1,3},{2,0},{3,1},{4,6},{5,7},{6,4},{7,5},{8,10},{9,11},{10,... | collective-permute-start | bytes 3145736 | tf_op jit(solution)/shard_map/ppermute | solution.py:327
  550.3 34.3 %collective-permute-start.26 = (bf16[256,2048]{1,0:T(8,128)(2,1)}, bf16[256,2048]{1,0:T(8,128)(2,1)}, u32[]{:S(2)}, u32[]{:S(2)}) collective-permute-start(bf16[256,2048]{1,0:T(8,128)(2,1)} %add_convert_fusion.10), channel_id=1, source_target_pairs={{0,1},{1,0},{2,3},{3,2},{4,5},{5,4},{6,7},{7,6},{8,9},{9,8},{10,11... | collective-permute-start | bytes 3145736 | tf_op jit(solution)/shard_map/ppermute | solution.py:327
  594.9 26.1 %collective-permute-start.30 = (bf16[256,2048]{1,0:T(8,128)(2,1)S(1)}, bf16[256,2048]{1,0:T(8,128)(2,1)S(1)}, u32[]{:S(2)}, u32[]{:S(2)}) collective-permute-start(bf16[256,2048]{1,0:T(8,128)(2,1)S(1)} %get-tuple-element.52), channel_id=1, source_target_pairs={{0,1},{1,0},{2,3},{3,2},{4,5},{5,4},{6,7},{7,6},{8,9},{9,8},{10,11... | collective-permute-start | bytes 3145736 | tf_op jit(solution)/shard_map/ppermute | solution.py:327
  596.4 49.3 %collective-permute-start.32 = (bf16[256,2048]{1,0:T(8,128)(2,1)S(1)}, bf16[256,2048]{1,0:T(8,128)(2,1)S(1)}, u32[]{:S(2)}, u32[]{:S(2)}) collective-permute-start(bf16[256,2048]{1,0:T(8,128)(2,1)S(1)} %get-tuple-element.52), channel_id=1, source_target_pairs={{0,2},{1,3},{2,0},{3,1},{4,6},{5,7},{6,4},{7,5},{8,10},{9,11},{10,... | collective-permute-start | bytes 3145736 | tf_op jit(solution)/shard_map/ppermute | solution.py:327
  598.2 47.4 %collective-permute-start.31 = (bf16[256,2048]{1,0:T(8,128)(2,1)S(1)}, bf16[256,2048]{1,0:T(8,128)(2,1)S(1)}, u32[]{:S(2)}, u32[]{:S(2)}) collective-permute-start(bf16[256,2048]{1,0:T(8,128)(2,1)S(1)} %get-tuple-element.53), channel_id=1, source_target_pairs={{0,1},{1,0},{2,3},{3,2},{4,5},{5,4},{6,7},{7,6},{8,9},{9,8},{10,11... | collective-permute-start | bytes 3145736 | tf_op jit(solution)/shard_map/ppermute | solution.py:327
  598.7 46.2 %collective-permute-start.33 = (bf16[256,2048]{1,0:T(8,128)(2,1)S(1)}, bf16[256,2048]{1,0:T(8,128)(2,1)S(1)}, u32[]{:S(2)}, u32[]{:S(2)}) collective-permute-start(bf16[256,2048]{1,0:T(8,128)(2,1)S(1)} %get-tuple-element.53), channel_id=1, source_target_pairs={{0,2},{1,3},{2,0},{3,1},{4,6},{5,7},{6,4},{7,5},{8,10},{9,11},{10,... | collective-permute-start | bytes 3145736 | tf_op jit(solution)/shard_map/ppermute | solution.py:327
  621.0 42.8 %collective-permute-start.34 = (bf16[256,2048]{1,0:T(8,128)(2,1)S(1)}, bf16[256,2048]{1,0:T(8,128)(2,1)S(1)}, u32[]{:S(2)}, u32[]{:S(2)}) collective-permute-start(bf16[256,2048]{1,0:T(8,128)(2,1)S(1)} %collective-permute-done.30), channel_id=1, source_target_pairs={{0,2},{1,3},{2,0},{3,1},{4,6},{5,7},{6,4},{7,5},{8,10},{9,11},{10,... | collective-permute-start | bytes 3145736 | tf_op jit(solution)/shard_map/ppermute | solution.py:327
  644.9 19.0 %collective-permute-start.35 = (bf16[256,2048]{1,0:T(8,128)(2,1)S(1)}, bf16[256,2048]{1,0:T(8,128)(2,1)S(1)}, u32[]{:S(2)}, u32[]{:S(2)}) collective-permute-start(bf16[256,2048]{1,0:T(8,128)(2,1)S(1)} %collective-permute-done.33), channel_id=1, source_target_pairs={{0,1},{1,0},{2,3},{3,2},{4,5},{5,4},{6,7},{7,6},{8,9},{9,8},{10,11... | collective-permute-start | bytes 3145736 | tf_op jit(solution)/shard_map/ppermute | solution.py:327
  723.7 222.1 %reduce-scatter.12.cloned.1.call-start = ((), (), s32[]{:S(2)}) async-start(), calls=%async_computation.13 | async-start | bytes 9437184 | tf_op jit(solution)/shard_map/reduce_scatter | solution.py:508
  724.4 224.2 %reduce-scatter.10.cloned.1.call-start = ((), (), s32[]{:S(2)}) async-start(), calls=%async_computation.12 | async-start | bytes 9437184 | tf_op jit(solution)/shard_map/reduce_scatter | solution.py:508
  725.2 282.6 %reduce-scatter.6.cloned.1.call-start = ((), (), s32[]{:S(2)}) async-start(), calls=%async_computation.10 | async-start | bytes 7077888 | tf_op jit(solution)/shard_map/reduce_scatter | solution.py:508
  771.8 326.1 %reduce-scatter.14.cloned.1.call-start = ((), (), s32[]{:S(2)}) async-start(), calls=%async_computation.14 | async-start | bytes 9437184 | tf_op jit(solution)/shard_map/reduce_scatter | solution.py:508
  774.7 21.3 %collective-permute-start.46 = (bf16[256,2048]{1,0:T(8,128)(2,1)S(1)}, bf16[256,2048]{1,0:T(8,128)(2,1)S(1)}, u32[]{:S(2)}, u32[]{:S(2)}) collective-permute-start(bf16[256,2048]{1,0:T(8,128)(2,1)S(1)} %get-tuple-element.108), channel_id=1, source_target_pairs={{0,1},{1,0},{2,3},{3,2},{4,5},{5,4},{6,7},{7,6},{8,9},{9,8},{10,11... | collective-permute-start | bytes 3145736 | tf_op jit(solution)/shard_map/ppermute | solution.py:327
  775.4 23.9 %collective-permute-start.43 = (bf16[256,2048]{1,0:T(8,128)(2,1)S(1)}, bf16[256,2048]{1,0:T(8,128)(2,1)S(1)}, u32[]{:S(2)}, u32[]{:S(2)}) collective-permute-start(bf16[256,2048]{1,0:T(8,128)(2,1)S(1)} %get-tuple-element.109), channel_id=1, source_target_pairs={{0,2},{1,3},{2,0},{3,1},{4,6},{5,7},{6,4},{7,5},{8,10},{9,11},{10,... | collective-permute-start | bytes 3145736 | tf_op jit(solution)/shard_map/ppermute | solution.py:327
  786.8 57.8 %collective-permute-start.45 = (bf16[256,2048]{1,0:T(8,128)(2,1)S(1)}, bf16[256,2048]{1,0:T(8,128)(2,1)S(1)}, u32[]{:S(2)}, u32[]{:S(2)}) collective-permute-start(bf16[256,2048]{1,0:T(8,128)(2,1)S(1)} %slice.243), channel_id=1, source_target_pairs={{0,1},{1,0},{2,3},{3,2},{4,5},{5,4},{6,7},{7,6},{8,9},{9,8},{10,11... | collective-permute-start | bytes 3145736 | tf_op jit(solution)/shard_map/ppermute | solution.py:327
  788.4 57.9 %collective-permute-start.42 = (bf16[256,2048]{1,0:T(8,128)(2,1)S(1)}, bf16[256,2048]{1,0:T(8,128)(2,1)}, u32[]{:S(2)}, u32[]{:S(2)}) collective-permute-start(bf16[256,2048]{1,0:T(8,128)(2,1)S(1)} %get-tuple-element.107), channel_id=1, source_target_pairs={{0,2},{1,3},{2,0},{3,1},{4,6},{5,7},{6,4},{7,5},{8,10},{9,11},{10,... | collective-permute-start | bytes 3145736 | tf_op jit(solution)/shard_map/ppermute | solution.py:327
  790.1 51.7 %collective-permute-start.37 = (bf16[256,2048]{1,0:T(8,128)(2,1)S(1)}, bf16[256,2048]{1,0:T(8,128)(2,1)S(1)}, u32[]{:S(2)}, u32[]{:S(2)}) collective-permute-start(bf16[256,2048]{1,0:T(8,128)(2,1)S(1)} %get-tuple-element.100), channel_id=1, source_target_pairs={{0,2},{1,3},{2,0},{3,1},{4,6},{5,7},{6,4},{7,5},{8,10},{9,11},{10,... | collective-permute-start | bytes 3145736 | tf_op jit(solution)/shard_map/ppermute | solution.py:327
  797.7 66.6 %collective-permute-start.47 = (bf16[256,2048]{1,0:T(8,128)(2,1)S(1)}, bf16[256,2048]{1,0:T(8,128)(2,1)S(1)}, u32[]{:S(2)}, u32[]{:S(2)}) collective-permute-start(bf16[256,2048]{1,0:T(8,128)(2,1)S(1)} %add_convert_fusion), channel_id=1, source_target_pairs={{0,2},{1,3},{2,0},{3,1},{4,6},{5,7},{6,4},{7,5},{8,10},{9,11},{10,... | collective-permute-start | bytes 3145736 | tf_op jit(solution)/shard_map/ppermute | solution.py:327
  800.8 65.9 %collective-permute-start.44 = (bf16[256,2048]{1,0:T(8,128)(2,1)}, bf16[256,2048]{1,0:T(8,128)(2,1)}, u32[]{:S(2)}, u32[]{:S(2)}) collective-permute-start(bf16[256,2048]{1,0:T(8,128)(2,1)} %add_convert_fusion.2), channel_id=1, source_target_pairs={{0,1},{1,0},{2,3},{3,2},{4,5},{5,4},{6,7},{7,6},{8,9},{9,8},{10,11... | collective-permute-start | bytes 3145736 | tf_op jit(solution)/shard_map/ppermute | solution.py:327
  841.8 45.0 %collective-permute-start.36 = (bf16[256,2048]{1,0:T(8,128)(2,1)}, bf16[256,2048]{1,0:T(8,128)(2,1)}, u32[]{:S(2)}, u32[]{:S(2)}) collective-permute-start(bf16[256,2048]{1,0:T(8,128)(2,1)} %get-tuple-element.97), channel_id=1, source_target_pairs={{0,2},{1,3},{2,0},{3,1},{4,6},{5,7},{6,4},{7,5},{8,10},{9,11},{10,... | collective-permute-start | bytes 3145736 | tf_op jit(solution)/shard_map/ppermute | solution.py:327
  844.6 42.2 %collective-permute-start.40 = (bf16[256,2048]{1,0:T(8,128)(2,1)}, bf16[256,2048]{1,0:T(8,128)(2,1)}, u32[]{:S(2)}, u32[]{:S(2)}) collective-permute-start(bf16[256,2048]{1,0:T(8,128)(2,1)} %get-tuple-element.98), channel_id=1, source_target_pairs={{0,1},{1,0},{2,3},{3,2},{4,5},{5,4},{6,7},{7,6},{8,9},{9,8},{10,11... | collective-permute-start | bytes 3145736 | tf_op jit(solution)/shard_map/ppermute | solution.py:327
  846.3 40.6 %collective-permute-start.38 = (bf16[256,2048]{1,0:T(8,128)(2,1)}, bf16[256,2048]{1,0:T(8,128)(2,1)}, u32[]{:S(2)}, u32[]{:S(2)}) collective-permute-start(bf16[256,2048]{1,0:T(8,128)(2,1)} %add_convert_fusion.6), channel_id=1, source_target_pairs={{0,1},{1,0},{2,3},{3,2},{4,5},{5,4},{6,7},{7,6},{8,9},{9,8},{10,11... | collective-permute-start | bytes 3145736 | tf_op jit(solution)/shard_map/ppermute | solution.py:327
  865.3 74.5 %collective-permute-start.39 = (bf16[256,2048]{1,0:T(8,128)(2,1)}, bf16[256,2048]{1,0:T(8,128)(2,1)}, u32[]{:S(2)}, u32[]{:S(2)}) collective-permute-start(bf16[256,2048]{1,0:T(8,128)(2,1)} %get-tuple-element.99), channel_id=1, source_target_pairs={{0,1},{1,0},{2,3},{3,2},{4,5},{5,4},{6,7},{7,6},{8,9},{9,8},{10,11... | collective-permute-start | bytes 3145736 | tf_op jit(solution)/shard_map/ppermute | solution.py:327
  870.9 20.7 %collective-permute-start.48 = (f32[2,1024]{1,0:T(2,128)S(1)}, f32[2,1024]{1,0:T(2,128)S(1)}, u32[]{:S(2)}, u32[]{:S(2)}) collective-permute-start(f32[2,1024]{1,0:T(2,128)S(1)} %bitcast.58), channel_id=1, source_target_pairs={{0,16},{1,17},{2,18},{3,19},{4,20},{5,21},{6,22},{7,23},{8,24},{9,... | collective-permute-start | bytes 24584 | tf_op jit(solution)/shard_map/ppermute | solution.py:381
  891.7 9.0 collective-permute-start.49
  900.7 10.2 collective-permute-start.50
  910.1 29.7 %collective-permute-start.41 = (bf16[256,2048]{1,0:T(8,128)(2,1)}, bf16[256,2048]{1,0:T(8,128)(2,1)}, u32[]{:S(2)}, u32[]{:S(2)}) collective-permute-start(bf16[256,2048]{1,0:T(8,128)(2,1)} %get-tuple-element.96), channel_id=1, source_target_pairs={{0,2},{1,3},{2,0},{3,1},{4,6},{5,7},{6,4},{7,5},{8,10},{9,11},{10,... | collective-permute-start | bytes 3145736 | tf_op jit(solution)/shard_map/ppermute | solution.py:327
  910.9 24.6 %collective-permute-start.51 = (f32[2,128]{1,0:T(2,128)S(1)}, f32[2,128]{1,0:T(2,128)S(1)}, u32[]{:S(2)}, u32[]{:S(2)}) collective-permute-start(f32[2,128]{1,0:T(2,128)S(1)} %fusion.40), channel_id=1, source_target_pairs={{0,2},{1,3},{2,0},{3,1},{4,6},{5,7},{6,4},{7,5},{8,10},{9,11},{10,... | collective-permute-start | bytes 3080 | tf_op jit(solution)/shard_map/ppermute | solution.py:381
  935.6 3.6 collective-permute-start.52
  (48 other events, 1044.2 us)
Sparse Core Ops, SparseCore 0:
  10.2 67.4 all-gather.5
  79.3 27.7 all-gather.7
  108.7 81.4 all-gather.9
  191.6 80.5 all-gather.11
  273.6 80.5 all-gather.13
  723.8 32.3 reduce-scatter.7
  758.5 88.1 reduce-scatter.11
  849.0 88.2 reduce-scatter.9
  939.6 68.1 reduce-scatter.5
  1009.9 87.9 reduce-scatter.13

commit v3 on v2

--- a/solution.py
+++ b/solution.py
@@ -47,14 +47,14 @@
 
 
 def turn(field, cosine, sine):
-    lane = lax.broadcasted_iota(jnp.int32, field.shape, 1)
-    swapped = jnp.where(lane % HD < HD // 2, pltpu.roll(field, LANES - HD // 2, 1), pltpu.roll(field, HD // 2, 1))
+    lane = lax.broadcasted_iota(jnp.int32, (1, LANES), 1)
+    swapped = jnp.where((lane & (HD - 1)) < HD // 2, pltpu.roll(field, LANES - HD // 2, 1), pltpu.roll(field, HD // 2, 1))
     return field * cosine + swapped * sine
 
 
-def head_lanes(rows, head):
-    lane = lax.broadcasted_iota(jnp.int32, (rows, LANES), 1)
-    return (lane // HD) == head
+def head_lanes(head):
+    lane = lax.broadcasted_iota(jnp.int32, (1, LANES), 1)
+    return lane >= HD if head else lane < HD
 
 
 def only(values, keep):
@@ -67,12 +67,12 @@
 
 
 def diag_mask(block, live):
-    row = lax.broadcasted_iota(jnp.int32, (QB, QB), 0)
-    col = lax.broadcasted_iota(jnp.int32, (QB, QB), 1)
-    return (col <= row) & (col + block * QB < live)
-
-
-def attend_kernel(own, info, q_ref, k_ref, v_ref, cos_ref, sin_ref, qo, ko, vo, ao, qs, ks, vs):
+    key = lax.broadcasted_iota(jnp.int32, (QB, QB), 0)
+    query = lax.broadcasted_iota(jnp.int32, (QB, QB), 1)
+    return (key <= query) & (key + block * QB < live)
+
+
+def attend_kernel(own, info, q_ref, k_ref, v_ref, cos_ref, sin_ref, qo, ko, vo, ao, lo, qs, ks, vt):
     length = q_ref.shape[0]
     live, flip = info[0], info[1]
     for b in range(length // QB):
@@ -81,13 +81,13 @@
         cosine, sine = cos_ref[here, :], sin_ref[here, :]
         query = (turn(q_ref[rows, :], cosine, sine) * HD ** (-0.5)).astype(BF16)
         key = turn(k_ref[rows, :], cosine, sine).astype(BF16)
-        value = v_ref[rows, :].astype(BF16)
+        value = v_ref[rows, :]
         qo[rows, :] = query
         ko[rows, :] = key
-        vo[rows, :] = value
+        vo[rows, :] = value.astype(BF16)
         qs[here, :] = query
         ks[here, :] = key
-        vs[here, :] = value
+        vt[:, b * QB : (b + 1) * QB] = value.T.astype(BF16)
     for b in range(length // QB):
         rows = pl.ds(place_of(b, own, flip), QB)
 
@@ -96,26 +96,29 @@
             allowed = diag_mask(b, live)
             outs = []
             for head in range(2):
-                query = only(qs[pl.ds(b * QB, QB), :], head_lanes(QB, head))
-                diag = matmul_nt(query, ks[pl.ds(b * QB, QB), :])
+                lanes = slice(head * HD, (head + 1) * HD)
+                query = only(qs[pl.ds(b * QB, QB), :], head_lanes(head))
+                diag = matmul_nt(ks[pl.ds(b * QB, QB), :], query)
                 diag = jnp.where(allowed, diag, NEGATIVE)
-                top = jnp.max(diag, axis=1, keepdims=True)
+                top = jnp.max(diag, axis=0, keepdims=True)
                 if b:
-                    past = matmul_nt(query, ks[pl.ds(0, b * QB), :])
-                    top = jnp.maximum(top, jnp.max(past, axis=1, keepdims=True))
+                    past = matmul_nt(ks[pl.ds(0, b * QB), :], query)
+                    top = jnp.maximum(top, jnp.max(past, axis=0, keepdims=True))
                 diag = jnp.exp(diag - top)
-                total = jnp.sum(diag, axis=1, keepdims=True)
-                mixed = matmul(diag.astype(BF16), vs[pl.ds(b * QB, QB), :])
+                total = jnp.sum(diag, axis=0, keepdims=True)
+                mixed = matmul(vt[lanes, b * QB : (b + 1) * QB], diag.astype(BF16))
                 if b:
                     past = jnp.exp(past - top)
-                    total = total + jnp.sum(past, axis=1, keepdims=True)
-                    mixed = mixed + matmul(past.astype(BF16), vs[pl.ds(0, b * QB), :])
+                    total = total + jnp.sum(past, axis=0, keepdims=True)
+                    mixed = mixed + matmul(vt[lanes, : b * QB], past.astype(BF16))
                 outs.append(mixed / total)
-            ao[rows, :] = jnp.where(head_lanes(QB, 0), outs[0], outs[1]).astype(BF16)
+                lo[0, head : head + 1, b * QB : (b + 1) * QB] = top + jnp.log(total)
+            ao[rows, :] = jnp.concatenate(outs, axis=0).T.astype(BF16)
 
         @pl.when(b * QB >= live)
         def _():
             ao[rows, :] = jnp.zeros((QB, LANES), BF16)
+            lo[0, 0:2, b * QB : (b + 1) * QB] = jnp.zeros((2, QB), F32)
 
 
 def attend(qkv, slot, info, cosine, sine, own, length):
@@ -130,13 +133,13 @@
     out = pl.BlockSpec((length, LANES), lambda i, s: (0, i))
     return pl.pallas_call(
         functools.partial(attend_kernel, own),
-        out_shape=[wide] * 4,
+        out_shape=[wide] * 4 + [jax.ShapeDtypeStruct((pairs, 8, length), F32)],
         grid_spec=pltpu.PrefetchScalarGridSpec(
             num_scalar_prefetch=1,
             grid=(pairs,),
             in_specs=[column(0), column(1), column(2), whole, whole],
-            out_specs=[out] * 4,
-            scratch_shapes=[pltpu.VMEM((length, LANES), BF16)] * 3,
+            out_specs=[out] * 4 + [pl.BlockSpec((1, 8, length), lambda i, s: (i, 0, 0))],
+            scratch_shapes=[pltpu.VMEM((length, LANES), BF16)] * 2 + [pltpu.VMEM((LANES, length), BF16)],
         ),
         compiler_params=pltpu.CompilerParams(dimension_semantics=("arbitrary",)),
         cost_estimate=pl.CostEstimate(
@@ -146,18 +149,33 @@
     )(info, qkv, qkv, qkv, cosine, sine)
 
 
-def attend_back_kernel(own, info, q_ref, k_ref, v_ref, g_ref, cos_ref, sin_ref, out, qs, ks, vs, gs, dq, dk, dv):
+def attend_back_kernel(
+    own, info, q_ref, k_ref, v_ref, a_ref, l_ref, g_ref, cos_ref, sin_ref, out, qs, ks, vs, gs, kt, centre, dq, dk, dv
+):
     length = q_ref.shape[0]
     width = out.shape[1] // 3
     live, flip = info[0], info[1]
     pair = pl.program_id(0)
+    row = lax.broadcasted_iota(jnp.int32, (8, LANES), 0)
+    lane = lax.broadcasted_iota(jnp.int32, (8, LANES), 1)
+    sum_head = (lane // HD == row).astype(F32)
     for b in range(length // QB):
         rows = pl.ds(place_of(b, own, flip), QB)
         here = pl.ds(b * QB, QB)
+        key = k_ref[rows, :]
+        grad = g_ref[rows, :]
         qs[here, :] = q_ref[rows, :]
-        ks[here, :] = k_ref[rows, :]
+        ks[here, :] = key
         vs[here, :] = v_ref[rows, :]
-        gs[here, :] = g_ref[rows, :]
+        gs[here, :] = grad
+        kt[:, b * QB : (b + 1) * QB] = key.astype(F32).T.astype(BF16)
+        centre[:, b * QB : (b + 1) * QB] = lax.dot_general(
+            sum_head,
+            grad.astype(F32) * a_ref[rows, :].astype(F32),
+            (((1,), (1,)), ((), ())),
+            precision=lax.Precision.HIGHEST,
+            preferred_element_type=F32,
+        )
     dq[...] = jnp.zeros_like(dq)
     dk[...] = jnp.zeros_like(dk)
     dv[...] = jnp.zeros_like(dv)
@@ -166,40 +184,40 @@
         @pl.when(b * QB < live)
         def _():
             here = pl.ds(b * QB, QB)
+            columns = slice(b * QB, (b + 1) * QB)
             allowed = diag_mask(b, live)
+            diag_p, diag_ds, past_p, past_ds, queries, grads, outs = [], [], [], [], [], [], []
             for head in range(2):
-                keep = head_lanes(QB, head)
+                keep = head_lanes(head)
+                lanes = slice(head * HD, (head + 1) * HD)
                 query = only(qs[here, :], keep)
                 grad = only(gs[here, :], keep)
-                diag = jnp.where(allowed, matmul_nt(query, ks[here, :]), NEGATIVE)
-                top = jnp.max(diag, axis=1, keepdims=True)
+                log_total = l_ref[0, head : head + 1, columns]
+                middle = centre[head : head + 1, columns]
+                queries.append(query)
+                grads.append(grad)
+                prob = jnp.exp(jnp.where(allowed, matmul_nt(ks[here, :], query), NEGATIVE) - log_total)
+                slope = (prob * (matmul_nt(vs[here, :], grad) - middle)).astype(BF16)
+                diag_p.append(prob.astype(BF16))
+                diag_ds.append(slope)
+                turned = matmul(kt[lanes, columns], slope)
                 if b:
                     before = pl.ds(0, b * QB)
-                    past = matmul_nt(query, ks[before, :])
-                    top = jnp.maximum(top, jnp.max(past, axis=1, keepdims=True))
-                diag = jnp.exp(diag - top)
-                total = jnp.sum(diag, axis=1, keepdims=True)
-                if b:
-                    past = jnp.exp(past - top)
-                    total = total + jnp.sum(past, axis=1, keepdims=True)
-                scale = 1.0 / total
-                diag = diag * scale
-                diag_dp = matmul_nt(grad, vs[here, :])
-                centre = jnp.sum(diag * diag_dp, axis=1, keepdims=True)
-                if b:
-                    past = past * scale
-                    past_dp = matmul_nt(grad, vs[before, :])
-                    centre = centre + jnp.sum(past * past_dp, axis=1, keepdims=True)
-                diag_ds = (diag * (diag_dp - centre)).astype(BF16)
-                dq_b = matmul(diag_ds, only(ks[here, :], keep))
-                dk[here, :] += matmul_tn(diag_ds, query)
-                dv[here, :] += matmul_tn(diag.astype(BF16), grad)
-                if b:
-                    past_ds = (past * (past_dp - centre)).astype(BF16)
-                    dq_b = dq_b + matmul(past_ds, only(ks[before, :], head_lanes(b * QB, head)))
-                    dk[before, :] += matmul_tn(past_ds, query)
-                    dv[before, :] += matmul_tn(past.astype(BF16), grad)
-                dq[here, :] += dq_b
+                    prob = jnp.exp(matmul_nt(ks[before, :], query) - log_total)
+                    slope = (prob * (matmul_nt(vs[before, :], grad) - middle)).astype(BF16)
+                    past_p.append(prob.astype(BF16))
+                    past_ds.append(slope)
+                    turned = turned + matmul(kt[lanes, : b * QB], slope)
+                outs.append(turned)
+            queries = jnp.concatenate(queries, axis=0)
+            grads = jnp.concatenate(grads, axis=0)
+            dk[here, :] += matmul(jnp.concatenate(diag_ds, axis=1), queries)
+            dv[here, :] += matmul(jnp.concatenate(diag_p, axis=1), grads)
+            if b:
+                before = pl.ds(0, b * QB)
+                dk[before, :] += matmul(jnp.concatenate(past_ds, axis=1), queries)
+                dv[before, :] += matmul(jnp.concatenate(past_p, axis=1), grads)
+            dq[here, :] = jnp.concatenate(outs, axis=0).T
 
     for b in range(length // QB):
         rows = pl.ds(place_of(b, own, flip), QB)
@@ -214,7 +232,7 @@
         out[rows, columns(2)] = dv[here, :].astype(BF16)
 
 
-def attend_back(query, keys, values, grad, slot, info, cosine, sine, own, length):
+def attend_back(query, keys, values, mixed, log_total, grad, slot, info, cosine, sine, own, length):
     width = query.shape[1]
     pairs = width // LANES
     block = pl.BlockSpec((length, LANES), lambda i, s: (0, i))
@@ -226,16 +244,19 @@
         grid_spec=pltpu.PrefetchScalarGridSpec(
             num_scalar_prefetch=1,
             grid=(pairs,),
-            in_specs=[block, block, block, block_grad, whole, whole],
+            in_specs=[block] * 4
+            + [pl.BlockSpec((1, 8, length), lambda i, s: (i, 0, 0)), block_grad, whole, whole],
             out_specs=pl.BlockSpec((length, 3 * width), lambda i, s: (0, 0)),
-            scratch_shapes=[pltpu.VMEM((length, LANES), BF16)] * 4 + [pltpu.VMEM((length, LANES), F32)] * 3,
+            scratch_shapes=[pltpu.VMEM((length, LANES), BF16)] * 4
+            + [pltpu.VMEM((LANES, length), BF16), pltpu.VMEM((8, length), F32)]
+            + [pltpu.VMEM((length, LANES), F32)] * 3,
         ),
         compiler_params=pltpu.CompilerParams(dimension_semantics=("arbitrary",)),
         cost_estimate=pl.CostEstimate(
             flops=20 * length * length * width, bytes_accessed=20 * length * width, transcendentals=0
         ),
         name="attend_back",
-    )(info, query, keys, values, grad, cosine, sine)
+    )(info, query, keys, values, mixed, log_total, grad, cosine, sine)
 
 
 def gate_up_kernel(h_ref, g_ref, u_ref, hid_ref, gate_slope, up_slope):
@@ -424,7 +445,6 @@
     normed_one = [v * s for v, s in zip(x, scale_one)]
     h1 = gather_tp([(n * gain_attn).astype(BF16) for n in normed_one], size)
     grad_rows = [m * g.astype(F32) for m, g in zip(valid, split_halves(out_grad))]
-    dm = gather_tp([after(g.astype(BF16), h1) for g in grad_rows], size)
 
     qkv = matmul(h1, qkv_full)
     saved = {}
@@ -443,15 +463,18 @@
     normed_two = [v * s for v, s in zip(middle, scale_two)]
     h2 = gather_tp([(n * gain_mlp).astype(BF16) for n in normed_two], size)
 
+    dm_own = after(jnp.concatenate([g.astype(BF16) for g in grad_rows], axis=0), h2)
+    dm = jnp.concatenate([dm_own] + [hop(dm_own, r, size) for r in range(1, size)], axis=0)
+
     hid, gate_slope, up_slope = gate_up(h2, gate_full, up_full)
     down_term = matmul_tn(dm, hid).astype(BF16)
     grad_gate, grad_up = hidden_back(dm, down_full, after(gate_slope, down_term), up_slope)
     half_group = group // 2
     two = {}
     two[1] = two_nt(grad_gate, grad_up, gate_full, up_full, half_group, half_group)
-    two[0] = two_nt(after(grad_gate, two[1]), grad_up, gate_full, up_full, 0, half_group)
-    gate_term = matmul_tn(h2, after(grad_gate, two[0])).astype(BF16)
-    up_term = matmul_tn(h2, after(grad_up, gate_term)).astype(BF16)
+    gate_term = matmul_tn(h2, after(grad_gate, two[1])).astype(BF16)
+    two[0] = two_nt(after(grad_gate, gate_term), grad_up, gate_full, up_full, 0, half_group)
+    up_term = matmul_tn(h2, after(grad_up, two[0])).astype(BF16)
     mlp = matmul_nt(after(hid, up_term), down_full).astype(BF16)
 
     def two_piece(r):
@@ -477,16 +500,17 @@
     partial_one = {}
     last = None
     for s in reversed(range(count)):
-        query, keys, values, _ = saved[s]
+        query, keys, values, mixed_s, log_total = saved[s]
         if last is not None:
             query = after(query, last)
-        grad_qkv[s] = attend_back(query, keys, values, grad_mixed, s, infos[s], cosine, sine, own, length)
+        grad_qkv[s] = attend_back(query, keys, values, mixed_s, log_total, grad_mixed, s, infos[s], cosine, sine, own, length)
         if s:
             last = partial_one[s] = matmul_nt(grad_qkv[s], qkv_full).astype(BF16)
         if s == count - 1:
             mixed = after(jnp.concatenate([saved[i][3] for i in range(count)], axis=0), last)
             last = out_term = matmul_tn(grad_attn, mixed).astype(BF16)
-    qkv_term = matmul_tn(h1, jnp.concatenate([grad_qkv[s] for s in range(count)], axis=0)).astype(BF16)
+    grad_all = jnp.concatenate([grad_qkv[s] for s in range(count)], axis=0)
+    qkv_term = matmul_tn(h1, grad_all).astype(BF16)
     partial_one[0] = matmul_nt(after(grad_qkv[0], qkv_term), qkv_full).astype(BF16)
 
     def one_piece(r):
@@ -512,7 +536,7 @@
     up_grad = back_fsdp(up_term)
     out_proj_grad = back_fsdp(out_term)
     qkv_grad = back_fsdp(qkv_term)
-    gains = scatter_vectors(jnp.stack([gain_attn_term, gain_mlp_term]))
+    gains = scatter_vectors(after(jnp.stack([gain_attn_term, gain_mlp_term]), down_grad, gate_grad, up_grad))
     return (
         output,
         input_grad,

time: 1110 us -> 960 us (0.86)
  waiting for transfers between devices: 497 us -> 376 us
  starting transfers between devices: 68.5 us -> 50.5 us
    reduce_scatter x5, waiting for transfers between devices: 144 us -> 0.03 us  [back_fsdp(): lax.psum_scatter(term, 'fsdp', scatter_dimension=0, tiled=True).astype(F32)]
    ppermute x48 -> x45, waiting for transfers between devices: 328 us -> 372 us  [hop(): return lax.ppermute(value, 'tp', [(i, i ^ bit) for i in range(size)])]
    ppermute x5, waiting for transfers between devices: 20.5 us -> 0.33 us  [scatter_vectors(): lax.ppermute(sent, axes, [(i, i ^ bit) for i in range(devices)])]
    ppermute x5, starting transfers between devices: 19.4 us -> 1.92 us  [scatter_vectors(): lax.ppermute(sent, axes, [(i, i ^ bit) for i in range(devices)])]
    pallas_call x2, Pallas kernels: 64.9 us -> 51.8 us  [attend_back(): pl.pallas_call(functools.partial(attend_back_kernel, own), out_shape=jax....]
    ppermute x48 -> x45, starting transfers between devices: 48.8 us -> 48.2 us  [hop(): return lax.ppermute(value, 'tp', [(i, i ^ bit) for i in range(size)])]
    unnamed x126 -> x129, local copies, waits for them, and re-layouts: 23.8 us -> 23.5 us
  transfers between devices with their start and end apart: 63 -> 60, of which waited for: 29 -> 27; matrix products, arithmetic and copies ran while one was open for 22% -> 23% of each run, Pallas kernels for 10% -> 15%
where the time goes in v3:
time: 960 us; the launch traced here: 955 us
  waiting for transfers between devices  376 us (39%)
  Pallas kernels  232 us (24%)
  matrix products  166 us (17%)
  other arithmetic  70.9 us (7%)
  starting transfers between devices  50.5 us (5%)
  local copies, waits for them, and re-layouts  44.3 us (5%)
  between operations  15.5 us (2%)
    ppermute x45, waiting for transfers between devices, hop(): return lax.ppermute(value, 'tp', [(i, i ^ bit) for i in range(size)])  372 us
    dot_general x5, matrix products, matmul_tn(): lax.dot_general(left, right, (((0,), (0,)), ((), ())), preferred_element_...  93.3 us
    pallas_call x2, Pallas kernels, two_nt(): pl.pallas_call(two_nt_kernel, out_shape=jax.ShapeDtypeStruct((rows, width...  55.6 us
    pallas_call x2, Pallas kernels, attend_back(): pl.pallas_call(functools.partial(attend_back_kernel, own), out_shape=jax....  51.8 us
    pallas_call x1, Pallas kernels, gate_up(): pl.pallas_call(gate_up_kernel, out_shape=[jax.ShapeDtypeStruct((rows, wid...  48.5 us
    ppermute x45, starting transfers between devices, hop(): return lax.ppermute(value, 'tp', [(i, i ^ bit) for i in range(size)])  48.2 us
    dot_general x5, matrix products, matmul_nt(): lax.dot_general(left, right, (((1,), (1,)), ((), ())), preferred_element_...  47.5 us
    pallas_call x2, Pallas kernels, attend(): pl.pallas_call(functools.partial(attend_kernel, own), out_shape=[wide] *...  41.7 us
  transfers between devices with their start and end apart: 60, of which 27 were waited for; matrix products, arithmetic and copies ran while one was open for 23% of the time, Pallas kernels for 15%

profile of v3, /device:TPU:0, one launch (start us, length us, event | category | flops | bytes accessed | tf_op | source)
XLA Modules:
  0.0 954.7 jit_solution(7998604787985665233)
XLA Ops:
  13.7 3.0 collective-permute-start
  24.8 16.1 %collective-permute-done = bf16[256,2048]{1,0:T(8,128)(2,1)S(1)} collective-permute-done((bf16[256,2048]{1,0:T(8,128)(2,1)}, bf16[256,2048]{1,0:T(8,128)(2,1)S(1)}, u32[]{:S(2)}, u32[]{:S(2)}) %collective-permute-start) | collective-permute-done | bytes 1048608 | tf_op jit(solution)/shard_map/ppermute | solution.py:348
  47.5 16.0 %collective-permute-done.1 = bf16[256,2048]{1,0:T(8,128)(2,1)} collective-permute-done((bf16[256,2048]{1,0:T(8,128)(2,1)}, bf16[256,2048]{1,0:T(8,128)(2,1)}, u32[]{:S(2)}, u32[]{:S(2)}) %collective-permute-start.1) | collective-permute-done | bytes 1048608 | tf_op jit(solution)/shard_map/ppermute | solution.py:348
  67.1 2.4 constant_dynamic-update-slice_fusion.3
  71.8 16.3 %collective-permute-done.4 = bf16[256,2048]{1,0:T(8,128)(2,1)S(1)} collective-permute-done((bf16[256,2048]{1,0:T(8,128)(2,1)S(1)}, bf16[256,2048]{1,0:T(8,128)(2,1)S(1)}, u32[]{:S(2)}, u32[]{:S(2)}) %collective-permute-start.4) | collective-permute-done | bytes 1048608 | tf_op jit(solution)/shard_map/ppermute | solution.py:348
  90.2 19.5 %fusion.53.q_ref.k_ref.v_ref = f32[2048,1536]{1,0:T(8,128)} fusion(bf16[2048,2048]{1,0:T(8,128)(2,1)} %constant_dynamic-update-slice_fusion, bf16[2048,1536]{1,0:T(8,128)(2,1)} %all-gather.6.cloned.1.call-done), kind=kOutput, calls=%fused_computation.169 | convolution fusion | flops 12884901888 | bytes 27262976 | tf_op jit(solution)/shard_map/dot_general | solution.py:22
  109.7 23.3 %attend.3 = (bf16[1024,512]{1,0:T(8,128)(2,1)}, bf16[1024,512]{1,0:T(8,128)(2,1)}, bf16[1024,512]{1,0:T(8,128)(2,1)}, bf16[1024,512]{1,0:T(8,128)(2,1)}, f32[4,8,1024]{2,1,0:T(8,128)}) custom-call(s32[2]{0:T(128)} %get-tuple-element.143.info, f32[2048,1536]{1,0:T(8,128)} %fusion.53.q_ref.k_ref.v_ref, f32[2048,1536]{1,0:T(8,128)} %fusion.53.q_ref.k_ref.v_ref, ...), custom_call_target="tpu_custom_call" | custom-call | flops 4294967296 | bytes 10485760 | tf_op jit(solution)/shard_map/attend/pallas_call | solution.py:134
  133.1 4.3 convolution_convert_fusion.7
  140.7 18.4 %attend.2 = (bf16[1024,512]{1,0:T(8,128)(2,1)}, bf16[1024,512]{1,0:T(8,128)(2,1)}, bf16[1024,512]{1,0:T(8,128)(2,1)}, bf16[1024,512]{1,0:T(8,128)(2,1)}, f32[4,8,1024]{2,1,0:T(8,128)}) custom-call(s32[2]{0:T(128)} %get-tuple-element.142.info, f32[2048,1536]{1,0:T(8,128)} %fusion.53.q_ref.k_ref.v_ref, f32[2048,1536]{1,0:T(8,128)} %fusion.53.q_ref.k_ref.v_ref, ...), custom_call_target="tpu_custom_call" | custom-call | flops 4294967296 | bytes 10485760 | tf_op jit(solution)/shard_map/attend/pallas_call | solution.py:134
  159.1 4.3 convolution_convert_fusion.8
  166.3 7.2 collective-permute-start.6
  173.5 2.6 add_convert_fusion.12
  178.5 8.3 collective-permute-done.9
  186.8 11.1 %collective-permute-done.6 = bf16[256,2048]{1,0:T(8,128)(2,1)} collective-permute-done((bf16[256,2048]{1,0:T(8,128)(2,1)}, bf16[256,2048]{1,0:T(8,128)(2,1)}, u32[]{:S(2)}, u32[]{:S(2)}) %collective-permute-start.6) | collective-permute-done | bytes 1048608 | tf_op jit(solution)/shard_map/ppermute | solution.py:348
  197.9 20.9 %collective-permute-done.11 = bf16[256,2048]{1,0:T(8,128)(2,1)} collective-permute-done((bf16[256,2048]{1,0:T(8,128)(2,1)}, bf16[256,2048]{1,0:T(8,128)(2,1)}, u32[]{:S(2)}, u32[]{:S(2)}) %collective-permute-start.11) | collective-permute-done | bytes 1048608 | tf_op jit(solution)/shard_map/ppermute | solution.py:348
  218.8 4.1 multiply_reduce_fusion.5
  230.0 20.2 %collective-permute-done.12 = bf16[256,2048]{1,0:T(8,128)(2,1)S(1)} collective-permute-done((bf16[256,2048]{1,0:T(8,128)(2,1)S(1)}, bf16[256,2048]{1,0:T(8,128)(2,1)S(1)}, u32[]{:S(2)}, u32[]{:S(2)}) %collective-permute-start.12) | collective-permute-done | bytes 1048608 | tf_op jit(solution)/shard_map/ppermute | solution.py:348
  252.9 19.8 %collective-permute-done.13 = bf16[256,2048]{1,0:T(8,128)(2,1)S(1)} collective-permute-done((bf16[256,2048]{1,0:T(8,128)(2,1)S(1)}, bf16[256,2048]{1,0:T(8,128)(2,1)S(1)}, u32[]{:S(2)}, u32[]{:S(2)}) %collective-permute-start.13) | collective-permute-done | bytes 1048608 | tf_op jit(solution)/shard_map/ppermute | solution.py:348
  273.9 19.9 %collective-permute-done.16 = bf16[256,2048]{1,0:T(8,128)(2,1)S(1)} collective-permute-done((bf16[256,2048]{1,0:T(8,128)(2,1)S(1)}, bf16[256,2048]{1,0:T(8,128)(2,1)S(1)}, u32[]{:S(2)}, u32[]{:S(2)}) %collective-permute-start.16) | collective-permute-done | bytes 1048608 | tf_op jit(solution)/shard_map/ppermute | solution.py:348
  297.5 2.4 collective-permute-start.20
  300.0 48.5 %gate_up.1 = (bf16[2048,2048]{1,0:T(8,128)(2,1)}, bf16[2048,2048]{1,0:T(8,128)(2,1)}, bf16[2048,2048]{1,0:T(8,128)(2,1)}) custom-call(bf16[2048,2048]{1,0:T(8,128)(2,1)} %copy-done.24, bf16[2048,2048]{1,0:T(8,128)(2,1)} %all-gather.10.cloned.1.call-done.g_ref.wa_ref, bf16[2048,2048]{1,0:T(8,128)(2,1)} %all-gather.12.cloned.1.call-done.u_ref.wb_ref), custom_call_target="tpu_custom_call" | custom-call | flops 34359738368 | bytes 50331648 | tf_op jit(solution)/shard_map/gate_up/pallas_call | solution.py:282
  350.5 37.1 %collective-permute-done.19 = bf16[512,2048]{1,0:T(8,128)(2,1)} collective-permute-done((bf16[512,2048]{1,0:T(8,128)(2,1)S(1)}, bf16[512,2048]{1,0:T(8,128)(2,1)}, u32[]{:S(2)}, u32[]{:S(2)}) %collective-permute-start.19) | collective-permute-done | bytes 2097184 | tf_op jit(solution)/shard_map/ppermute | solution.py:348
  391.1 3.4 copy-done.19
  394.5 20.7 %convolution_convert_fusion.3 = bf16[2048,2048]{1,0:T(8,128)(2,1)} fusion(bf16[2048,2048]{1,0:T(8,128)(2,1)S(1)} %constant_dynamic-update-slice_fusion.16.g_ref, bf16[2048,2048]{1,0:T(8,128)(2,1)S(1)} %bitcast.70), kind=kOutput, calls=%fused_computation.3 | convolution fusion | flops 17184063488 | bytes 25165824 | tf_op jit(solution)/shard_map/dot_general | solution.py:30
  415.1 34.1 %hidden_back.1 = (bf16[2048,2048]{1,0:T(8,128)(2,1)}, bf16[2048,2048]{1,0:T(8,128)(2,1)}) custom-call(bf16[2048,2048]{1,0:T(8,128)(2,1)} %copy-done.19, bf16[2048,2048]{1,0:T(8,128)(2,1)} %all-gather.14.cloned.1.call-done.w_ref, bf16[2048,2048]{1,0:T(8,128)(2,1)} %get-tuple-element.45.gate_slope, bf16[2048,2048]{1,0:T(8,128)(2,1)} %get-tuple-element.46.up_slope), custom_call_target="tpu_custom_call" | custom-call | flops 17179869184 | bytes 50331648 | tf_op jit(solution)/shard_map/hidden_back/pallas_call | solution.py:306
  449.2 27.7 %two_nt.2 = bf16[1024,2048]{1,0:T(8,128)(2,1)} custom-call(bf16[2048,2048]{1,0:T(8,128)(2,1)} %get-tuple-element.50.a_ref, bf16[2048,2048]{1,0:T(8,128)(2,1)} %get-tuple-element.51.b_ref, bf16[2048,2048]{1,0:T(8,128)(2,1)} %all-gather.10.cloned.1.call-done.g_ref.wa_ref, bf16[2048,2048]{1,0:T(8,128)(2,1)} %all-gather.12.cloned.1.call-done.u_ref.wb_ref), custom_call_target="tpu_custom_call" | custom-call | flops 17179869184 | bytes 29360128 | tf_op jit(solution)/shard_map/two_nt/pallas_call | solution.py:334
  476.9 23.8 %convolution_convert_fusion.2 = bf16[2048,2048]{1,0:T(8,128)(2,1)} fusion(bf16[2048,2048]{1,0:T(8,128)(2,1)} %copy-done.24, bf16[2048,2048]{1,0:T(8,128)(2,1)} %get-tuple-element.50.a_ref), kind=kOutput, calls=%fused_computation.2 | convolution fusion | flops 17184063488 | bytes 25165824 | tf_op jit(solution)/shard_map/dot_general | solution.py:30
  500.7 27.9 %two_nt.3 = bf16[1024,2048]{1,0:T(8,128)(2,1)} custom-call(bf16[2048,2048]{1,0:T(8,128)(2,1)} %get-tuple-element.50.a_ref, bf16[2048,2048]{1,0:T(8,128)(2,1)} %get-tuple-element.51.b_ref, bf16[2048,2048]{1,0:T(8,128)(2,1)} %all-gather.10.cloned.1.call-done.g_ref.wa_ref, bf16[2048,2048]{1,0:T(8,128)(2,1)} %all-gather.12.cloned.1.call-done.u_ref.wb_ref), custom_call_target="tpu_custom_call" | custom-call | flops 17179869184 | bytes 29360128 | tf_op jit(solution)/shard_map/two_nt/pallas_call | solution.py:334
  528.6 23.8 %convolution_convert_fusion.1 = bf16[2048,2048]{1,0:T(8,128)(2,1)} fusion(bf16[2048,2048]{1,0:T(8,128)(2,1)} %copy-done.24, bf16[2048,2048]{1,0:T(8,128)(2,1)} %get-tuple-element.51.b_ref), kind=kOutput, calls=%fused_computation.1 | convolution fusion | flops 17184063488 | bytes 25165824 | tf_op jit(solution)/shard_map/dot_general | solution.py:30
  554.0 3.1 fusion.48
  561.3 21.8 %collective-permute-done.25 = bf16[256,2048]{1,0:T(8,128)(2,1)S(1)} collective-permute-done((bf16[256,2048]{1,0:T(8,128)(2,1)S(1)}, bf16[256,2048]{1,0:T(8,128)(2,1)S(1)}, u32[]{:S(2)}, u32[]{:S(2)}) %collective-permute-start.25) | collective-permute-done | bytes 1048608 | tf_op jit(solution)/shard_map/ppermute | solution.py:348
  587.8 17.8 %collective-permute-done.24 = bf16[256,2048]{1,0:T(8,128)(2,1)S(1)} collective-permute-done((bf16[256,2048]{1,0:T(8,128)(2,1)S(1)}, bf16[256,2048]{1,0:T(8,128)(2,1)S(1)}, u32[]{:S(2)}, u32[]{:S(2)}) %collective-permute-start.24) | collective-permute-done | bytes 1048608 | tf_op jit(solution)/shard_map/ppermute | solution.py:348
  605.9 17.8 %collective-permute-done.26 = bf16[256,2048]{1,0:T(8,128)(2,1)S(1)} collective-permute-done((bf16[256,2048]{1,0:T(8,128)(2,1)S(1)}, bf16[256,2048]{1,0:T(8,128)(2,1)S(1)}, u32[]{:S(2)}, u32[]{:S(2)}) %collective-permute-start.26) | collective-permute-done | bytes 1048608 | tf_op jit(solution)/shard_map/ppermute | solution.py:348
  623.8 2.7 multiply_reduce_fusion.1
  626.5 3.7 fusion.42
  634.3 20.5 %convolution_convert_fusion = bf16[2048,2048]{1,0:T(8,128)(2,1)} fusion(bf16[2048,2048]{1,0:T(8,128)(2,1)S(1)} %bitcast.72, bf16[2048,2048]{1,0:T(8,128)(2,1)S(1)} %bitcast.66), kind=kOutput, calls=%fused_computation | convolution fusion | flops 17184063488 | bytes 25165824 | tf_op jit(solution)/shard_map/dot_general | solution.py:26
  656.7 23.4 %collective-permute-done.30 = bf16[256,2048]{1,0:T(8,128)(2,1)S(1)} collective-permute-done((bf16[256,2048]{1,0:T(8,128)(2,1)S(1)}, bf16[256,2048]{1,0:T(8,128)(2,1)S(1)}, u32[]{:S(2)}, u32[]{:S(2)}) %collective-permute-start.30) | collective-permute-done | bytes 1048608 | tf_op jit(solution)/shard_map/ppermute | solution.py:348
  681.2 15.2 %collective-permute-done.31 = bf16[256,2048]{1,0:T(8,128)(2,1)S(1)} collective-permute-done((bf16[256,2048]{1,0:T(8,128)(2,1)S(1)}, bf16[256,2048]{1,0:T(8,128)(2,1)S(1)}, u32[]{:S(2)}, u32[]{:S(2)}) %collective-permute-start.31) | collective-permute-done | bytes 1048608 | tf_op jit(solution)/shard_map/ppermute | solution.py:348
  696.7 5.6 convolution_convert_fusion.10.g_ref
  702.3 29.1 %attend_back.2 = bf16[1024,1536]{1,0:T(8,128)(2,1)} custom-call(s32[2]{0:T(128)} %get-tuple-element.143.info, bf16[1024,512]{1,0:T(8,128)(2,1)} %get-tuple-element.58.q_ref, bf16[1024,512]{1,0:T(8,128)(2,1)} %get-tuple-element.59.k_ref, bf16[1024,512]{1,0:T(8,128)(2,1)} %get-tuple-element.60.v_ref, bf16[1024,512]{1,0:T(8,128)(2,1)} %get-tuple-element.41.a_ref, ...), custom_call_target="tpu_custom_call" | custom-call | flops 10737418240 | bytes 10485760 | tf_op jit(solution)/shard_map/attend_back/pallas_call | solution.py:241
  731.5 11.3 %convolution_convert_fusion.6 = bf16[1024,2048]{1,0:T(8,128)(2,1)} fusion(bf16[1024,1536]{1,0:T(8,128)(2,1)} %attend_back.2, bf16[2048,1536]{1,0:T(8,128)(2,1)} %all-gather.6.cloned.1.call-done), kind=kOutput, calls=%fused_computation.9 | convolution fusion | flops 6444548096 | bytes 13631488 | tf_op jit(solution)/shard_map/dot_general | solution.py:26
  742.7 5.7 convolution_convert_fusion.9
  748.6 22.7 %attend_back.3 = bf16[1024,1536]{1,0:T(8,128)(2,1)} custom-call(s32[2]{0:T(128)} %get-tuple-element.142.info, bf16[1024,512]{1,0:T(8,128)(2,1)} %get-tuple-element.63.q_ref, bf16[1024,512]{1,0:T(8,128)(2,1)} %get-tuple-element.64.k_ref, bf16[1024,512]{1,0:T(8,128)(2,1)} %get-tuple-element.65.v_ref, bf16[1024,512]{1,0:T(8,128)(2,1)} %get-tuple-element.40.a_ref, ...), custom_call_target="tpu_custom_call" | custom-call | flops 10737418240 | bytes 10485760 | tf_op jit(solution)/shard_map/attend_back/pallas_call | solution.py:241
  771.2 19.3 %convolution_convert_fusion.4 = bf16[2048,1536]{1,0:T(8,128)(2,1)} fusion(bf16[2048,2048]{1,0:T(8,128)(2,1)} %constant_dynamic-update-slice_fusion, bf16[1024,1536]{1,0:T(8,128)(2,1)} %attend_back.2, bf16[1024,1536]{1,0:T(8,128)(2,1)} %attend_back.3), kind=kOutput, calls=%fused_computation.4 | convolution fusion | flops 12900630528 | bytes 20971520 | tf_op jit(solution)/shard_map/dot_general | solution.py:30
  790.5 3.3 fusion.47
  795.2 3.7 fusion.46
  800.6 7.1 convolution_convert_fusion.5
  810.8 32.8 %collective-permute-done.34 = bf16[256,2048]{1,0:T(8,128)(2,1)S(1)} collective-permute-done((bf16[256,2048]{1,0:T(8,128)(2,1)S(1)}, bf16[256,2048]{1,0:T(8,128)(2,1)S(1)}, u32[]{:S(2)}, u32[]{:S(2)}) %collective-permute-start.34) | collective-permute-done | bytes 1048608 | tf_op jit(solution)/shard_map/ppermute | solution.py:348
  844.4 2.6 add_convert_fusion.6
  848.2 2.6 add_convert_fusion
  852.4 13.7 %collective-permute-done.33 = bf16[256,2048]{1,0:T(8,128)(2,1)} collective-permute-done((bf16[256,2048]{1,0:T(8,128)(2,1)S(1)}, bf16[256,2048]{1,0:T(8,128)(2,1)}, u32[]{:S(2)}, u32[]{:S(2)}) %collective-permute-start.33) | collective-permute-done | bytes 1048608 | tf_op jit(solution)/shard_map/ppermute | solution.py:348
  866.3 3.4 collective-permute-done.37
  870.5 21.5 %collective-permute-done.35 = bf16[256,2048]{1,0:T(8,128)(2,1)S(1)} collective-permute-done((bf16[256,2048]{1,0:T(8,128)(2,1)}, bf16[256,2048]{1,0:T(8,128)(2,1)S(1)}, u32[]{:S(2)}, u32[]{:S(2)}) %collective-permute-start.35) | collective-permute-done | bytes 1048608 | tf_op jit(solution)/shard_map/ppermute | solution.py:348
  893.9 5.3 multiply_convert_fusion.1
  899.9 11.1 %collective-permute-done.44 = bf16[256,2048]{1,0:T(8,128)(2,1)} collective-permute-done((bf16[256,2048]{1,0:T(8,128)(2,1)}, bf16[256,2048]{1,0:T(8,128)(2,1)}, u32[]{:S(2)}, u32[]{:S(2)}) %collective-permute-start.44) | collective-permute-done | bytes 1048608 | tf_op jit(solution)/shard_map/ppermute | solution.py:348
  911.0 3.6 collective-permute-done.41
  914.6 3.6 fusion.17
  918.3 2.8 convert_element_type.385
  921.1 2.8 convert_element_type.384
  923.9 3.0 convert_element_type.383
  927.0 6.1 fusion.16
  933.3 3.3 pad_maximum_fusion.3
  937.0 2.6 multiply_convert_fusion
  944.8 2.3 fusion.50
  (292 shorter events, 95.4 us)
Async XLA Ops:
  7.2 83.0 %all-gather.6.cloned.1.call-start = ((), (), s32[]{:S(2)}) async-start(), calls=%async_computation.5 | async-start | bytes 7077888 | tf_op jit(solution)/shard_map/all_gather | solution.py:427
  9.4 123.6 %all-gather.8.cloned.1.call-start = ((), (), s32[]{:S(2)}) async-start(), calls=%async_computation.6 | async-start | bytes 2359296 | tf_op jit(solution)/shard_map/all_gather | solution.py:427
  10.2 289.8 %all-gather.10.cloned.1.call-start = ((), (), s32[]{:S(2)}) async-start(), calls=%async_computation.7 | async-start | bytes 9437184 | tf_op jit(solution)/shard_map/all_gather | solution.py:427
  10.9 289.0 %all-gather.12.cloned.1.call-start = ((), (), s32[]{:S(2)}) async-start(), calls=%async_computation.8 | async-start | bytes 9437184 | tf_op jit(solution)/shard_map/all_gather | solution.py:427
  11.5 403.6 %all-gather.14.cloned.1.call-start = ((), (), s32[]{:S(2)}) async-start(), calls=%async_computation.9 | async-start | bytes 9437184 | tf_op jit(solution)/shard_map/all_gather | solution.py:427
  13.7 27.2 %collective-permute-start = (bf16[256,2048]{1,0:T(8,128)(2,1)}, bf16[256,2048]{1,0:T(8,128)(2,1)S(1)}, u32[]{:S(2)}, u32[]{:S(2)}) collective-permute-start(bf16[256,2048]{1,0:T(8,128)(2,1)} %get-tuple-element.98), channel_id=1, source_target_pairs={{0,1},{1,0},{2,3},{3,2},{4,5},{5,4},{6,7},{7,6},{8,9},{9,8},{10,11... | collective-permute-start | bytes 3145736 | tf_op jit(solution)/shard_map/ppermute | solution.py:348
  18.3 26.6 %collective-permute-start.3 = (bf16[256,2048]{1,0:T(8,128)(2,1)}, bf16[256,2048]{1,0:T(8,128)(2,1)}, u32[]{:S(2)}, u32[]{:S(2)}) collective-permute-start(bf16[256,2048]{1,0:T(8,128)(2,1)} %get-tuple-element.96), channel_id=1, source_target_pairs={{0,2},{1,3},{2,0},{3,1},{4,6},{5,7},{6,4},{7,5},{8,10},{9,11},{10,... | collective-permute-start | bytes 3145736 | tf_op jit(solution)/shard_map/ppermute | solution.py:348
  19.8 43.7 %collective-permute-start.1 = (bf16[256,2048]{1,0:T(8,128)(2,1)}, bf16[256,2048]{1,0:T(8,128)(2,1)}, u32[]{:S(2)}, u32[]{:S(2)}) collective-permute-start(bf16[256,2048]{1,0:T(8,128)(2,1)} %get-tuple-element.96), channel_id=1, source_target_pairs={{0,1},{1,0},{2,3},{3,2},{4,5},{5,4},{6,7},{7,6},{8,9},{9,8},{10,11... | collective-permute-start | bytes 3145736 | tf_op jit(solution)/shard_map/ppermute | solution.py:348
  20.4 46.8 %collective-permute-start.2 = (bf16[256,2048]{1,0:T(8,128)(2,1)}, bf16[256,2048]{1,0:T(8,128)(2,1)}, u32[]{:S(2)}, u32[]{:S(2)}) collective-permute-start(bf16[256,2048]{1,0:T(8,128)(2,1)} %get-tuple-element.98), channel_id=1, source_target_pairs={{0,2},{1,3},{2,0},{3,1},{4,6},{5,7},{6,4},{7,5},{8,10},{9,11},{10,... | collective-permute-start | bytes 3145736 | tf_op jit(solution)/shard_map/ppermute | solution.py:348
  40.9 47.2 %collective-permute-start.4 = (bf16[256,2048]{1,0:T(8,128)(2,1)S(1)}, bf16[256,2048]{1,0:T(8,128)(2,1)S(1)}, u32[]{:S(2)}, u32[]{:S(2)}) collective-permute-start(bf16[256,2048]{1,0:T(8,128)(2,1)S(1)} %collective-permute-done), channel_id=1, source_target_pairs={{0,2},{1,3},{2,0},{3,1},{4,6},{5,7},{6,4},{7,5},{8,10},{9,11},{10,... | collective-permute-start | bytes 3145736 | tf_op jit(solution)/shard_map/ppermute | solution.py:348
  44.9 44.2 %collective-permute-start.5 = (bf16[256,2048]{1,0:T(8,128)(2,1)}, bf16[256,2048]{1,0:T(8,128)(2,1)S(1)}, u32[]{:S(2)}, u32[]{:S(2)}) collective-permute-start(bf16[256,2048]{1,0:T(8,128)(2,1)} %collective-permute-done.3), channel_id=1, source_target_pairs={{0,1},{1,0},{2,3},{3,2},{4,5},{5,4},{6,7},{7,6},{8,9},{9,8},{10,11... | collective-permute-start | bytes 3145736 | tf_op jit(solution)/shard_map/ppermute | solution.py:348
  140.3 33.2 %collective-permute-start.10 = (bf16[256,2048]{1,0:T(8,128)(2,1)}, bf16[256,2048]{1,0:T(8,128)(2,1)S(1)}, u32[]{:S(2)}, u32[]{:S(2)}) collective-permute-start(bf16[256,2048]{1,0:T(8,128)(2,1)} %get-tuple-element.118), channel_id=1, source_target_pairs={{0,1},{1,0},{2,3},{3,2},{4,5},{5,4},{6,7},{7,6},{8,9},{9,8},{10,11... | collective-permute-start | bytes 3145736 | tf_op jit(solution)/shard_map/ppermute | solution.py:348
  140.6 777.7 %reduce-scatter.10.cloned.1.call-start = ((), (), s32[]{:S(2)}) async-start(), calls=%async_computation.12 | async-start | bytes 9437184 | tf_op jit(solution)/shard_map/reduce_scatter | solution.py:532
  140.6 35.5 %collective-permute-start.7 = (bf16[256,2048]{1,0:T(8,128)(2,1)}, bf16[256,2048]{1,0:T(8,128)(2,1)}, u32[]{:S(2)}, u32[]{:S(2)}) collective-permute-start(bf16[256,2048]{1,0:T(8,128)(2,1)} %get-tuple-element.119), channel_id=1, source_target_pairs={{0,2},{1,3},{2,0},{3,1},{4,6},{5,7},{6,4},{7,5},{8,10},{9,11},{10,... | collective-permute-start | bytes 3145736 | tf_op jit(solution)/shard_map/ppermute | solution.py:348
  164.5 22.2 %collective-permute-start.9 = (bf16[256,2048]{1,0:T(8,128)(2,1)}, bf16[256,2048]{1,0:T(8,128)(2,1)}, u32[]{:S(2)}, u32[]{:S(2)}) collective-permute-start(bf16[256,2048]{1,0:T(8,128)(2,1)} %slice.227), channel_id=1, source_target_pairs={{0,1},{1,0},{2,3},{3,2},{4,5},{5,4},{6,7},{7,6},{8,9},{9,8},{10,11... | collective-permute-start | bytes 3145736 | tf_op jit(solution)/shard_map/ppermute | solution.py:348
  166.3 31.5 %collective-permute-start.6 = (bf16[256,2048]{1,0:T(8,128)(2,1)}, bf16[256,2048]{1,0:T(8,128)(2,1)}, u32[]{:S(2)}, u32[]{:S(2)}) collective-permute-start(bf16[256,2048]{1,0:T(8,128)(2,1)} %get-tuple-element.117), channel_id=1, source_target_pairs={{0,2},{1,3},{2,0},{3,1},{4,6},{5,7},{6,4},{7,5},{8,10},{9,11},{10,... | collective-permute-start | bytes 3145736 | tf_op jit(solution)/shard_map/ppermute | solution.py:348
  176.2 42.6 %collective-permute-start.11 = (bf16[256,2048]{1,0:T(8,128)(2,1)}, bf16[256,2048]{1,0:T(8,128)(2,1)}, u32[]{:S(2)}, u32[]{:S(2)}) collective-permute-start(bf16[256,2048]{1,0:T(8,128)(2,1)} %add_convert_fusion.12), channel_id=1, source_target_pairs={{0,2},{1,3},{2,0},{3,1},{4,6},{5,7},{6,4},{7,5},{8,10},{9,11},{10,... | collective-permute-start | bytes 3145736 | tf_op jit(solution)/shard_map/ppermute | solution.py:348
  177.8 40.9 %collective-permute-start.8 = (bf16[256,2048]{1,0:T(8,128)(2,1)S(1)}, bf16[256,2048]{1,0:T(8,128)(2,1)}, u32[]{:S(2)}, u32[]{:S(2)}) collective-permute-start(bf16[256,2048]{1,0:T(8,128)(2,1)S(1)} %add_convert_fusion.14), channel_id=1, source_target_pairs={{0,1},{1,0},{2,3},{3,2},{4,5},{5,4},{6,7},{7,6},{8,9},{9,8},{10,11... | collective-permute-start | bytes 3145736 | tf_op jit(solution)/shard_map/ppermute | solution.py:348
  178.5 44.4 %copy-start.20 = (f32[2048]{0:T(1024)S(1)}, f32[2048]{0:T(1024)}, u32[]{:S(2)}) copy-start(f32[2048]{0:T(1024)} %param.14) | copy-start | bytes 24580
  224.2 26.0 %collective-permute-start.12 = (bf16[256,2048]{1,0:T(8,128)(2,1)S(1)}, bf16[256,2048]{1,0:T(8,128)(2,1)S(1)}, u32[]{:S(2)}, u32[]{:S(2)}) collective-permute-start(bf16[256,2048]{1,0:T(8,128)(2,1)S(1)} %get-tuple-element.92), channel_id=1, source_target_pairs={{0,1},{1,0},{2,3},{3,2},{4,5},{5,4},{6,7},{7,6},{8,9},{9,8},{10,11... | collective-permute-start | bytes 3145736 | tf_op jit(solution)/shard_map/ppermute | solution.py:348
  225.2 26.1 %collective-permute-start.15 = (bf16[256,2048]{1,0:T(8,128)(2,1)S(1)}, bf16[256,2048]{1,0:T(8,128)(2,1)S(1)}, u32[]{:S(2)}, u32[]{:S(2)}) collective-permute-start(bf16[256,2048]{1,0:T(8,128)(2,1)S(1)} %get-tuple-element.88), channel_id=1, source_target_pairs={{0,2},{1,3},{2,0},{3,1},{4,6},{5,7},{6,4},{7,5},{8,10},{9,11},{10,... | collective-permute-start | bytes 3145736 | tf_op jit(solution)/shard_map/ppermute | solution.py:348
  226.5 46.2 %collective-permute-start.13 = (bf16[256,2048]{1,0:T(8,128)(2,1)S(1)}, bf16[256,2048]{1,0:T(8,128)(2,1)S(1)}, u32[]{:S(2)}, u32[]{:S(2)}) collective-permute-start(bf16[256,2048]{1,0:T(8,128)(2,1)S(1)} %get-tuple-element.88), channel_id=1, source_target_pairs={{0,1},{1,0},{2,3},{3,2},{4,5},{5,4},{6,7},{7,6},{8,9},{9,8},{10,11... | collective-permute-start | bytes 3145736 | tf_op jit(solution)/shard_map/ppermute | solution.py:348
  228.0 45.7 %collective-permute-start.14 = (bf16[256,2048]{1,0:T(8,128)(2,1)S(1)}, bf16[256,2048]{1,0:T(8,128)(2,1)S(1)}, u32[]{:S(2)}, u32[]{:S(2)}) collective-permute-start(bf16[256,2048]{1,0:T(8,128)(2,1)S(1)} %get-tuple-element.92), channel_id=1, source_target_pairs={{0,2},{1,3},{2,0},{3,1},{4,6},{5,7},{6,4},{7,5},{8,10},{9,11},{10,... | collective-permute-start | bytes 3145736 | tf_op jit(solution)/shard_map/ppermute | solution.py:348
  250.2 43.5 %collective-permute-start.16 = (bf16[256,2048]{1,0:T(8,128)(2,1)S(1)}, bf16[256,2048]{1,0:T(8,128)(2,1)S(1)}, u32[]{:S(2)}, u32[]{:S(2)}) collective-permute-start(bf16[256,2048]{1,0:T(8,128)(2,1)S(1)} %collective-permute-done.12), channel_id=1, source_target_pairs={{0,2},{1,3},{2,0},{3,1},{4,6},{5,7},{6,4},{7,5},{8,10},{9,11},{10,... | collective-permute-start | bytes 3145736 | tf_op jit(solution)/shard_map/ppermute | solution.py:348
  251.2 42.6 %collective-permute-start.17 = (bf16[256,2048]{1,0:T(8,128)(2,1)S(1)}, bf16[256,2048]{1,0:T(8,128)(2,1)S(1)}, u32[]{:S(2)}, u32[]{:S(2)}) collective-permute-start(bf16[256,2048]{1,0:T(8,128)(2,1)S(1)} %collective-permute-done.15), channel_id=1, source_target_pairs={{0,1},{1,0},{2,3},{3,2},{4,5},{5,4},{6,7},{7,6},{8,9},{9,8},{10,11... | collective-permute-start | bytes 3145736 | tf_op jit(solution)/shard_map/ppermute | solution.py:348
  293.9 54.7 %collective-permute-start.18 = (bf16[512,2048]{1,0:T(8,128)(2,1)S(1)}, bf16[512,2048]{1,0:T(8,128)(2,1)}, u32[]{:S(2)}, u32[]{:S(2)}) collective-permute-start(bf16[512,2048]{1,0:T(8,128)(2,1)S(1)} %pad_maximum_fusion), channel_id=1, source_target_pairs={{0,1},{1,0},{2,3},{3,2},{4,5},{5,4},{6,7},{7,6},{8,9},{9,8},{10,11... | collective-permute-start | bytes 6291464 | tf_op jit(solution)/shard_map/ppermute | solution.py:348
  297.2 90.3 %collective-permute-start.19 = (bf16[512,2048]{1,0:T(8,128)(2,1)S(1)}, bf16[512,2048]{1,0:T(8,128)(2,1)}, u32[]{:S(2)}, u32[]{:S(2)}) collective-permute-start(bf16[512,2048]{1,0:T(8,128)(2,1)S(1)} %pad_maximum_fusion), channel_id=1, source_target_pairs={{0,2},{1,3},{2,0},{3,1},{4,6},{5,7},{6,4},{7,5},{8,10},{9,11},{10,... | collective-permute-start | bytes 6291464 | tf_op jit(solution)/shard_map/ppermute | solution.py:348
  297.5 91.8 %collective-permute-start.20 = (bf16[512,2048]{1,0:T(8,128)(2,1)S(1)}, bf16[512,2048]{1,0:T(8,128)(2,1)}, u32[]{:S(2)}, u32[]{:S(2)}) collective-permute-start(bf16[512,2048]{1,0:T(8,128)(2,1)S(1)} %pad_maximum_fusion), channel_id=1, source_target_pairs={{0,3},{1,2},{2,1},{3,0},{4,7},{5,6},{6,5},{7,4},{8,11},{9,10},{10,... | collective-permute-start | bytes 6291464 | tf_op jit(solution)/shard_map/ppermute | solution.py:348
  348.5 46.0 %slice-start.4 = ((s8[8388608]{0:T(1024)(128)(4,1)}), s8[4194304]{0:T(1024)(128)(4,1)S(1)}, s32[]{:S(2)}) async-start(s8[8388608]{0:T(1024)(128)(4,1)} %bitcast.69), calls=%async_computation.19 | async-start | bytes 8388608
  350.5 43.9 %slice-start.5 = ((s8[8388608]{0:T(1024)(128)(4,1)}), s8[4194304]{0:T(1024)(128)(4,1)S(1)}, s32[]{:S(2)}) async-start(s8[8388608]{0:T(1024)(128)(4,1)} %bitcast.69), calls=%async_computation.20 | async-start | bytes 8388608
  552.4 368.7 %reduce-scatter.8.cloned.1.call-start = ((), (), s32[]{:S(2)}) async-start(), calls=%async_computation.11 | async-start | bytes 9437184 | tf_op jit(solution)/shard_map/reduce_scatter | solution.py:532
  553.2 370.7 %reduce-scatter.6.cloned.1.call-start = ((), (), s32[]{:S(2)}) async-start(), calls=%async_computation.10 | async-start | bytes 9437184 | tf_op jit(solution)/shard_map/reduce_scatter | solution.py:532
  553.9 387.6 %reduce-scatter.14.cloned.1.call-start = ((), (), s32[]{:S(2)}) async-start(), calls=%async_computation.14 | async-start | bytes 2359296 | tf_op jit(solution)/shard_map/reduce_scatter | solution.py:532
  557.0 26.1 %collective-permute-start.25 = (bf16[256,2048]{1,0:T(8,128)(2,1)S(1)}, bf16[256,2048]{1,0:T(8,128)(2,1)S(1)}, u32[]{:S(2)}, u32[]{:S(2)}) collective-permute-start(bf16[256,2048]{1,0:T(8,128)(2,1)S(1)} %get-tuple-element.114), channel_id=1, source_target_pairs={{0,1},{1,0},{2,3},{3,2},{4,5},{5,4},{6,7},{7,6},{8,9},{9,8},{10,11... | collective-permute-start | bytes 3145736 | tf_op jit(solution)/shard_map/ppermute | solution.py:348
  557.4 27.5 %collective-permute-start.22 = (bf16[256,2048]{1,0:T(8,128)(2,1)S(1)}, bf16[256,2048]{1,0:T(8,128)(2,1)S(1)}, u32[]{:S(2)}, u32[]{:S(2)}) collective-permute-start(bf16[256,2048]{1,0:T(8,128)(2,1)S(1)} %get-tuple-element.115), channel_id=1, source_target_pairs={{0,2},{1,3},{2,0},{3,1},{4,6},{5,7},{6,4},{7,5},{8,10},{9,11},{10,... | collective-permute-start | bytes 3145736 | tf_op jit(solution)/shard_map/ppermute | solution.py:348
  557.9 47.6 %collective-permute-start.24 = (bf16[256,2048]{1,0:T(8,128)(2,1)S(1)}, bf16[256,2048]{1,0:T(8,128)(2,1)S(1)}, u32[]{:S(2)}, u32[]{:S(2)}) collective-permute-start(bf16[256,2048]{1,0:T(8,128)(2,1)S(1)} %slice.235), channel_id=1, source_target_pairs={{0,1},{1,0},{2,3},{3,2},{4,5},{5,4},{6,7},{7,6},{8,9},{9,8},{10,11... | collective-permute-start | bytes 3145736 | tf_op jit(solution)/shard_map/ppermute | solution.py:348
  559.3 46.6 %collective-permute-start.21 = (bf16[256,2048]{1,0:T(8,128)(2,1)S(1)}, bf16[256,2048]{1,0:T(8,128)(2,1)S(1)}, u32[]{:S(2)}, u32[]{:S(2)}) collective-permute-start(bf16[256,2048]{1,0:T(8,128)(2,1)S(1)} %get-tuple-element.116), channel_id=1, source_target_pairs={{0,2},{1,3},{2,0},{3,1},{4,6},{5,7},{6,4},{7,5},{8,10},{9,11},{10,... | collective-permute-start | bytes 3145736 | tf_op jit(solution)/shard_map/ppermute | solution.py:348
  584.8 39.0 %collective-permute-start.26 = (bf16[256,2048]{1,0:T(8,128)(2,1)S(1)}, bf16[256,2048]{1,0:T(8,128)(2,1)S(1)}, u32[]{:S(2)}, u32[]{:S(2)}) collective-permute-start(bf16[256,2048]{1,0:T(8,128)(2,1)S(1)} %add_convert_fusion.8), channel_id=1, source_target_pairs={{0,2},{1,3},{2,0},{3,1},{4,6},{5,7},{6,4},{7,5},{8,10},{9,11},{10,... | collective-permute-start | bytes 3145736 | tf_op jit(solution)/shard_map/ppermute | solution.py:348
  585.3 38.4 %collective-permute-start.23 = (bf16[256,2048]{1,0:T(8,128)(2,1)S(1)}, bf16[256,2048]{1,0:T(8,128)(2,1)S(1)}, u32[]{:S(2)}, u32[]{:S(2)}) collective-permute-start(bf16[256,2048]{1,0:T(8,128)(2,1)S(1)} %add_convert_fusion.10), channel_id=1, source_target_pairs={{0,1},{1,0},{2,3},{3,2},{4,5},{5,4},{6,7},{7,6},{8,9},{9,8},{10,11... | collective-permute-start | bytes 3145736 | tf_op jit(solution)/shard_map/ppermute | solution.py:348
  630.2 26.0 %collective-permute-start.27 = (bf16[256,2048]{1,0:T(8,128)(2,1)S(1)}, bf16[256,2048]{1,0:T(8,128)(2,1)S(1)}, u32[]{:S(2)}, u32[]{:S(2)}) collective-permute-start(bf16[256,2048]{1,0:T(8,128)(2,1)S(1)} %get-tuple-element.53), channel_id=1, source_target_pairs={{0,1},{1,0},{2,3},{3,2},{4,5},{5,4},{6,7},{7,6},{8,9},{9,8},{10,11... | collective-permute-start | bytes 3145736 | tf_op jit(solution)/shard_map/ppermute | solution.py:348
  631.6 49.4 %collective-permute-start.29 = (bf16[256,2048]{1,0:T(8,128)(2,1)S(1)}, bf16[256,2048]{1,0:T(8,128)(2,1)S(1)}, u32[]{:S(2)}, u32[]{:S(2)}) collective-permute-start(bf16[256,2048]{1,0:T(8,128)(2,1)S(1)} %get-tuple-element.53), channel_id=1, source_target_pairs={{0,2},{1,3},{2,0},{3,1},{4,6},{5,7},{6,4},{7,5},{8,10},{9,11},{10,... | collective-permute-start | bytes 3145736 | tf_op jit(solution)/shard_map/ppermute | solution.py:348
  631.8 49.0 %collective-permute-start.28 = (bf16[256,2048]{1,0:T(8,128)(2,1)S(1)}, bf16[256,2048]{1,0:T(8,128)(2,1)S(1)}, u32[]{:S(2)}, u32[]{:S(2)}) collective-permute-start(bf16[256,2048]{1,0:T(8,128)(2,1)S(1)} %get-tuple-element.54), channel_id=1, source_target_pairs={{0,1},{1,0},{2,3},{3,2},{4,5},{5,4},{6,7},{7,6},{8,9},{9,8},{10,11... | collective-permute-start | bytes 3145736 | tf_op jit(solution)/shard_map/ppermute | solution.py:348
  632.6 47.5 %collective-permute-start.30 = (bf16[256,2048]{1,0:T(8,128)(2,1)S(1)}, bf16[256,2048]{1,0:T(8,128)(2,1)S(1)}, u32[]{:S(2)}, u32[]{:S(2)}) collective-permute-start(bf16[256,2048]{1,0:T(8,128)(2,1)S(1)} %get-tuple-element.54), channel_id=1, source_target_pairs={{0,2},{1,3},{2,0},{3,1},{4,6},{5,7},{6,4},{7,5},{8,10},{9,11},{10,... | collective-permute-start | bytes 3145736 | tf_op jit(solution)/shard_map/ppermute | solution.py:348
  656.3 40.2 %collective-permute-start.31 = (bf16[256,2048]{1,0:T(8,128)(2,1)S(1)}, bf16[256,2048]{1,0:T(8,128)(2,1)S(1)}, u32[]{:S(2)}, u32[]{:S(2)}) collective-permute-start(bf16[256,2048]{1,0:T(8,128)(2,1)S(1)} %collective-permute-done.27), channel_id=1, source_target_pairs={{0,2},{1,3},{2,0},{3,1},{4,6},{5,7},{6,4},{7,5},{8,10},{9,11},{10,... | collective-permute-start | bytes 3145736 | tf_op jit(solution)/shard_map/ppermute | solution.py:348
  680.1 16.5 %collective-permute-start.32 = (bf16[256,2048]{1,0:T(8,128)(2,1)S(1)}, bf16[256,2048]{1,0:T(8,128)(2,1)S(1)}, u32[]{:S(2)}, u32[]{:S(2)}) collective-permute-start(bf16[256,2048]{1,0:T(8,128)(2,1)S(1)} %collective-permute-done.30), channel_id=1, source_target_pairs={{0,1},{1,0},{2,3},{3,2},{4,5},{5,4},{6,7},{7,6},{8,9},{9,8},{10,11... | collective-permute-start | bytes 3145736 | tf_op jit(solution)/shard_map/ppermute | solution.py:348
  748.5 196.3 %reduce-scatter.12.cloned.1.call-start = ((), (), s32[]{:S(2)}) async-start(), calls=%async_computation.13 | async-start | bytes 7077888 | tf_op jit(solution)/shard_map/reduce_scatter | solution.py:532
  793.8 53.1 %collective-permute-start.43 = (bf16[256,2048]{1,0:T(8,128)(2,1)S(1)}, bf16[256,2048]{1,0:T(8,128)(2,1)S(1)}, u32[]{:S(2)}, u32[]{:S(2)}) collective-permute-start(bf16[256,2048]{1,0:T(8,128)(2,1)S(1)} %get-tuple-element.112), channel_id=1, source_target_pairs={{0,1},{1,0},{2,3},{3,2},{4,5},{5,4},{6,7},{7,6},{8,9},{9,8},{10,11... | collective-permute-start | bytes 3145736 | tf_op jit(solution)/shard_map/ppermute | solution.py:348
  795.0 55.7 %collective-permute-start.40 = (bf16[256,2048]{1,0:T(8,128)(2,1)S(1)}, bf16[256,2048]{1,0:T(8,128)(2,1)S(1)}, u32[]{:S(2)}, u32[]{:S(2)}) collective-permute-start(bf16[256,2048]{1,0:T(8,128)(2,1)S(1)} %get-tuple-element.113), channel_id=1, source_target_pairs={{0,2},{1,3},{2,0},{3,1},{4,6},{5,7},{6,4},{7,5},{8,10},{9,11},{10,... | collective-permute-start | bytes 3145736 | tf_op jit(solution)/shard_map/ppermute | solution.py:348
  798.9 44.6 %collective-permute-start.34 = (bf16[256,2048]{1,0:T(8,128)(2,1)S(1)}, bf16[256,2048]{1,0:T(8,128)(2,1)S(1)}, u32[]{:S(2)}, u32[]{:S(2)}) collective-permute-start(bf16[256,2048]{1,0:T(8,128)(2,1)S(1)} %get-tuple-element.104), channel_id=1, source_target_pairs={{0,2},{1,3},{2,0},{3,1},{4,6},{5,7},{6,4},{7,5},{8,10},{9,11},{10,... | collective-permute-start | bytes 3145736 | tf_op jit(solution)/shard_map/ppermute | solution.py:348
  807.8 43.2 %copy-start.9 = (bf16[1024,2048]{1,0:T(8,128)(2,1)}, bf16[1024,2048]{1,0:T(8,128)(2,1)S(1)}, u32[]{:S(2)}) copy-start(bf16[1024,2048]{1,0:T(8,128)(2,1)S(1)} %convolution_convert_fusion.5) | copy-start | bytes 12582916
  808.9 90.3 %collective-permute-start.42 = (bf16[256,2048]{1,0:T(8,128)(2,1)}, bf16[256,2048]{1,0:T(8,128)(2,1)}, u32[]{:S(2)}, u32[]{:S(2)}) collective-permute-start(bf16[256,2048]{1,0:T(8,128)(2,1)} %slice.243), channel_id=1, source_target_pairs={{0,1},{1,0},{2,3},{3,2},{4,5},{5,4},{6,7},{7,6},{8,9},{9,8},{10,11... | collective-permute-start | bytes 3145736 | tf_op jit(solution)/shard_map/ppermute | solution.py:348
  810.0 56.1 %collective-permute-start.33 = (bf16[256,2048]{1,0:T(8,128)(2,1)S(1)}, bf16[256,2048]{1,0:T(8,128)(2,1)}, u32[]{:S(2)}, u32[]{:S(2)}) collective-permute-start(bf16[256,2048]{1,0:T(8,128)(2,1)S(1)} %get-tuple-element.101), channel_id=1, source_target_pairs={{0,2},{1,3},{2,0},{3,1},{4,6},{5,7},{6,4},{7,5},{8,10},{9,11},{10,... | collective-permute-start | bytes 3145736 | tf_op jit(solution)/shard_map/ppermute | solution.py:348
  843.5 26.1 %collective-permute-start.37 = (bf16[256,2048]{1,0:T(8,128)(2,1)S(1)}, bf16[256,2048]{1,0:T(8,128)(2,1)}, u32[]{:S(2)}, u32[]{:S(2)}) collective-permute-start(bf16[256,2048]{1,0:T(8,128)(2,1)S(1)} %get-tuple-element.102), channel_id=1, source_target_pairs={{0,1},{1,0},{2,3},{3,2},{4,5},{5,4},{6,7},{7,6},{8,9},{9,8},{10,11... | collective-permute-start | bytes 3145736 | tf_op jit(solution)/shard_map/ppermute | solution.py:348
  847.0 45.1 %collective-permute-start.35 = (bf16[256,2048]{1,0:T(8,128)(2,1)}, bf16[256,2048]{1,0:T(8,128)(2,1)S(1)}, u32[]{:S(2)}, u32[]{:S(2)}) collective-permute-start(bf16[256,2048]{1,0:T(8,128)(2,1)} %add_convert_fusion.6), channel_id=1, source_target_pairs={{0,1},{1,0},{2,3},{3,2},{4,5},{5,4},{6,7},{7,6},{8,9},{9,8},{10,11... | collective-permute-start | bytes 3145736 | tf_op jit(solution)/shard_map/ppermute | solution.py:348
  850.8 49.1 %collective-permute-start.39 = (bf16[256,2048]{1,0:T(8,128)(2,1)}, bf16[256,2048]{1,0:T(8,128)(2,1)}, u32[]{:S(2)}, u32[]{:S(2)}) collective-permute-start(bf16[256,2048]{1,0:T(8,128)(2,1)} %get-tuple-element.111), channel_id=1, source_target_pairs={{0,2},{1,3},{2,0},{3,1},{4,6},{5,7},{6,4},{7,5},{8,10},{9,11},{10,... | collective-permute-start | bytes 3145736 | tf_op jit(solution)/shard_map/ppermute | solution.py:348
  866.1 44.9 %collective-permute-start.44 = (bf16[256,2048]{1,0:T(8,128)(2,1)}, bf16[256,2048]{1,0:T(8,128)(2,1)}, u32[]{:S(2)}, u32[]{:S(2)}) collective-permute-start(bf16[256,2048]{1,0:T(8,128)(2,1)} %add_convert_fusion), channel_id=1, source_target_pairs={{0,2},{1,3},{2,0},{3,1},{4,6},{5,7},{6,4},{7,5},{8,10},{9,11},{10,... | collective-permute-start | bytes 3145736 | tf_op jit(solution)/shard_map/ppermute | solution.py:348
  869.7 44.9 %collective-permute-start.41 = (bf16[256,2048]{1,0:T(8,128)(2,1)}, bf16[256,2048]{1,0:T(8,128)(2,1)}, u32[]{:S(2)}, u32[]{:S(2)}) collective-permute-start(bf16[256,2048]{1,0:T(8,128)(2,1)} %add_convert_fusion.2), channel_id=1, source_target_pairs={{0,1},{1,0},{2,3},{3,2},{4,5},{5,4},{6,7},{7,6},{8,9},{9,8},{10,11... | collective-permute-start | bytes 3145736 | tf_op jit(solution)/shard_map/ppermute | solution.py:348
  893.0 43.9 %collective-permute-start.36 = (bf16[256,2048]{1,0:T(8,128)(2,1)}, bf16[256,2048]{1,0:T(8,128)(2,1)}, u32[]{:S(2)}, u32[]{:S(2)}) collective-permute-start(bf16[256,2048]{1,0:T(8,128)(2,1)} %get-tuple-element.103), channel_id=1, source_target_pairs={{0,1},{1,0},{2,3},{3,2},{4,5},{5,4},{6,7},{7,6},{8,9},{9,8},{10,11... | collective-permute-start | bytes 3145736 | tf_op jit(solution)/shard_map/ppermute | solution.py:348
  899.2 37.8 %collective-permute-start.38 = (bf16[256,2048]{1,0:T(8,128)(2,1)}, bf16[256,2048]{1,0:T(8,128)(2,1)}, u32[]{:S(2)}, u32[]{:S(2)}) collective-permute-start(bf16[256,2048]{1,0:T(8,128)(2,1)} %get-tuple-element.100), channel_id=1, source_target_pairs={{0,2},{1,3},{2,0},{3,1},{4,6},{5,7},{6,4},{7,5},{8,10},{9,11},{10,... | collective-permute-start | bytes 3145736 | tf_op jit(solution)/shard_map/ppermute | solution.py:348
  926.9 6.2 collective-permute-start.45
  933.2 3.7 collective-permute-start.46
  936.9 2.7 collective-permute-start.47
  939.6 3.7 collective-permute-start.48
  943.4 3.7 collective-permute-start.49
  (49 other events, 637.3 us)
Sparse Core Ops, SparseCore 0:
  10.2 67.4 all-gather.5
  79.3 27.7 all-gather.7
  108.7 81.4 all-gather.9
  191.7 80.4 all-gather.11
  273.6 80.5 all-gather.13
  552.5 86.2 reduce-scatter.9
  641.1 87.9 reduce-scatter.7
  731.4 87.9 reduce-scatter.5
  821.8 34.4 reduce-scatter.13
  858.4 68.6 reduce-scatter.11

commit v4 on v3

--- a/solution.py
+++ b/solution.py
@@ -357,30 +357,36 @@
     return (bits, bits[::-1])
 
 
-def gather_tp(halves, size):
+def gather_tp(halves, size, hold=None):
     got = []
     for half, order in zip(halves, bit_orders(size)):
         have = {0: half}
         for bit in order:
             for r in sorted(have):
-                have[r ^ bit] = hop(have[r], bit, size)
+                sent = have[r] if hold is None or not r else after(have[r], hold)
+                have[r ^ bit] = hop(sent, bit, size)
         got.append(have)
-    return jnp.concatenate([got[h][r] for r in range(size) for h in range(2)], axis=0)
-
-
-def scatter_tp(piece, size):
+    return [got[h][r] for r in range(size) for h in range(2)]
+
+
+def rows_of(pieces):
+    return jnp.concatenate(pieces, axis=0)
+
+
+def scatter_tp(piece, size, settle=False):
     out = []
     parts = [piece(r) for r in range(size)]
     own = parts[0].shape[0]
     for h, order in enumerate(bit_orders(size)):
         have = {r: parts[r][h * (own // 2) : (h + 1) * (own // 2)] for r in range(size)}
         for step, bit in enumerate(order[::-1]):
-            last = step == len(order) - 1
             for r in sorted(have, reverse=True):
                 if r & bit:
                     came = hop(have.pop(r), bit, size).astype(F32)
                     total = have[r ^ bit].astype(F32) + came
-                    have[r ^ bit] = total if last else total.astype(BF16)
+                    if r ^ bit or (settle and step < len(order) - 1):
+                        total = lax.optimization_barrier(total.astype(BF16))
+                    have[r ^ bit] = total
         out.append(have[0].astype(F32))
     return out
 
@@ -390,17 +396,15 @@
 
 
 def scatter_vectors(values):
-    axes = ("fsdp", "tp")
-    devices = lax.axis_size("fsdp") * lax.axis_size("tp")
-    index = lax.axis_index("fsdp") * lax.axis_size("tp") + lax.axis_index("tp")
-    bit = devices // 2
-    while bit:
-        pair = values.reshape(values.shape[0], 2, values.shape[1] // 2)
-        mine = (index // bit) % 2
-        kept = lax.dynamic_index_in_dim(pair, mine, axis=1, keepdims=False)
-        sent = lax.dynamic_index_in_dim(pair, 1 - mine, axis=1, keepdims=False)
-        values = kept + lax.ppermute(sent, axes, [(i, i ^ bit) for i in range(devices)])
-        bit //= 2
+    sizes = {axis: lax.axis_size(axis) for axis in ("fsdp", "tp")}
+    values = values.reshape(values.shape[0], sizes["fsdp"], sizes["tp"], -1)
+    for axis, dim in (("tp", 2), ("fsdp", 1)):
+        size, me = sizes[axis], lax.axis_index(axis)
+        total = lax.dynamic_index_in_dim(values, me, axis=dim, keepdims=False)
+        for r in range(1, size):
+            sent = lax.dynamic_index_in_dim(values, me ^ r, axis=dim, keepdims=False)
+            total = total + lax.ppermute(sent, axis, [(i, i ^ r) for i in range(size)])
+        values = total
     return values
 
 
@@ -432,6 +436,9 @@
     up_full = along_fsdp(w_up)
     down_full = along_fsdp(w_down)
 
+    def back_fsdp(term):
+        return lax.psum_scatter(term, "fsdp", scatter_dimension=0, tiled=True).astype(F32)
+
     own_length = lax.dynamic_index_in_dim(lengths, my_slot, keepdims=False)
     places = flip * own + jnp.arange(own, dtype=jnp.int32)
     valid = split_halves((places < own_length).astype(F32)[:, None])
@@ -443,14 +450,17 @@
     x = [half.astype(F32) for half in split_halves(tokens)]
     scale_one = [inverse_rms(v) for v in x]
     normed_one = [v * s for v, s in zip(x, scale_one)]
-    h1 = gather_tp([(n * gain_attn).astype(BF16) for n in normed_one], size)
+    h1_pieces = gather_tp([(n * gain_attn).astype(BF16) for n in normed_one], size)
+    h1_slot = [rows_of(h1_pieces[2 * per_slot * s : 2 * per_slot * (s + 1)]) for s in range(count)]
     grad_rows = [m * g.astype(F32) for m, g in zip(valid, split_halves(out_grad))]
 
-    qkv = matmul(h1, qkv_full)
+    qkv = [matmul(h1_slot[0], qkv_full)]
+    for s in range(1, count):
+        qkv.append(matmul(after(h1_slot[s], qkv[-1]), qkv_full))
     saved = {}
     partial = {}
     for s in reversed(range(count)):
-        saved[s] = attend(qkv, s, infos[s], cosine, sine, own, length)
+        saved[s] = attend(qkv[s], 0, infos[s], cosine, sine, own, length)
         partial[s] = matmul_nt(saved[s][3], out_full).astype(BF16)
 
     def attn_piece(r):
@@ -461,10 +471,9 @@
     middle = [v + a for v, a in zip(x, attn_out)]
     scale_two = [inverse_rms(v) for v in middle]
     normed_two = [v * s for v, s in zip(middle, scale_two)]
-    h2 = gather_tp([(n * gain_mlp).astype(BF16) for n in normed_two], size)
-
-    dm_own = after(jnp.concatenate([g.astype(BF16) for g in grad_rows], axis=0), h2)
-    dm = jnp.concatenate([dm_own] + [hop(dm_own, r, size) for r in range(1, size)], axis=0)
+    h2 = rows_of(gather_tp([(n * gain_mlp).astype(BF16) for n in normed_two], size))
+
+    dm = rows_of(gather_tp([after(g.astype(BF16), h1_slot[-1]) for g in grad_rows], size, h2))
 
     hid, gate_slope, up_slope = gate_up(h2, gate_full, up_full)
     down_term = matmul_tn(dm, hid).astype(BF16)
@@ -472,9 +481,9 @@
     half_group = group // 2
     two = {}
     two[1] = two_nt(grad_gate, grad_up, gate_full, up_full, half_group, half_group)
-    gate_term = matmul_tn(h2, after(grad_gate, two[1])).astype(BF16)
-    two[0] = two_nt(after(grad_gate, gate_term), grad_up, gate_full, up_full, 0, half_group)
-    up_term = matmul_tn(h2, after(grad_up, two[0])).astype(BF16)
+    two[0] = two_nt(after(grad_gate, two[1]), grad_up, gate_full, up_full, 0, half_group)
+    gate_term = matmul_tn(h2, after(grad_gate, two[0])).astype(BF16)
+    up_term = matmul_tn(h2, after(grad_up, gate_term)).astype(BF16)
     mlp = matmul_nt(after(hid, up_term), down_full).astype(BF16)
 
     def two_piece(r):
@@ -488,9 +497,12 @@
         g + s * (i - n * jnp.mean(i * n, axis=-1, keepdims=True))
         for g, s, i, n in zip(grad_rows, scale_two, inner_two, normed_two)
     ]
-    grad_attn = gather_tp([after(g.astype(BF16), gate_term, up_term) for g in grad_middle], size)
-    mlp, grad_attn = lax.optimization_barrier((mlp, grad_attn))
-    mlp_out = scatter_tp(lambda r: mlp[r * own : (r + 1) * own], size)
+    grad_attn = rows_of(gather_tp([after(g.astype(BF16), gate_term, up_term) for g in grad_middle], size))
+    down_grad = back_fsdp(down_term)
+    gate_grad = back_fsdp(gate_term)
+    up_grad = back_fsdp(up_term)
+    mlp, grad_attn, down_grad, gate_grad = lax.optimization_barrier((mlp, grad_attn, down_grad, gate_grad))
+    mlp_out = scatter_tp(lambda r: mlp[r * own : (r + 1) * own], size, settle=True)
     output = jnp.concatenate(
         [(m * (v + o)).astype(BF16) for m, v, o in zip(valid, middle, mlp_out)], axis=0
     )
@@ -510,8 +522,8 @@
             mixed = after(jnp.concatenate([saved[i][3] for i in range(count)], axis=0), last)
             last = out_term = matmul_tn(grad_attn, mixed).astype(BF16)
     grad_all = jnp.concatenate([grad_qkv[s] for s in range(count)], axis=0)
-    qkv_term = matmul_tn(h1, grad_all).astype(BF16)
-    partial_one[0] = matmul_nt(after(grad_qkv[0], qkv_term), qkv_full).astype(BF16)
+    qkv_term = matmul_tn(rows_of(h1_slot), grad_all).astype(BF16)
+    partial_one[0] = matmul_nt(after(grad_qkv[0], qkv_term, up_grad), qkv_full).astype(BF16)
 
     def one_piece(r):
         s, inside = divmod(r, per_slot)
@@ -528,15 +540,9 @@
         axis=0,
     )
 
-    def back_fsdp(term):
-        return lax.psum_scatter(term, "fsdp", scatter_dimension=0, tiled=True).astype(F32)
-
-    down_grad = back_fsdp(down_term)
-    gate_grad = back_fsdp(gate_term)
-    up_grad = back_fsdp(up_term)
     out_proj_grad = back_fsdp(out_term)
     qkv_grad = back_fsdp(qkv_term)
-    gains = scatter_vectors(after(jnp.stack([gain_attn_term, gain_mlp_term]), down_grad, gate_grad, up_grad))
+    gains = scatter_vectors(jnp.stack([gain_attn_term, gain_mlp_term]))
     return (
         output,
         input_grad,

time: 960 us -> 992 us (1.033)
  matrix products: 166 us -> 185 us
  starting transfers between devices: 50.5 us -> 69.4 us
    ppermute x5 -> x10, starting transfers between devices: 1.92 us -> 13.6 us  [scatter_vectors(): total = total + lax.ppermute(sent, axis, [(i, i ^ r) for i in range(size)])]
    unnamed x129 -> x123, local copies, waits for them, and re-layouts: 23.5 us -> 33.8 us
    ppermute x45 -> x48, waiting for transfers between devices: 372 us -> 363 us  [hop(): return lax.ppermute(value, 'tp', [(i, i ^ bit) for i in range(size)])]
    dot_general x2 -> x3, matrix products: 25.2 us -> 33.4 us  [matmul(): return jnp.dot(left, right, preferred_element_type=F32)]
    ppermute x45 -> x48, starting transfers between devices: 48.2 us -> 55.3 us  [hop(): return lax.ppermute(value, 'tp', [(i, i ^ bit) for i in range(size)])]
  transfers between devices with their start and end apart: 60 -> 68, of which waited for: 27 -> 32; matrix products, arithmetic and copies ran while one was open for 23% -> 27% of each run, Pallas kernels for 15% -> 14%
where the time goes in v4:
time: 992 us; the launch traced here: 987 us
  waiting for transfers between devices  369 us (37%)
  Pallas kernels  232 us (23%)
  matrix products  185 us (19%)
  starting transfers between devices  69.4 us (7%)
  other arithmetic  63.8 us (6%)
  local copies, waits for them, and re-layouts  51.3 us (5%)
  between operations  15.4 us (2%)
    ppermute x48, waiting for transfers between devices, hop(): return lax.ppermute(value, 'tp', [(i, i ^ bit) for i in range(size)])  363 us
    dot_general x5, matrix products, matmul_tn(): lax.dot_general(left, right, (((0,), (0,)), ((), ())), preferred_element_...  100 us
    pallas_call x2, Pallas kernels, two_nt(): pl.pallas_call(two_nt_kernel, out_shape=jax.ShapeDtypeStruct((rows, width...  55.5 us
    ppermute x48, starting transfers between devices, hop(): return lax.ppermute(value, 'tp', [(i, i ^ bit) for i in range(size)])  55.3 us
    pallas_call x2, Pallas kernels, attend_back(): pl.pallas_call(functools.partial(attend_back_kernel, own), out_shape=jax....  51.8 us
    dot_general x5, matrix products, matmul_nt(): lax.dot_general(left, right, (((1,), (1,)), ((), ())), preferred_element_...  51.4 us
    pallas_call x1, Pallas kernels, gate_up(): pl.pallas_call(gate_up_kernel, out_shape=[jax.ShapeDtypeStruct((rows, wid...  48.4 us
    pallas_call x2, Pallas kernels, attend(): pl.pallas_call(functools.partial(attend_kernel, own), out_shape=[wide] *...  42.3 us
  transfers between devices with their start and end apart: 68, of which 32 were waited for; matrix products, arithmetic and copies ran while one was open for 27% of the time, Pallas kernels for 14%

profile of v4, /device:TPU:0, one launch (start us, length us, event | category | flops | bytes accessed | tf_op | source)
XLA Modules:
  0.0 986.6 jit_solution(10877471946260558640)
XLA Ops:
  13.7 3.0 collective-permute-start
  26.2 14.8 %collective-permute-done = bf16[256,2048]{1,0:T(8,128)(2,1)} collective-permute-done((bf16[256,2048]{1,0:T(8,128)(2,1)}, bf16[256,2048]{1,0:T(8,128)(2,1)}, u32[]{:S(2)}, u32[]{:S(2)}) %collective-permute-start) | collective-permute-done | bytes 1048608 | tf_op jit(solution)/shard_map/ppermute | solution.py:348
  46.9 16.6 %collective-permute-done.1 = bf16[256,2048]{1,0:T(8,128)(2,1)} collective-permute-done((bf16[256,2048]{1,0:T(8,128)(2,1)}, bf16[256,2048]{1,0:T(8,128)(2,1)}, u32[]{:S(2)}, u32[]{:S(2)}) %collective-permute-start.1) | collective-permute-done | bytes 1048608 | tf_op jit(solution)/shard_map/ppermute | solution.py:348
  67.2 2.9 constant_dynamic-update-slice_fusion.31
  71.7 16.5 %collective-permute-done.4 = bf16[256,2048]{1,0:T(8,128)(2,1)S(1)} collective-permute-done((bf16[256,2048]{1,0:T(8,128)(2,1)}, bf16[256,2048]{1,0:T(8,128)(2,1)S(1)}, u32[]{:S(2)}, u32[]{:S(2)}) %collective-permute-start.4) | collective-permute-done | bytes 1048608 | tf_op jit(solution)/shard_map/ppermute | solution.py:348
  91.2 13.5 %fusion.3.q_ref.k_ref.v_ref = f32[1024,1536]{1,0:T(8,128)} fusion(bf16[2048,1536]{1,0:T(8,128)(2,1)} %all-gather.6.cloned.1.call-done, bf16[256,2048]{1,0:T(8,128)(2,1)} %collective-permute-done.1, bf16[256,2048]{1,0:T(8,128)(2,1)} %collective-permute-done, bf16[256,2048]{1,0:T(8,128)(2,1)} %get-tuple-element.94, bf16[256,2048]{1,0:T(8,128)(2,1)} %get-tuple-element.96), kind=kOutput, calls=%fused_computation.8 | convolution fusion | flops 6459228160 | bytes 16777216 | tf_op jit(solution)/shard_map/dot_general | solution.py:22
  104.7 10.1 %fusion.54.q_ref.k_ref.v_ref = f32[1024,1536]{1,0:T(8,128)} fusion(bf16[1024,2048]{1,0:T(8,128)(2,1)} %get-tuple-element.46, bf16[2048,1536]{1,0:T(8,128)(2,1)S(1)} %copy-done.43), kind=kOutput, calls=%fused_computation.170 | convolution fusion | flops 6442450944 | bytes 16777216 | tf_op jit(solution)/shard_map/dot_general | solution.py:22
  114.8 23.7 %attend.3 = (bf16[1024,512]{1,0:T(8,128)(2,1)}, bf16[1024,512]{1,0:T(8,128)(2,1)}, bf16[1024,512]{1,0:T(8,128)(2,1)}, bf16[1024,512]{1,0:T(8,128)(2,1)}, f32[4,8,1024]{2,1,0:T(8,128)}) custom-call(s32[2]{0:T(128)} %pad_add_fusion.1.info, f32[1024,1536]{1,0:T(8,128)} %fusion.54.q_ref.k_ref.v_ref, f32[1024,1536]{1,0:T(8,128)} %fusion.54.q_ref.k_ref.v_ref, ...), custom_call_target="tpu_custom_call" | custom-call | flops 4294967296 | bytes 10485760 | tf_op jit(solution)/shard_map/attend/pallas_call | solution.py:134
  138.5 4.3 convolution_convert_fusion.7
  147.4 18.6 %attend.2 = (bf16[1024,512]{1,0:T(8,128)(2,1)}, bf16[1024,512]{1,0:T(8,128)(2,1)}, bf16[1024,512]{1,0:T(8,128)(2,1)}, bf16[1024,512]{1,0:T(8,128)(2,1)}, f32[4,8,1024]{2,1,0:T(8,128)}) custom-call(s32[2]{0:T(128)} %pad_add_fusion.info, f32[1024,1536]{1,0:T(8,128)} %fusion.3.q_ref.k_ref.v_ref, f32[1024,1536]{1,0:T(8,128)} %fusion.3.q_ref.k_ref.v_ref, ...), custom_call_target="tpu_custom_call" | custom-call | flops 4294967296 | bytes 10485760 | tf_op jit(solution)/shard_map/attend/pallas_call | solution.py:134
  166.1 7.3 collective-permute-start.6
  173.4 4.3 convolution_convert_fusion.8
  187.5 10.1 %collective-permute-done.6 = bf16[256,2048]{1,0:T(8,128)(2,1)S(1)} collective-permute-done((bf16[256,2048]{1,0:T(8,128)(2,1)}, bf16[256,2048]{1,0:T(8,128)(2,1)S(1)}, u32[]{:S(2)}, u32[]{:S(2)}) %collective-permute-start.6) | collective-permute-done | bytes 1048608 | tf_op jit(solution)/shard_map/ppermute | solution.py:348
  199.6 4.3 collective-permute-done.9
  205.7 14.4 %collective-permute-done.11 = bf16[256,2048]{1,0:T(8,128)(2,1)S(1)} collective-permute-done((bf16[256,2048]{1,0:T(8,128)(2,1)S(1)}, bf16[256,2048]{1,0:T(8,128)(2,1)S(1)}, u32[]{:S(2)}, u32[]{:S(2)}) %collective-permute-start.11) | collective-permute-done | bytes 1048608 | tf_op jit(solution)/shard_map/ppermute | solution.py:348
  222.1 4.3 collective-permute-done.8
  230.5 18.3 %collective-permute-done.18 = bf16[256,2048]{1,0:T(8,128)(2,1)S(1)} collective-permute-done((bf16[256,2048]{1,0:T(8,128)(2,1)S(1)}, bf16[256,2048]{1,0:T(8,128)(2,1)S(1)}, u32[]{:S(2)}, u32[]{:S(2)}) %collective-permute-start.18) | collective-permute-done | bytes 1048608 | tf_op jit(solution)/shard_map/ppermute | solution.py:348
  250.0 21.3 %collective-permute-done.19 = bf16[256,2048]{1,0:T(8,128)(2,1)S(1)} collective-permute-done((bf16[256,2048]{1,0:T(8,128)(2,1)S(1)}, bf16[256,2048]{1,0:T(8,128)(2,1)S(1)}, u32[]{:S(2)}, u32[]{:S(2)}) %collective-permute-start.19) | collective-permute-done | bytes 1048608 | tf_op jit(solution)/shard_map/ppermute | solution.py:348
  276.5 17.4 %collective-permute-done.12 = bf16[256,2048]{1,0:T(8,128)(2,1)S(1)} collective-permute-done((bf16[256,2048]{1,0:T(8,128)(2,1)S(1)}, bf16[256,2048]{1,0:T(8,128)(2,1)S(1)}, u32[]{:S(2)}, u32[]{:S(2)}) %collective-permute-start.12) | collective-permute-done | bytes 1048608 | tf_op jit(solution)/shard_map/ppermute | solution.py:348
  298.0 18.3 %collective-permute-done.13 = bf16[256,2048]{1,0:T(8,128)(2,1)S(1)} collective-permute-done((bf16[256,2048]{1,0:T(8,128)(2,1)S(1)}, bf16[256,2048]{1,0:T(8,128)(2,1)S(1)}, u32[]{:S(2)}, u32[]{:S(2)}) %collective-permute-start.13) | collective-permute-done | bytes 1048608 | tf_op jit(solution)/shard_map/ppermute | solution.py:348
  316.5 14.6 %collective-permute-done.16 = bf16[256,2048]{1,0:T(8,128)(2,1)S(1)} collective-permute-done((bf16[256,2048]{1,0:T(8,128)(2,1)S(1)}, bf16[256,2048]{1,0:T(8,128)(2,1)S(1)}, u32[]{:S(2)}, u32[]{:S(2)}) %collective-permute-start.16) | collective-permute-done | bytes 1048608 | tf_op jit(solution)/shard_map/ppermute | solution.py:348
  331.2 4.5 collective-permute-done.17
  335.8 3.3 copy-done.25
  342.4 48.4 %gate_up.1 = (bf16[2048,2048]{1,0:T(8,128)(2,1)}, bf16[2048,2048]{1,0:T(8,128)(2,1)}, bf16[2048,2048]{1,0:T(8,128)(2,1)}) custom-call(bf16[2048,2048]{1,0:T(8,128)(2,1)} %copy-done.25, bf16[2048,2048]{1,0:T(8,128)(2,1)} %all-gather.10.cloned.1.call-done.g_ref.wa_ref, bf16[2048,2048]{1,0:T(8,128)(2,1)} %all-gather.12.cloned.1.call-done.u_ref.wb_ref), custom_call_target="tpu_custom_call" | custom-call | flops 34359738368 | bytes 50331648 | tf_op jit(solution)/shard_map/gate_up/pallas_call | solution.py:282
  392.9 23.8 %convolution_convert_fusion.3 = bf16[2048,2048]{1,0:T(8,128)(2,1)} fusion(bf16[2048,2048]{1,0:T(8,128)(2,1)} %constant_dynamic-update-slice_fusion.12.g_ref, bf16[2048,2048]{1,0:T(8,128)(2,1)} %get-tuple-element.61), kind=kOutput, calls=%fused_computation.3 | convolution fusion | flops 17184063488 | bytes 25165824 | tf_op jit(solution)/shard_map/dot_general | solution.py:30
  416.6 34.1 %hidden_back.1 = (bf16[2048,2048]{1,0:T(8,128)(2,1)}, bf16[2048,2048]{1,0:T(8,128)(2,1)}) custom-call(bf16[2048,2048]{1,0:T(8,128)(2,1)} %constant_dynamic-update-slice_fusion.12.g_ref, bf16[2048,2048]{1,0:T(8,128)(2,1)} %all-gather.14.cloned.1.call-done.w_ref, bf16[2048,2048]{1,0:T(8,128)(2,1)} %get-tuple-element.54.gate_slope, ...), custom_call_target="tpu_custom_call" | custom-call | flops 17179869184 | bytes 50331648 | tf_op jit(solution)/shard_map/hidden_back/pallas_call | solution.py:306
  450.7 27.7 %two_nt.2 = bf16[1024,2048]{1,0:T(8,128)(2,1)} custom-call(bf16[2048,2048]{1,0:T(8,128)(2,1)} %get-tuple-element.59.a_ref, bf16[2048,2048]{1,0:T(8,128)(2,1)} %get-tuple-element.60.b_ref, bf16[2048,2048]{1,0:T(8,128)(2,1)} %all-gather.10.cloned.1.call-done.g_ref.wa_ref, bf16[2048,2048]{1,0:T(8,128)(2,1)} %all-gather.12.cloned.1.call-done.u_ref.wb_ref), custom_call_target="tpu_custom_call" | custom-call | flops 17179869184 | bytes 29360128 | tf_op jit(solution)/shard_map/two_nt/pallas_call | solution.py:334
  478.5 27.7 %two_nt.3 = bf16[1024,2048]{1,0:T(8,128)(2,1)} custom-call(bf16[2048,2048]{1,0:T(8,128)(2,1)} %get-tuple-element.59.a_ref, bf16[2048,2048]{1,0:T(8,128)(2,1)} %get-tuple-element.60.b_ref, bf16[2048,2048]{1,0:T(8,128)(2,1)} %all-gather.10.cloned.1.call-done.g_ref.wa_ref, bf16[2048,2048]{1,0:T(8,128)(2,1)} %all-gather.12.cloned.1.call-done.u_ref.wb_ref), custom_call_target="tpu_custom_call" | custom-call | flops 17179869184 | bytes 29360128 | tf_op jit(solution)/shard_map/two_nt/pallas_call | solution.py:334
  506.2 23.9 %convolution_convert_fusion.2 = bf16[2048,2048]{1,0:T(8,128)(2,1)} fusion(bf16[2048,2048]{1,0:T(8,128)(2,1)} %copy-done.25, bf16[2048,2048]{1,0:T(8,128)(2,1)} %get-tuple-element.59.a_ref), kind=kOutput, calls=%fused_computation.2 | convolution fusion | flops 17184063488 | bytes 25165824 | tf_op jit(solution)/shard_map/dot_general | solution.py:30
  531.0 24.5 %convolution_convert_fusion.1 = bf16[2048,2048]{1,0:T(8,128)(2,1)} fusion(bf16[2048,2048]{1,0:T(8,128)(2,1)} %copy-done.25, bf16[2048,2048]{1,0:T(8,128)(2,1)} %get-tuple-element.60.b_ref), kind=kOutput, calls=%fused_computation.1 | convolution fusion | flops 17184063488 | bytes 25165824 | tf_op jit(solution)/shard_map/dot_general | solution.py:30
  562.1 21.8 %collective-permute-done.28 = bf16[256,2048]{1,0:T(8,128)(2,1)S(1)} collective-permute-done((bf16[256,2048]{1,0:T(8,128)(2,1)S(1)}, bf16[256,2048]{1,0:T(8,128)(2,1)S(1)}, u32[]{:S(2)}, u32[]{:S(2)}) %collective-permute-start.28) | collective-permute-done | bytes 1048608 | tf_op jit(solution)/shard_map/ppermute | solution.py:348
  586.6 19.8 %collective-permute-done.27 = bf16[256,2048]{1,0:T(8,128)(2,1)S(1)} collective-permute-done((bf16[256,2048]{1,0:T(8,128)(2,1)S(1)}, bf16[256,2048]{1,0:T(8,128)(2,1)S(1)}, u32[]{:S(2)}, u32[]{:S(2)}) %collective-permute-start.27) | collective-permute-done | bytes 1048608 | tf_op jit(solution)/shard_map/ppermute | solution.py:348
  606.5 18.9 %collective-permute-done.29 = bf16[256,2048]{1,0:T(8,128)(2,1)S(1)} collective-permute-done((bf16[256,2048]{1,0:T(8,128)(2,1)S(1)}, bf16[256,2048]{1,0:T(8,128)(2,1)S(1)}, u32[]{:S(2)}, u32[]{:S(2)}) %collective-permute-start.29) | collective-permute-done | bytes 1048608 | tf_op jit(solution)/shard_map/ppermute | solution.py:348
  625.5 2.8 multiply_reduce_fusion.1
  628.3 3.7 fusion.45
  636.1 21.7 %convolution_convert_fusion = bf16[2048,2048]{1,0:T(8,128)(2,1)} fusion(bf16[2048,2048]{1,0:T(8,128)(2,1)} %get-tuple-element.61, bf16[2048,2048]{1,0:T(8,128)(2,1)S(1)} %bitcast.57), kind=kOutput, calls=%fused_computation | convolution fusion | flops 17184063488 | bytes 25165824 | tf_op jit(solution)/shard_map/dot_general | solution.py:26
  660.1 22.1 %collective-permute-done.33 = bf16[256,2048]{1,0:T(8,128)(2,1)S(1)} collective-permute-done((bf16[256,2048]{1,0:T(8,128)(2,1)S(1)}, bf16[256,2048]{1,0:T(8,128)(2,1)S(1)}, u32[]{:S(2)}, u32[]{:S(2)}) %collective-permute-start.33) | collective-permute-done | bytes 1048608 | tf_op jit(solution)/shard_map/ppermute | solution.py:348
  686.8 12.9 %collective-permute-done.34 = bf16[256,2048]{1,0:T(8,128)(2,1)S(1)} collective-permute-done((bf16[256,2048]{1,0:T(8,128)(2,1)S(1)}, bf16[256,2048]{1,0:T(8,128)(2,1)S(1)}, u32[]{:S(2)}, u32[]{:S(2)}) %collective-permute-start.34) | collective-permute-done | bytes 1048608 | tf_op jit(solution)/shard_map/ppermute | solution.py:348
  701.9 2.8 convert_element_type.299
  704.7 2.6 reduce-scatter.6.cloned.1.call-done
  707.3 2.8 convert_element_type.298
  710.1 9.9 %convolution_convert_fusion.10.g_ref = bf16[2048,512]{1,0:T(8,128)(2,1)} fusion(bf16[2048,2048]{1,0:T(8,128)(2,1)} %constant_dynamic-update-slice_fusion.20, bf16[2048,512]{1,0:T(8,128)(2,1)} %all-gather.8.cloned.1.call-done), kind=kOutput, calls=%fused_computation.35 | convolution fusion | flops 4296015872 | bytes 12582912 | tf_op jit(solution)/shard_map/dot_general | solution.py:22
  720.0 29.0 %attend_back.2 = bf16[1024,1536]{1,0:T(8,128)(2,1)} custom-call(s32[2]{0:T(128)} %pad_add_fusion.1.info, bf16[1024,512]{1,0:T(8,128)(2,1)} %get-tuple-element.67.q_ref, bf16[1024,512]{1,0:T(8,128)(2,1)} %get-tuple-element.68.k_ref, bf16[1024,512]{1,0:T(8,128)(2,1)} %get-tuple-element.69.v_ref, bf16[1024,512]{1,0:T(8,128)(2,1)} %get-tuple-element.47.a_ref, ...), custom_call_target="tpu_custom_call" | custom-call | flops 10737418240 | bytes 10485760 | tf_op jit(solution)/shard_map/attend_back/pallas_call | solution.py:241
  749.0 11.2 %convolution_convert_fusion.6 = bf16[1024,2048]{1,0:T(8,128)(2,1)} fusion(bf16[1024,1536]{1,0:T(8,128)(2,1)} %attend_back.2, bf16[2048,1536]{1,0:T(8,128)(2,1)} %all-gather.6.cloned.1.call-done), kind=kOutput, calls=%fused_computation.17 | convolution fusion | flops 6444548096 | bytes 13631488 | tf_op jit(solution)/shard_map/dot_general | solution.py:26
  760.2 9.5 convolution_convert_fusion.9
  769.8 22.8 %attend_back.3 = bf16[1024,1536]{1,0:T(8,128)(2,1)} custom-call(s32[2]{0:T(128)} %pad_add_fusion.info, bf16[1024,512]{1,0:T(8,128)(2,1)} %get-tuple-element.72.q_ref, bf16[1024,512]{1,0:T(8,128)(2,1)} %get-tuple-element.73.k_ref, bf16[1024,512]{1,0:T(8,128)(2,1)} %get-tuple-element.74.v_ref, bf16[1024,512]{1,0:T(8,128)(2,1)} %get-tuple-element.45.a_ref, ...), custom_call_target="tpu_custom_call" | custom-call | flops 10737418240 | bytes 10485760 | tf_op jit(solution)/shard_map/attend_back/pallas_call | solution.py:241
  792.6 18.7 %convolution_convert_fusion.4 = bf16[2048,1536]{1,0:T(8,128)(2,1)} fusion(bf16[2048,2048]{1,0:T(8,128)(2,1)} %get-tuple-element.134, bf16[1024,1536]{1,0:T(8,128)(2,1)S(1)} %copy-done.44, bf16[1024,1536]{1,0:T(8,128)(2,1)} %attend_back.3), kind=kOutput, calls=%fused_computation.4 | convolution fusion | flops 12900630528 | bytes 20971520 | tf_op jit(solution)/shard_map/dot_general | solution.py:30
  811.3 3.2 fusion.48
  815.9 2.9 convert_element_type.322
  820.3 9.8 convolution_convert_fusion.5
  838.9 2.6 add_convert_fusion
  844.1 20.4 %collective-permute-done.36 = bf16[256,2048]{1,0:T(8,128)(2,1)S(1)} collective-permute-done((bf16[256,2048]{1,0:T(8,128)(2,1)S(1)}, bf16[256,2048]{1,0:T(8,128)(2,1)S(1)}, u32[]{:S(2)}, u32[]{:S(2)}) %collective-permute-start.36) | collective-permute-done | bytes 1048608 | tf_op jit(solution)/shard_map/ppermute | solution.py:348
  867.0 20.1 %collective-permute-done.37 = bf16[256,2048]{1,0:T(8,128)(2,1)} collective-permute-done((bf16[256,2048]{1,0:T(8,128)(2,1)S(1)}, bf16[256,2048]{1,0:T(8,128)(2,1)}, u32[]{:S(2)}, u32[]{:S(2)}) %collective-permute-start.37) | collective-permute-done | bytes 1048608 | tf_op jit(solution)/shard_map/ppermute | solution.py:348
  889.3 6.9 add_convert_fusion.5
  897.7 8.2 collective-permute-done.45
  906.8 2.7 collective-permute-done.42
  909.5 22.6 %collective-permute-done.47 = bf16[256,2048]{1,0:T(8,128)(2,1)} collective-permute-done((bf16[256,2048]{1,0:T(8,128)(2,1)}, bf16[256,2048]{1,0:T(8,128)(2,1)}, u32[]{:S(2)}, u32[]{:S(2)}) %collective-permute-start.47) | collective-permute-done | bytes 1048608 | tf_op jit(solution)/shard_map/ppermute | solution.py:348
  932.1 3.2 fusion.25
  939.1 11.9 %collective-permute-done.38 = bf16[256,2048]{1,0:T(8,128)(2,1)} collective-permute-done((bf16[256,2048]{1,0:T(8,128)(2,1)}, bf16[256,2048]{1,0:T(8,128)(2,1)}, u32[]{:S(2)}, u32[]{:S(2)}) %collective-permute-start.38) | collective-permute-done | bytes 1048608 | tf_op jit(solution)/shard_map/ppermute | solution.py:348
  951.0 2.8 multiply_convert_fusion.1
  956.8 4.1 fusion.24
  962.4 2.5 collective-permute-start.51
  966.3 3.0 collective-permute-start.55
  969.3 3.2 collective-permute-start.57
  (293 shorter events, 131.2 us)
Async XLA Ops:
  7.2 84.0 %all-gather.6.cloned.1.call-start = ((), (), s32[]{:S(2)}) async-start(), calls=%async_computation.5 | async-start | bytes 7077888 | tf_op jit(solution)/shard_map/all_gather | solution.py:431
  9.4 129.1 %all-gather.8.cloned.1.call-start = ((), (), s32[]{:S(2)}) async-start(), calls=%async_computation.6 | async-start | bytes 2359296 | tf_op jit(solution)/shard_map/all_gather | solution.py:431
  10.2 332.2 %all-gather.10.cloned.1.call-start = ((), (), s32[]{:S(2)}) async-start(), calls=%async_computation.7 | async-start | bytes 9437184 | tf_op jit(solution)/shard_map/all_gather | solution.py:431
  10.9 331.5 %all-gather.12.cloned.1.call-start = ((), (), s32[]{:S(2)}) async-start(), calls=%async_computation.8 | async-start | bytes 9437184 | tf_op jit(solution)/shard_map/all_gather | solution.py:431
  11.5 405.1 %all-gather.14.cloned.1.call-start = ((), (), s32[]{:S(2)}) async-start(), calls=%async_computation.9 | async-start | bytes 9437184 | tf_op jit(solution)/shard_map/all_gather | solution.py:431
  13.7 27.3 %collective-permute-start = (bf16[256,2048]{1,0:T(8,128)(2,1)}, bf16[256,2048]{1,0:T(8,128)(2,1)}, u32[]{:S(2)}, u32[]{:S(2)}) collective-permute-start(bf16[256,2048]{1,0:T(8,128)(2,1)} %get-tuple-element.96), channel_id=1, source_target_pairs={{0,1},{1,0},{2,3},{3,2},{4,5},{5,4},{6,7},{7,6},{8,9},{9,8},{10,11... | collective-permute-start | bytes 3145736 | tf_op jit(solution)/shard_map/ppermute | solution.py:348
  18.3 26.2 %collective-permute-start.3 = (bf16[256,2048]{1,0:T(8,128)(2,1)}, bf16[256,2048]{1,0:T(8,128)(2,1)S(1)}, u32[]{:S(2)}, u32[]{:S(2)}) collective-permute-start(bf16[256,2048]{1,0:T(8,128)(2,1)} %get-tuple-element.94), channel_id=1, source_target_pairs={{0,2},{1,3},{2,0},{3,1},{4,6},{5,7},{6,4},{7,5},{8,10},{9,11},{10,... | collective-permute-start | bytes 3145736 | tf_op jit(solution)/shard_map/ppermute | solution.py:348
  19.9 43.6 %collective-permute-start.1 = (bf16[256,2048]{1,0:T(8,128)(2,1)}, bf16[256,2048]{1,0:T(8,128)(2,1)}, u32[]{:S(2)}, u32[]{:S(2)}) collective-permute-start(bf16[256,2048]{1,0:T(8,128)(2,1)} %get-tuple-element.94), channel_id=1, source_target_pairs={{0,1},{1,0},{2,3},{3,2},{4,5},{5,4},{6,7},{7,6},{8,9},{9,8},{10,11... | collective-permute-start | bytes 3145736 | tf_op jit(solution)/shard_map/ppermute | solution.py:348
  20.4 46.8 %collective-permute-start.2 = (bf16[256,2048]{1,0:T(8,128)(2,1)}, bf16[256,2048]{1,0:T(8,128)(2,1)}, u32[]{:S(2)}, u32[]{:S(2)}) collective-permute-start(bf16[256,2048]{1,0:T(8,128)(2,1)} %get-tuple-element.96), channel_id=1, source_target_pairs={{0,2},{1,3},{2,0},{3,1},{4,6},{5,7},{6,4},{7,5},{8,10},{9,11},{10,... | collective-permute-start | bytes 3145736 | tf_op jit(solution)/shard_map/ppermute | solution.py:348
  41.0 47.1 %collective-permute-start.4 = (bf16[256,2048]{1,0:T(8,128)(2,1)}, bf16[256,2048]{1,0:T(8,128)(2,1)S(1)}, u32[]{:S(2)}, u32[]{:S(2)}) collective-permute-start(bf16[256,2048]{1,0:T(8,128)(2,1)} %collective-permute-done), channel_id=1, source_target_pairs={{0,2},{1,3},{2,0},{3,1},{4,6},{5,7},{6,4},{7,5},{8,10},{9,11},{10,... | collective-permute-start | bytes 3145736 | tf_op jit(solution)/shard_map/ppermute | solution.py:348
  44.6 45.1 %collective-permute-start.5 = (bf16[256,2048]{1,0:T(8,128)(2,1)S(1)}, bf16[256,2048]{1,0:T(8,128)(2,1)S(1)}, u32[]{:S(2)}, u32[]{:S(2)}) collective-permute-start(bf16[256,2048]{1,0:T(8,128)(2,1)S(1)} %collective-permute-done.3), channel_id=1, source_target_pairs={{0,1},{1,0},{2,3},{3,2},{4,5},{5,4},{6,7},{7,6},{8,9},{9,8},{10,11... | collective-permute-start | bytes 3145736 | tf_op jit(solution)/shard_map/ppermute | solution.py:348
  145.9 33.8 %collective-permute-start.10 = (bf16[256,2048]{1,0:T(8,128)(2,1)}, bf16[256,2048]{1,0:T(8,128)(2,1)S(1)}, u32[]{:S(2)}, u32[]{:S(2)}) collective-permute-start(bf16[256,2048]{1,0:T(8,128)(2,1)} %get-tuple-element.130), channel_id=1, source_target_pairs={{0,1},{1,0},{2,3},{3,2},{4,5},{5,4},{6,7},{7,6},{8,9},{9,8},{10,11... | collective-permute-start | bytes 3145736 | tf_op jit(solution)/shard_map/ppermute | solution.py:348
  146.2 555.7 %reduce-scatter.8.cloned.1.call-start = ((), (), s32[]{:S(2)}) async-start(), calls=%async_computation.11 | async-start | bytes 9437184 | tf_op jit(solution)/shard_map/reduce_scatter | solution.py:440
  147.4 34.0 %collective-permute-start.7 = (bf16[256,2048]{1,0:T(8,128)(2,1)}, bf16[256,2048]{1,0:T(8,128)(2,1)}, u32[]{:S(2)}, u32[]{:S(2)}) collective-permute-start(bf16[256,2048]{1,0:T(8,128)(2,1)} %get-tuple-element.131), channel_id=1, source_target_pairs={{0,2},{1,3},{2,0},{3,1},{4,6},{5,7},{6,4},{7,5},{8,10},{9,11},{10,... | collective-permute-start | bytes 3145736 | tf_op jit(solution)/shard_map/ppermute | solution.py:348
  166.1 31.5 %collective-permute-start.6 = (bf16[256,2048]{1,0:T(8,128)(2,1)}, bf16[256,2048]{1,0:T(8,128)(2,1)S(1)}, u32[]{:S(2)}, u32[]{:S(2)}) collective-permute-start(bf16[256,2048]{1,0:T(8,128)(2,1)} %get-tuple-element.129), channel_id=1, source_target_pairs={{0,2},{1,3},{2,0},{3,1},{4,6},{5,7},{6,4},{7,5},{8,10},{9,11},{10,... | collective-permute-start | bytes 3145736 | tf_op jit(solution)/shard_map/ppermute | solution.py:348
  177.8 26.1 %collective-permute-start.9 = (bf16[256,2048]{1,0:T(8,128)(2,1)S(1)}, bf16[256,2048]{1,0:T(8,128)(2,1)S(1)}, u32[]{:S(2)}, u32[]{:S(2)}) collective-permute-start(bf16[256,2048]{1,0:T(8,128)(2,1)S(1)} %slice.227), channel_id=1, source_target_pairs={{0,1},{1,0},{2,3},{3,2},{4,5},{5,4},{6,7},{7,6},{8,9},{9,8},{10,11... | collective-permute-start | bytes 3145736 | tf_op jit(solution)/shard_map/ppermute | solution.py:348
  181.3 38.8 %collective-permute-start.11 = (bf16[256,2048]{1,0:T(8,128)(2,1)S(1)}, bf16[256,2048]{1,0:T(8,128)(2,1)S(1)}, u32[]{:S(2)}, u32[]{:S(2)}) collective-permute-start(bf16[256,2048]{1,0:T(8,128)(2,1)S(1)} %add_convert_fusion.8), channel_id=1, source_target_pairs={{0,2},{1,3},{2,0},{3,1},{4,6},{5,7},{6,4},{7,5},{8,10},{9,11},{10,... | collective-permute-start | bytes 3145736 | tf_op jit(solution)/shard_map/ppermute | solution.py:348
  183.1 43.3 %collective-permute-start.8 = (bf16[256,2048]{1,0:T(8,128)(2,1)S(1)}, bf16[256,2048]{1,0:T(8,128)(2,1)S(1)}, u32[]{:S(2)}, u32[]{:S(2)}) collective-permute-start(bf16[256,2048]{1,0:T(8,128)(2,1)S(1)} %add_convert_fusion.9), channel_id=1, source_target_pairs={{0,1},{1,0},{2,3},{3,2},{4,5},{5,4},{6,7},{7,6},{8,9},{9,8},{10,11... | collective-permute-start | bytes 3145736 | tf_op jit(solution)/shard_map/ppermute | solution.py:348
  184.7 64.2 %collective-permute-start.18 = (bf16[256,2048]{1,0:T(8,128)(2,1)S(1)}, bf16[256,2048]{1,0:T(8,128)(2,1)S(1)}, u32[]{:S(2)}, u32[]{:S(2)}) collective-permute-start(bf16[256,2048]{1,0:T(8,128)(2,1)S(1)} %get-tuple-element.49), channel_id=1, source_target_pairs={{0,1},{1,0},{2,3},{3,2},{4,5},{5,4},{6,7},{7,6},{8,9},{9,8},{10,11... | collective-permute-start | bytes 3145736 | tf_op jit(solution)/shard_map/ppermute | solution.py:348
  197.6 96.2 %collective-permute-start.21 = (bf16[256,2048]{1,0:T(8,128)(2,1)S(1)}, bf16[256,2048]{1,0:T(8,128)(2,1)}, u32[]{:S(2)}, u32[]{:S(2)}) collective-permute-start(bf16[256,2048]{1,0:T(8,128)(2,1)S(1)} %get-tuple-element.50), channel_id=1, source_target_pairs={{0,2},{1,3},{2,0},{3,1},{4,6},{5,7},{6,4},{7,5},{8,10},{9,11},{10,... | collective-permute-start | bytes 3145736 | tf_op jit(solution)/shard_map/ppermute | solution.py:348
  203.9 67.4 %collective-permute-start.19 = (bf16[256,2048]{1,0:T(8,128)(2,1)S(1)}, bf16[256,2048]{1,0:T(8,128)(2,1)S(1)}, u32[]{:S(2)}, u32[]{:S(2)}) collective-permute-start(bf16[256,2048]{1,0:T(8,128)(2,1)S(1)} %get-tuple-element.50), channel_id=1, source_target_pairs={{0,1},{1,0},{2,3},{3,2},{4,5},{5,4},{6,7},{7,6},{8,9},{9,8},{10,11... | collective-permute-start | bytes 3145736 | tf_op jit(solution)/shard_map/ppermute | solution.py:348
  220.1 54.2 %collective-permute-start.20 = (bf16[256,2048]{1,0:T(8,128)(2,1)S(1)}, bf16[256,2048]{1,0:T(8,128)(2,1)S(1)}, u32[]{:S(2)}, u32[]{:S(2)}) collective-permute-start(bf16[256,2048]{1,0:T(8,128)(2,1)S(1)} %get-tuple-element.49), channel_id=1, source_target_pairs={{0,2},{1,3},{2,0},{3,1},{4,6},{5,7},{6,4},{7,5},{8,10},{9,11},{10,... | collective-permute-start | bytes 3145736 | tf_op jit(solution)/shard_map/ppermute | solution.py:348
  228.4 65.4 %collective-permute-start.12 = (bf16[256,2048]{1,0:T(8,128)(2,1)S(1)}, bf16[256,2048]{1,0:T(8,128)(2,1)S(1)}, u32[]{:S(2)}, u32[]{:S(2)}) collective-permute-start(bf16[256,2048]{1,0:T(8,128)(2,1)S(1)} %get-tuple-element.106), channel_id=1, source_target_pairs={{0,1},{1,0},{2,3},{3,2},{4,5},{5,4},{6,7},{7,6},{8,9},{9,8},{10,11... | collective-permute-start | bytes 3145736 | tf_op jit(solution)/shard_map/ppermute | solution.py:348
  248.9 47.3 %collective-permute-start.15 = (bf16[256,2048]{1,0:T(8,128)(2,1)S(1)}, bf16[256,2048]{1,0:T(8,128)(2,1)S(1)}, u32[]{:S(2)}, u32[]{:S(2)}) collective-permute-start(bf16[256,2048]{1,0:T(8,128)(2,1)S(1)} %get-tuple-element.102), channel_id=1, source_target_pairs={{0,2},{1,3},{2,0},{3,1},{4,6},{5,7},{6,4},{7,5},{8,10},{9,11},{10,... | collective-permute-start | bytes 3145736 | tf_op jit(solution)/shard_map/ppermute | solution.py:348
  271.3 44.9 %collective-permute-start.13 = (bf16[256,2048]{1,0:T(8,128)(2,1)S(1)}, bf16[256,2048]{1,0:T(8,128)(2,1)S(1)}, u32[]{:S(2)}, u32[]{:S(2)}) collective-permute-start(bf16[256,2048]{1,0:T(8,128)(2,1)S(1)} %get-tuple-element.102), channel_id=1, source_target_pairs={{0,1},{1,0},{2,3},{3,2},{4,5},{5,4},{6,7},{7,6},{8,9},{9,8},{10,11... | collective-permute-start | bytes 3145736 | tf_op jit(solution)/shard_map/ppermute | solution.py:348
  274.3 42.1 %collective-permute-start.14 = (bf16[256,2048]{1,0:T(8,128)(2,1)S(1)}, bf16[256,2048]{1,0:T(8,128)(2,1)S(1)}, u32[]{:S(2)}, u32[]{:S(2)}) collective-permute-start(bf16[256,2048]{1,0:T(8,128)(2,1)S(1)} %get-tuple-element.106), channel_id=1, source_target_pairs={{0,2},{1,3},{2,0},{3,1},{4,6},{5,7},{6,4},{7,5},{8,10},{9,11},{10,... | collective-permute-start | bytes 3145736 | tf_op jit(solution)/shard_map/ppermute | solution.py:348
  293.8 37.4 %collective-permute-start.16 = (bf16[256,2048]{1,0:T(8,128)(2,1)S(1)}, bf16[256,2048]{1,0:T(8,128)(2,1)S(1)}, u32[]{:S(2)}, u32[]{:S(2)}) collective-permute-start(bf16[256,2048]{1,0:T(8,128)(2,1)S(1)} %collective-permute-done.12), channel_id=1, source_target_pairs={{0,2},{1,3},{2,0},{3,1},{4,6},{5,7},{6,4},{7,5},{8,10},{9,11},{10,... | collective-permute-start | bytes 3145736 | tf_op jit(solution)/shard_map/ppermute | solution.py:348
  296.2 39.6 %collective-permute-start.17 = (bf16[256,2048]{1,0:T(8,128)(2,1)S(1)}, bf16[256,2048]{1,0:T(8,128)(2,1)S(1)}, u32[]{:S(2)}, u32[]{:S(2)}) collective-permute-start(bf16[256,2048]{1,0:T(8,128)(2,1)S(1)} %collective-permute-done.15), channel_id=1, source_target_pairs={{0,1},{1,0},{2,3},{3,2},{4,5},{5,4},{6,7},{7,6},{8,9},{9,8},{10,11... | collective-permute-start | bytes 3145736 | tf_op jit(solution)/shard_map/ppermute | solution.py:348
  339.1 52.7 %collective-permute-start.23 = (bf16[256,2048]{1,0:T(8,128)(2,1)}, bf16[256,2048]{1,0:T(8,128)(2,1)S(1)}, u32[]{:S(2)}, u32[]{:S(2)}) collective-permute-start(bf16[256,2048]{1,0:T(8,128)(2,1)} %collective-permute-done.21), channel_id=1, source_target_pairs={{0,1},{1,0},{2,3},{3,2},{4,5},{5,4},{6,7},{7,6},{8,9},{9,8},{10,11... | collective-permute-start | bytes 3145736 | tf_op jit(solution)/shard_map/ppermute | solution.py:348
  340.8 50.0 %collective-permute-start.22 = (bf16[256,2048]{1,0:T(8,128)(2,1)S(1)}, bf16[256,2048]{1,0:T(8,128)(2,1)S(1)}, u32[]{:S(2)}, u32[]{:S(2)}) collective-permute-start(bf16[256,2048]{1,0:T(8,128)(2,1)S(1)} %collective-permute-done.18), channel_id=1, source_target_pairs={{0,2},{1,3},{2,0},{3,1},{4,6},{5,7},{6,4},{7,5},{8,10},{9,11},{10,... | collective-permute-start | bytes 3145736 | tf_op jit(solution)/shard_map/ppermute | solution.py:348
  530.2 177.2 %reduce-scatter.6.cloned.1.call-start = ((), (), s32[]{:S(2)}) async-start(), calls=%async_computation.10 | async-start | bytes 9437184 | tf_op jit(solution)/shard_map/reduce_scatter | solution.py:440
  530.9 285.0 %reduce-scatter.10.cloned.1.call-start = ((), (), s32[]{:S(2)}) async-start(), calls=%async_computation.12 | async-start | bytes 9437184 | tf_op jit(solution)/shard_map/reduce_scatter | solution.py:440
  555.5 419.7 %reduce-scatter.14.cloned.1.call-start = ((), (), s32[]{:S(2)}) async-start(), calls=%async_computation.14 | async-start | bytes 2359296 | tf_op jit(solution)/shard_map/reduce_scatter | solution.py:440
  557.9 26.1 %collective-permute-start.28 = (bf16[256,2048]{1,0:T(8,128)(2,1)S(1)}, bf16[256,2048]{1,0:T(8,128)(2,1)S(1)}, u32[]{:S(2)}, u32[]{:S(2)}) collective-permute-start(bf16[256,2048]{1,0:T(8,128)(2,1)S(1)} %get-tuple-element.126), channel_id=1, source_target_pairs={{0,1},{1,0},{2,3},{3,2},{4,5},{5,4},{6,7},{7,6},{8,9},{9,8},{10,11... | collective-permute-start | bytes 3145736 | tf_op jit(solution)/shard_map/ppermute | solution.py:348
  557.9 27.8 %collective-permute-start.25 = (bf16[256,2048]{1,0:T(8,128)(2,1)S(1)}, bf16[256,2048]{1,0:T(8,128)(2,1)S(1)}, u32[]{:S(2)}, u32[]{:S(2)}) collective-permute-start(bf16[256,2048]{1,0:T(8,128)(2,1)S(1)} %get-tuple-element.127), channel_id=1, source_target_pairs={{0,2},{1,3},{2,0},{3,1},{4,6},{5,7},{6,4},{7,5},{8,10},{9,11},{10,... | collective-permute-start | bytes 3145736 | tf_op jit(solution)/shard_map/ppermute | solution.py:348
  558.8 47.6 %collective-permute-start.27 = (bf16[256,2048]{1,0:T(8,128)(2,1)S(1)}, bf16[256,2048]{1,0:T(8,128)(2,1)S(1)}, u32[]{:S(2)}, u32[]{:S(2)}) collective-permute-start(bf16[256,2048]{1,0:T(8,128)(2,1)S(1)} %slice.235), channel_id=1, source_target_pairs={{0,1},{1,0},{2,3},{3,2},{4,5},{5,4},{6,7},{7,6},{8,9},{9,8},{10,11... | collective-permute-start | bytes 3145736 | tf_op jit(solution)/shard_map/ppermute | solution.py:348
  560.1 46.4 %collective-permute-start.24 = (bf16[256,2048]{1,0:T(8,128)(2,1)S(1)}, bf16[256,2048]{1,0:T(8,128)(2,1)S(1)}, u32[]{:S(2)}, u32[]{:S(2)}) collective-permute-start(bf16[256,2048]{1,0:T(8,128)(2,1)S(1)} %get-tuple-element.128), channel_id=1, source_target_pairs={{0,2},{1,3},{2,0},{3,1},{4,6},{5,7},{6,4},{7,5},{8,10},{9,11},{10,... | collective-permute-start | bytes 3145736 | tf_op jit(solution)/shard_map/ppermute | solution.py:348
  585.6 39.8 %collective-permute-start.29 = (bf16[256,2048]{1,0:T(8,128)(2,1)S(1)}, bf16[256,2048]{1,0:T(8,128)(2,1)S(1)}, u32[]{:S(2)}, u32[]{:S(2)}) collective-permute-start(bf16[256,2048]{1,0:T(8,128)(2,1)S(1)} %add_convert_fusion.6), channel_id=1, source_target_pairs={{0,2},{1,3},{2,0},{3,1},{4,6},{5,7},{6,4},{7,5},{8,10},{9,11},{10,... | collective-permute-start | bytes 3145736 | tf_op jit(solution)/shard_map/ppermute | solution.py:348
  586.2 39.2 %collective-permute-start.26 = (bf16[256,2048]{1,0:T(8,128)(2,1)S(1)}, bf16[256,2048]{1,0:T(8,128)(2,1)S(1)}, u32[]{:S(2)}, u32[]{:S(2)}) collective-permute-start(bf16[256,2048]{1,0:T(8,128)(2,1)S(1)} %add_convert_fusion.7), channel_id=1, source_target_pairs={{0,1},{1,0},{2,3},{3,2},{4,5},{5,4},{6,7},{7,6},{8,9},{9,8},{10,11... | collective-permute-start | bytes 3145736 | tf_op jit(solution)/shard_map/ppermute | solution.py:348
  632.1 26.8 %collective-permute-start.30 = (bf16[256,2048]{1,0:T(8,128)(2,1)S(1)}, bf16[256,2048]{1,0:T(8,128)(2,1)S(1)}, u32[]{:S(2)}, u32[]{:S(2)}) collective-permute-start(bf16[256,2048]{1,0:T(8,128)(2,1)S(1)} %get-tuple-element.62), channel_id=1, source_target_pairs={{0,1},{1,0},{2,3},{3,2},{4,5},{5,4},{6,7},{7,6},{8,9},{9,8},{10,11... | collective-permute-start | bytes 3145736 | tf_op jit(solution)/shard_map/ppermute | solution.py:348
  633.7 51.0 %collective-permute-start.32 = (bf16[256,2048]{1,0:T(8,128)(2,1)S(1)}, bf16[256,2048]{1,0:T(8,128)(2,1)S(1)}, u32[]{:S(2)}, u32[]{:S(2)}) collective-permute-start(bf16[256,2048]{1,0:T(8,128)(2,1)S(1)} %get-tuple-element.62), channel_id=1, source_target_pairs={{0,2},{1,3},{2,0},{3,1},{4,6},{5,7},{6,4},{7,5},{8,10},{9,11},{10,... | collective-permute-start | bytes 3145736 | tf_op jit(solution)/shard_map/ppermute | solution.py:348
  634.0 49.6 %collective-permute-start.31 = (bf16[256,2048]{1,0:T(8,128)(2,1)S(1)}, bf16[256,2048]{1,0:T(8,128)(2,1)S(1)}, u32[]{:S(2)}, u32[]{:S(2)}) collective-permute-start(bf16[256,2048]{1,0:T(8,128)(2,1)S(1)} %get-tuple-element.63), channel_id=1, source_target_pairs={{0,1},{1,0},{2,3},{3,2},{4,5},{5,4},{6,7},{7,6},{8,9},{9,8},{10,11... | collective-permute-start | bytes 3145736 | tf_op jit(solution)/shard_map/ppermute | solution.py:348
  634.4 47.9 %collective-permute-start.33 = (bf16[256,2048]{1,0:T(8,128)(2,1)S(1)}, bf16[256,2048]{1,0:T(8,128)(2,1)S(1)}, u32[]{:S(2)}, u32[]{:S(2)}) collective-permute-start(bf16[256,2048]{1,0:T(8,128)(2,1)S(1)} %get-tuple-element.63), channel_id=1, source_target_pairs={{0,2},{1,3},{2,0},{3,1},{4,6},{5,7},{6,4},{7,5},{8,10},{9,11},{10,... | collective-permute-start | bytes 3145736 | tf_op jit(solution)/shard_map/ppermute | solution.py:348
  658.9 40.9 %collective-permute-start.34 = (bf16[256,2048]{1,0:T(8,128)(2,1)S(1)}, bf16[256,2048]{1,0:T(8,128)(2,1)S(1)}, u32[]{:S(2)}, u32[]{:S(2)}) collective-permute-start(bf16[256,2048]{1,0:T(8,128)(2,1)S(1)} %collective-permute-done.30), channel_id=1, source_target_pairs={{0,2},{1,3},{2,0},{3,1},{4,6},{5,7},{6,4},{7,5},{8,10},{9,11},{10,... | collective-permute-start | bytes 3145736 | tf_op jit(solution)/shard_map/ppermute | solution.py:348
  682.2 18.6 %collective-permute-start.35 = (bf16[256,2048]{1,0:T(8,128)(2,1)S(1)}, bf16[256,2048]{1,0:T(8,128)(2,1)S(1)}, u32[]{:S(2)}, u32[]{:S(2)}) collective-permute-start(bf16[256,2048]{1,0:T(8,128)(2,1)S(1)} %collective-permute-done.33), channel_id=1, source_target_pairs={{0,1},{1,0},{2,3},{3,2},{4,5},{5,4},{6,7},{7,6},{8,9},{9,8},{10,11... | collective-permute-start | bytes 3145736 | tf_op jit(solution)/shard_map/ppermute | solution.py:348
  769.7 207.3 %reduce-scatter.12.cloned.1.call-start = ((), (), s32[]{:S(2)}) async-start(), calls=%async_computation.13 | async-start | bytes 7077888 | tf_op jit(solution)/shard_map/reduce_scatter | solution.py:440
  814.5 23.0 %collective-permute-start.46 = (bf16[256,2048]{1,0:T(8,128)(2,1)S(1)}, bf16[256,2048]{1,0:T(8,128)(2,1)S(1)}, u32[]{:S(2)}, u32[]{:S(2)}) collective-permute-start(bf16[256,2048]{1,0:T(8,128)(2,1)S(1)} %get-tuple-element.123), channel_id=1, source_target_pairs={{0,1},{1,0},{2,3},{3,2},{4,5},{5,4},{6,7},{7,6},{8,9},{9,8},{10,11... | collective-permute-start | bytes 3145736 | tf_op jit(solution)/shard_map/ppermute | solution.py:348
  818.9 23.2 %collective-permute-start.43 = (bf16[256,2048]{1,0:T(8,128)(2,1)S(1)}, bf16[256,2048]{1,0:T(8,128)(2,1)S(1)}, u32[]{:S(2)}, u32[]{:S(2)}) collective-permute-start(bf16[256,2048]{1,0:T(8,128)(2,1)S(1)} %get-tuple-element.124), channel_id=1, source_target_pairs={{0,2},{1,3},{2,0},{3,1},{4,6},{5,7},{6,4},{7,5},{8,10},{9,11},{10,... | collective-permute-start | bytes 3145736 | tf_op jit(solution)/shard_map/ppermute | solution.py:348
  833.0 31.6 %collective-permute-start.36 = (bf16[256,2048]{1,0:T(8,128)(2,1)S(1)}, bf16[256,2048]{1,0:T(8,128)(2,1)S(1)}, u32[]{:S(2)}, u32[]{:S(2)}) collective-permute-start(bf16[256,2048]{1,0:T(8,128)(2,1)S(1)} %get-tuple-element.113), channel_id=1, source_target_pairs={{0,2},{1,3},{2,0},{3,1},{4,6},{5,7},{6,4},{7,5},{8,10},{9,11},{10,... | collective-permute-start | bytes 3145736 | tf_op jit(solution)/shard_map/ppermute | solution.py:348
  833.8 53.3 %collective-permute-start.37 = (bf16[256,2048]{1,0:T(8,128)(2,1)S(1)}, bf16[256,2048]{1,0:T(8,128)(2,1)}, u32[]{:S(2)}, u32[]{:S(2)}) collective-permute-start(bf16[256,2048]{1,0:T(8,128)(2,1)S(1)} %get-tuple-element.116), channel_id=1, source_target_pairs={{0,2},{1,3},{2,0},{3,1},{4,6},{5,7},{6,4},{7,5},{8,10},{9,11},{10,... | collective-permute-start | bytes 3145736 | tf_op jit(solution)/shard_map/ppermute | solution.py:348
  835.0 53.7 %collective-permute-start.39 = (bf16[256,2048]{1,0:T(8,128)(2,1)S(1)}, bf16[256,2048]{1,0:T(8,128)(2,1)}, u32[]{:S(2)}, u32[]{:S(2)}) collective-permute-start(bf16[256,2048]{1,0:T(8,128)(2,1)S(1)} %get-tuple-element.115), channel_id=1, source_target_pairs={{0,1},{1,0},{2,3},{3,2},{4,5},{5,4},{6,7},{7,6},{8,9},{9,8},{10,11... | collective-permute-start | bytes 3145736 | tf_op jit(solution)/shard_map/ppermute | solution.py:348
  837.5 51.8 %collective-permute-start.40 = (bf16[256,2048]{1,0:T(8,128)(2,1)}, bf16[256,2048]{1,0:T(8,128)(2,1)}, u32[]{:S(2)}, u32[]{:S(2)}) collective-permute-start(bf16[256,2048]{1,0:T(8,128)(2,1)} %get-tuple-element.114), channel_id=1, source_target_pairs={{0,1},{1,0},{2,3},{3,2},{4,5},{5,4},{6,7},{7,6},{8,9},{9,8},{10,11... | collective-permute-start | bytes 3145736 | tf_op jit(solution)/shard_map/ppermute | solution.py:348
  842.1 63.9 %collective-permute-start.45 = (bf16[256,2048]{1,0:T(8,128)(2,1)}, bf16[256,2048]{1,0:T(8,128)(2,1)S(1)}, u32[]{:S(2)}, u32[]{:S(2)}) collective-permute-start(bf16[256,2048]{1,0:T(8,128)(2,1)} %slice.243), channel_id=1, source_target_pairs={{0,1},{1,0},{2,3},{3,2},{4,5},{5,4},{6,7},{7,6},{8,9},{9,8},{10,11... | collective-permute-start | bytes 3145736 | tf_op jit(solution)/shard_map/ppermute | solution.py:348
  865.5 44.0 %collective-permute-start.42 = (bf16[256,2048]{1,0:T(8,128)(2,1)}, bf16[256,2048]{1,0:T(8,128)(2,1)S(1)}, u32[]{:S(2)}, u32[]{:S(2)}) collective-permute-start(bf16[256,2048]{1,0:T(8,128)(2,1)} %get-tuple-element.125), channel_id=1, source_target_pairs={{0,2},{1,3},{2,0},{3,1},{4,6},{5,7},{6,4},{7,5},{8,10},{9,11},{10,... | collective-permute-start | bytes 3145736 | tf_op jit(solution)/shard_map/ppermute | solution.py:348
  887.1 44.9 %collective-permute-start.47 = (bf16[256,2048]{1,0:T(8,128)(2,1)}, bf16[256,2048]{1,0:T(8,128)(2,1)}, u32[]{:S(2)}, u32[]{:S(2)}) collective-permute-start(bf16[256,2048]{1,0:T(8,128)(2,1)} %add_convert_fusion), channel_id=1, source_target_pairs={{0,2},{1,3},{2,0},{3,1},{4,6},{5,7},{6,4},{7,5},{8,10},{9,11},{10,... | collective-permute-start | bytes 3145736 | tf_op jit(solution)/shard_map/ppermute | solution.py:348
  888.6 43.4 %collective-permute-start.44 = (bf16[256,2048]{1,0:T(8,128)(2,1)}, bf16[256,2048]{1,0:T(8,128)(2,1)}, u32[]{:S(2)}, u32[]{:S(2)}) collective-permute-start(bf16[256,2048]{1,0:T(8,128)(2,1)} %add_convert_fusion.1), channel_id=1, source_target_pairs={{0,1},{1,0},{2,3},{3,2},{4,5},{5,4},{6,7},{7,6},{8,9},{9,8},{10,11... | collective-permute-start | bytes 3145736 | tf_op jit(solution)/shard_map/ppermute | solution.py:348
  896.2 54.8 %collective-permute-start.38 = (bf16[256,2048]{1,0:T(8,128)(2,1)}, bf16[256,2048]{1,0:T(8,128)(2,1)}, u32[]{:S(2)}, u32[]{:S(2)}) collective-permute-start(bf16[256,2048]{1,0:T(8,128)(2,1)} %get-tuple-element.112), channel_id=1, source_target_pairs={{0,1},{1,0},{2,3},{3,2},{4,5},{5,4},{6,7},{7,6},{8,9},{9,8},{10,11... | collective-permute-start | bytes 3145736 | tf_op jit(solution)/shard_map/ppermute | solution.py:348
  906.0 48.8 %collective-permute-start.41 = (bf16[256,2048]{1,0:T(8,128)(2,1)}, bf16[256,2048]{1,0:T(8,128)(2,1)}, u32[]{:S(2)}, u32[]{:S(2)}) collective-permute-start(bf16[256,2048]{1,0:T(8,128)(2,1)} %get-tuple-element.110), channel_id=1, source_target_pairs={{0,2},{1,3},{2,0},{3,1},{4,6},{5,7},{6,4},{7,5},{8,10},{9,11},{10,... | collective-permute-start | bytes 3145736 | tf_op jit(solution)/shard_map/ppermute | solution.py:348
  935.5 26.8 %collective-permute-start.48 = (f32[2,8,64]{2,1,0:T(8,128)S(1)}, f32[2,8,64]{2,1,0:T(8,128)S(1)}, u32[]{:S(2)}, u32[]{:S(2)}) collective-permute-start(f32[2,8,64]{2,1,0:T(8,128)S(1)} %bitcast.47), channel_id=1, source_target_pairs={{0,1},{1,0},{2,3},{3,2},{4,5},{5,4},{6,7},{7,6},{8,9},{9,8},{10,11... | collective-permute-start | bytes 12296 | tf_op jit(solution)/shard_map/ppermute | solution.py:406
  936.3 26.1 %collective-permute-start.49 = (f32[2,8,64]{2,1,0:T(8,128)S(1)}, f32[2,8,64]{2,1,0:T(8,128)S(1)}, u32[]{:S(2)}, u32[]{:S(2)}) collective-permute-start(f32[2,8,64]{2,1,0:T(8,128)S(1)} %bitcast.46), channel_id=1, source_target_pairs={{0,2},{1,3},{2,0},{3,1},{4,6},{5,7},{6,4},{7,5},{8,10},{9,11},{10,... | collective-permute-start | bytes 12296 | tf_op jit(solution)/shard_map/ppermute | solution.py:406
  937.6 24.8 %collective-permute-start.50 = (f32[2,8,64]{2,1,0:T(8,128)S(1)}, f32[2,8,64]{2,1,0:T(8,128)S(1)}, u32[]{:S(2)}, u32[]{:S(2)}) collective-permute-start(f32[2,8,64]{2,1,0:T(8,128)S(1)} %bitcast.45), channel_id=1, source_target_pairs={{0,3},{1,2},{2,1},{3,0},{4,7},{5,6},{6,5},{7,4},{8,11},{9,10},{10,... | collective-permute-start | bytes 12296 | tf_op jit(solution)/shard_map/ppermute | solution.py:406
  964.9 9.1 collective-permute-start.53
  966.3 7.7 collective-permute-start.54
  966.3 7.7 collective-permute-start.55
  (53 other events, 1083.3 us)
Sparse Core Ops, SparseCore 0:
  10.2 67.4 all-gather.5
  79.3 27.7 all-gather.7
  108.7 81.4 all-gather.9
  191.7 80.4 all-gather.11
  273.6 80.5 all-gather.13
  530.3 86.6 reduce-scatter.7
  619.3 87.9 reduce-scatter.5
  709.6 87.9 reduce-scatter.9
  799.9 34.5 reduce-scatter.13
  836.7 68.3 reduce-scatter.11

commit v5 on v4

--- a/solution.py
+++ b/solution.py
@@ -398,7 +398,8 @@
 def scatter_vectors(values):
     sizes = {axis: lax.axis_size(axis) for axis in ("fsdp", "tp")}
     values = values.reshape(values.shape[0], sizes["fsdp"], sizes["tp"], -1)
-    for axis, dim in (("tp", 2), ("fsdp", 1)):
+    for axis in ("fsdp", "tp"):
+        dim = 1
         size, me = sizes[axis], lax.axis_index(axis)
         total = lax.dynamic_index_in_dim(values, me, axis=dim, keepdims=False)
         for r in range(1, size):
@@ -478,16 +479,18 @@
     hid, gate_slope, up_slope = gate_up(h2, gate_full, up_full)
     down_term = matmul_tn(dm, hid).astype(BF16)
     grad_gate, grad_up = hidden_back(dm, down_full, after(gate_slope, down_term), up_slope)
-    half_group = group // 2
+    half_group, quarter = group // 2, group // 4
     two = {}
-    two[1] = two_nt(grad_gate, grad_up, gate_full, up_full, half_group, half_group)
-    two[0] = two_nt(after(grad_gate, two[1]), grad_up, gate_full, up_full, 0, half_group)
+    two[2] = two_nt(grad_gate, grad_up, gate_full, up_full, half_group, half_group)
+    two[1] = two_nt(after(grad_gate, two[2]), grad_up, gate_full, up_full, quarter, quarter)
+    two[0] = two_nt(after(grad_gate, two[1]), grad_up, gate_full, up_full, 0, quarter)
     gate_term = matmul_tn(h2, after(grad_gate, two[0])).astype(BF16)
     up_term = matmul_tn(h2, after(grad_up, gate_term)).astype(BF16)
     mlp = matmul_nt(after(hid, up_term), down_full).astype(BF16)
 
     def two_piece(r):
-        i, inside = divmod(r, size // 2)
+        i = (r >= size // 4) + (r >= size // 2)
+        inside = r - (0, size // 4, size // 2)[i]
         return two[i][inside * own : (inside + 1) * own]
 
     grad_two = scatter_tp(two_piece, size)
@@ -497,11 +500,11 @@
         g + s * (i - n * jnp.mean(i * n, axis=-1, keepdims=True))
         for g, s, i, n in zip(grad_rows, scale_two, inner_two, normed_two)
     ]
-    grad_attn = rows_of(gather_tp([after(g.astype(BF16), gate_term, up_term) for g in grad_middle], size))
+    grad_attn = rows_of(gather_tp([after(g.astype(BF16), gate_term) for g in grad_middle], size))
     down_grad = back_fsdp(down_term)
     gate_grad = back_fsdp(gate_term)
     up_grad = back_fsdp(up_term)
-    mlp, grad_attn, down_grad, gate_grad = lax.optimization_barrier((mlp, grad_attn, down_grad, gate_grad))
+    mlp, grad_attn, down_grad = lax.optimization_barrier((mlp, grad_attn, down_grad))
     mlp_out = scatter_tp(lambda r: mlp[r * own : (r + 1) * own], size, settle=True)
     output = jnp.concatenate(
         [(m * (v + o)).astype(BF16) for m, v, o in zip(valid, middle, mlp_out)], axis=0
@@ -523,14 +526,15 @@
             last = out_term = matmul_tn(grad_attn, mixed).astype(BF16)
     grad_all = jnp.concatenate([grad_qkv[s] for s in range(count)], axis=0)
     qkv_term = matmul_tn(rows_of(h1_slot), grad_all).astype(BF16)
-    partial_one[0] = matmul_nt(after(grad_qkv[0], qkv_term, up_grad), qkv_full).astype(BF16)
+    partial_one[0] = matmul_nt(after(grad_qkv[0], qkv_term, gate_grad, up_grad), qkv_full).astype(BF16)
 
     def one_piece(r):
         s, inside = divmod(r, per_slot)
         return partial_one[s][inside * own : (inside + 1) * own]
 
     grad_one = scatter_tp(one_piece, size)
-    gain_attn_term = sum(jnp.sum(g * n, axis=0) for g, n in zip(grad_one, normed_one))
+    qkv_held = after(qkv_term, partial_one[0]).astype(F32)
+    gain_attn_term = jnp.sum(qkv_held * qkv_full.astype(F32), axis=1) / gain_attn
     inner_one = [g * gain_attn for g in grad_one]
     input_grad = jnp.concatenate(
         [

time: 992 us -> 1000 us (level)
  waiting for transfers between devices: 369 us -> 393 us
  other arithmetic: 63.8 us -> 53.8 us
    ppermute x10, waiting for transfers between devices: 0.7 us -> 61.2 us  [scatter_vectors(): total = total + lax.ppermute(sent, axis, [(i, i ^ r) for i in range(size)])]
    ppermute x48, waiting for transfers between devices: 363 us -> 329 us  [hop(): return lax.ppermute(value, 'tp', [(i, i ^ bit) for i in range(size)])]
    unnamed x123 -> x118, local copies, waits for them, and re-layouts: 33.8 us -> 32.3 us
    pallas_call x2 -> x3, Pallas kernels: 55.5 us -> 56.1 us  [two_nt(): pl.pallas_call(two_nt_kernel, out_shape=jax.ShapeDtypeStruct((rows, width...]
  transfers between devices with their start and end apart: 68 -> 68, of which waited for: 32 -> 29; matrix products, arithmetic and copies ran while one was open for 27% -> 28% of each run, Pallas kernels for 14% -> 23%
where the time goes in v5:
time: 1000 us
  waiting for transfers between devices  393 us (39%)
  Pallas kernels  233 us (23%)
  matrix products  186 us (19%)
  starting transfers between devices  69.2 us (7%)
  other arithmetic  53.8 us (5%)
  local copies, waits for them, and re-layouts  49.9 us (5%)
  between operations  15.6 us (2%)
    ppermute x48, waiting for transfers between devices, hop(): return lax.ppermute(value, 'tp', [(i, i ^ bit) for i in range(size)])  329 us
    dot_general x5, matrix products, matmul_tn(): lax.dot_general(left, right, (((0,), (0,)), ((), ())), preferred_element_...  100 us
    ppermute x10, waiting for transfers between devices, scatter_vectors(): total = total + lax.ppermute(sent, axis, [(i, i ^ r) for i in range(size)])  61.2 us
    pallas_call x3, Pallas kernels, two_nt(): pl.pallas_call(two_nt_kernel, out_shape=jax.ShapeDtypeStruct((rows, width...  56.1 us
    ppermute x48, starting transfers between devices, hop(): return lax.ppermute(value, 'tp', [(i, i ^ bit) for i in range(size)])  55.2 us
    dot_general x5, matrix products, matmul_nt(): lax.dot_general(left, right, (((1,), (1,)), ((), ())), preferred_element_...  51.8 us
    pallas_call x2, Pallas kernels, attend_back(): pl.pallas_call(functools.partial(attend_back_kernel, own), out_shape=jax....  51.5 us
    pallas_call x1, Pallas kernels, gate_up(): pl.pallas_call(gate_up_kernel, out_shape=[jax.ShapeDtypeStruct((rows, wid...  48.6 us
  transfers between devices with their start and end apart: 68, of which 29 were waited for; matrix products, arithmetic and copies ran while one was open for 28% of the time, Pallas kernels for 23%

profile of v5, /device:TPU:0, one launch (start us, length us, event | category | flops | bytes accessed | tf_op | source)
XLA Modules:
  0.0 999.7 jit_solution(13420783631591859718)
XLA Ops:
  13.8 3.0 collective-permute-start
  26.2 14.8 %collective-permute-done = bf16[256,2048]{1,0:T(8,128)(2,1)} collective-permute-done((bf16[256,2048]{1,0:T(8,128)(2,1)}, bf16[256,2048]{1,0:T(8,128)(2,1)}, u32[]{:S(2)}, u32[]{:S(2)}) %collective-permute-start) | collective-permute-done | bytes 1048608 | tf_op jit(solution)/shard_map/ppermute | solution.py:348
  44.6 2.4 constant_dynamic-update-slice_fusion.33
  47.1 16.5 %collective-permute-done.1 = bf16[256,2048]{1,0:T(8,128)(2,1)} collective-permute-done((bf16[256,2048]{1,0:T(8,128)(2,1)}, bf16[256,2048]{1,0:T(8,128)(2,1)}, u32[]{:S(2)}, u32[]{:S(2)}) %collective-permute-start.1) | collective-permute-done | bytes 1048608 | tf_op jit(solution)/shard_map/ppermute | solution.py:348
  67.2 2.8 constant_dynamic-update-slice_fusion.31
  71.6 16.6 %collective-permute-done.4 = bf16[256,2048]{1,0:T(8,128)(2,1)S(1)} collective-permute-done((bf16[256,2048]{1,0:T(8,128)(2,1)}, bf16[256,2048]{1,0:T(8,128)(2,1)S(1)}, u32[]{:S(2)}, u32[]{:S(2)}) %collective-permute-start.4) | collective-permute-done | bytes 1048608 | tf_op jit(solution)/shard_map/ppermute | solution.py:348
  91.3 13.4 %fusion.3.q_ref.k_ref.v_ref = f32[1024,1536]{1,0:T(8,128)} fusion(bf16[2048,1536]{1,0:T(8,128)(2,1)} %all-gather.6.cloned.1.call-done, bf16[256,2048]{1,0:T(8,128)(2,1)} %collective-permute-done.1, bf16[256,2048]{1,0:T(8,128)(2,1)} %collective-permute-done, bf16[256,2048]{1,0:T(8,128)(2,1)} %get-tuple-element.92, bf16[256,2048]{1,0:T(8,128)(2,1)} %get-tuple-element.94), kind=kOutput, calls=%fused_computation.9 | convolution fusion | flops 6459228160 | bytes 16777216 | tf_op jit(solution)/shard_map/dot_general | solution.py:22
  104.8 10.1 %fusion.78.q_ref.k_ref.v_ref = f32[1024,1536]{1,0:T(8,128)} fusion(bf16[1024,2048]{1,0:T(8,128)(2,1)} %get-tuple-element.47, bf16[2048,1536]{1,0:T(8,128)(2,1)S(1)} %copy-done.15), kind=kOutput, calls=%fused_computation.200 | convolution fusion | flops 6442450944 | bytes 16777216 | tf_op jit(solution)/shard_map/dot_general | solution.py:22
  114.9 23.6 %attend.3 = (bf16[1024,512]{1,0:T(8,128)(2,1)}, bf16[1024,512]{1,0:T(8,128)(2,1)}, bf16[1024,512]{1,0:T(8,128)(2,1)}, bf16[1024,512]{1,0:T(8,128)(2,1)}, f32[4,8,1024]{2,1,0:T(8,128)}) custom-call(s32[2]{0:T(128)} %pad_add_fusion.1.info, f32[1024,1536]{1,0:T(8,128)} %fusion.78.q_ref.k_ref.v_ref, f32[1024,1536]{1,0:T(8,128)} %fusion.78.q_ref.k_ref.v_ref, ...), custom_call_target="tpu_custom_call" | custom-call | flops 4294967296 | bytes 10485760 | tf_op jit(solution)/shard_map/attend/pallas_call | solution.py:134
  138.5 4.3 convolution_convert_fusion.7
  147.4 18.4 %attend.2 = (bf16[1024,512]{1,0:T(8,128)(2,1)}, bf16[1024,512]{1,0:T(8,128)(2,1)}, bf16[1024,512]{1,0:T(8,128)(2,1)}, bf16[1024,512]{1,0:T(8,128)(2,1)}, f32[4,8,1024]{2,1,0:T(8,128)}) custom-call(s32[2]{0:T(128)} %pad_add_fusion.info, f32[1024,1536]{1,0:T(8,128)} %fusion.3.q_ref.k_ref.v_ref, f32[1024,1536]{1,0:T(8,128)} %fusion.3.q_ref.k_ref.v_ref, ...), custom_call_target="tpu_custom_call" | custom-call | flops 4294967296 | bytes 10485760 | tf_op jit(solution)/shard_map/attend/pallas_call | solution.py:134
  165.9 7.3 collective-permute-start.6
  173.2 4.3 convolution_convert_fusion.8
  187.3 10.1 %collective-permute-done.6 = bf16[256,2048]{1,0:T(8,128)(2,1)S(1)} collective-permute-done((bf16[256,2048]{1,0:T(8,128)(2,1)}, bf16[256,2048]{1,0:T(8,128)(2,1)S(1)}, u32[]{:S(2)}, u32[]{:S(2)}) %collective-permute-start.6) | collective-permute-done | bytes 1048608 | tf_op jit(solution)/shard_map/ppermute | solution.py:348
  199.4 4.3 collective-permute-done.9
  205.5 14.3 %collective-permute-done.11 = bf16[256,2048]{1,0:T(8,128)(2,1)S(1)} collective-permute-done((bf16[256,2048]{1,0:T(8,128)(2,1)S(1)}, bf16[256,2048]{1,0:T(8,128)(2,1)S(1)}, u32[]{:S(2)}, u32[]{:S(2)}) %collective-permute-start.11) | collective-permute-done | bytes 1048608 | tf_op jit(solution)/shard_map/ppermute | solution.py:348
  221.9 4.3 collective-permute-done.8
  230.4 18.3 %collective-permute-done.18 = bf16[256,2048]{1,0:T(8,128)(2,1)S(1)} collective-permute-done((bf16[256,2048]{1,0:T(8,128)(2,1)S(1)}, bf16[256,2048]{1,0:T(8,128)(2,1)S(1)}, u32[]{:S(2)}, u32[]{:S(2)}) %collective-permute-start.18) | collective-permute-done | bytes 1048608 | tf_op jit(solution)/shard_map/ppermute | solution.py:348
  249.8 21.4 %collective-permute-done.19 = bf16[256,2048]{1,0:T(8,128)(2,1)S(1)} collective-permute-done((bf16[256,2048]{1,0:T(8,128)(2,1)S(1)}, bf16[256,2048]{1,0:T(8,128)(2,1)S(1)}, u32[]{:S(2)}, u32[]{:S(2)}) %collective-permute-start.19) | collective-permute-done | bytes 1048608 | tf_op jit(solution)/shard_map/ppermute | solution.py:348
  276.3 17.3 %collective-permute-done.12 = bf16[256,2048]{1,0:T(8,128)(2,1)S(1)} collective-permute-done((bf16[256,2048]{1,0:T(8,128)(2,1)S(1)}, bf16[256,2048]{1,0:T(8,128)(2,1)S(1)}, u32[]{:S(2)}, u32[]{:S(2)}) %collective-permute-start.12) | collective-permute-done | bytes 1048608 | tf_op jit(solution)/shard_map/ppermute | solution.py:348
  293.6 2.3 constant_dynamic-update-slice_fusion.14
  297.9 18.3 %collective-permute-done.13 = bf16[256,2048]{1,0:T(8,128)(2,1)S(1)} collective-permute-done((bf16[256,2048]{1,0:T(8,128)(2,1)S(1)}, bf16[256,2048]{1,0:T(8,128)(2,1)S(1)}, u32[]{:S(2)}, u32[]{:S(2)}) %collective-permute-start.13) | collective-permute-done | bytes 1048608 | tf_op jit(solution)/shard_map/ppermute | solution.py:348
  316.3 14.6 %collective-permute-done.16 = bf16[256,2048]{1,0:T(8,128)(2,1)S(1)} collective-permute-done((bf16[256,2048]{1,0:T(8,128)(2,1)S(1)}, bf16[256,2048]{1,0:T(8,128)(2,1)S(1)}, u32[]{:S(2)}, u32[]{:S(2)}) %collective-permute-start.16) | collective-permute-done | bytes 1048608 | tf_op jit(solution)/shard_map/ppermute | solution.py:348
  331.0 4.5 collective-permute-done.17
  335.6 3.3 copy-done.23
  342.2 48.6 %gate_up.1 = (bf16[2048,2048]{1,0:T(8,128)(2,1)}, bf16[2048,2048]{1,0:T(8,128)(2,1)}, bf16[2048,2048]{1,0:T(8,128)(2,1)}) custom-call(bf16[2048,2048]{1,0:T(8,128)(2,1)} %copy-done.23, bf16[2048,2048]{1,0:T(8,128)(2,1)} %all-gather.10.cloned.1.call-done.g_ref.wa_ref, bf16[2048,2048]{1,0:T(8,128)(2,1)} %all-gather.12.cloned.1.call-done.u_ref.wb_ref), custom_call_target="tpu_custom_call" | custom-call | flops 34359738368 | bytes 50331648 | tf_op jit(solution)/shard_map/gate_up/pallas_call | solution.py:282
  393.0 23.7 %convolution_convert_fusion.3 = bf16[2048,2048]{1,0:T(8,128)(2,1)} fusion(bf16[2048,2048]{1,0:T(8,128)(2,1)} %constant_dynamic-update-slice_fusion.12.g_ref, bf16[2048,2048]{1,0:T(8,128)(2,1)} %get-tuple-element.63), kind=kOutput, calls=%fused_computation.4 | convolution fusion | flops 17184063488 | bytes 25165824 | tf_op jit(solution)/shard_map/dot_general | solution.py:30
  416.8 34.8 %hidden_back.1 = (bf16[2048,2048]{1,0:T(8,128)(2,1)}, bf16[2048,2048]{1,0:T(8,128)(2,1)}) custom-call(bf16[2048,2048]{1,0:T(8,128)(2,1)} %constant_dynamic-update-slice_fusion.12.g_ref, bf16[2048,2048]{1,0:T(8,128)(2,1)} %all-gather.14.cloned.1.call-done.w_ref, bf16[2048,2048]{1,0:T(8,128)(2,1)} %get-tuple-element.55.gate_slope, ...), custom_call_target="tpu_custom_call" | custom-call | flops 17179869184 | bytes 50331648 | tf_op jit(solution)/shard_map/hidden_back/pallas_call | solution.py:306
  451.6 28.0 %two_nt.3 = bf16[1024,2048]{1,0:T(8,128)(2,1)} custom-call(bf16[2048,2048]{1,0:T(8,128)(2,1)} %get-tuple-element.61.a_ref, bf16[2048,2048]{1,0:T(8,128)(2,1)} %get-tuple-element.62.b_ref, bf16[2048,2048]{1,0:T(8,128)(2,1)} %all-gather.10.cloned.1.call-done.g_ref.wa_ref, bf16[2048,2048]{1,0:T(8,128)(2,1)} %all-gather.12.cloned.1.call-done.u_ref.wb_ref), custom_call_target="tpu_custom_call" | custom-call | flops 17179869184 | bytes 29360128 | tf_op jit(solution)/shard_map/two_nt/pallas_call | solution.py:334
  479.6 14.0 %two_nt.4 = bf16[512,2048]{1,0:T(8,128)(2,1)} custom-call(bf16[2048,2048]{1,0:T(8,128)(2,1)} %get-tuple-element.61.a_ref, bf16[2048,2048]{1,0:T(8,128)(2,1)} %get-tuple-element.62.b_ref, bf16[2048,2048]{1,0:T(8,128)(2,1)} %all-gather.10.cloned.1.call-done.g_ref.wa_ref, bf16[2048,2048]{1,0:T(8,128)(2,1)} %all-gather.12.cloned.1.call-done.u_ref.wb_ref), custom_call_target="tpu_custom_call" | custom-call | flops 8589934592 | bytes 23068672 | tf_op jit(solution)/shard_map/two_nt/pallas_call | solution.py:334
  493.6 14.0 %two_nt.5 = bf16[512,2048]{1,0:T(8,128)(2,1)} custom-call(bf16[2048,2048]{1,0:T(8,128)(2,1)} %get-tuple-element.61.a_ref, bf16[2048,2048]{1,0:T(8,128)(2,1)} %get-tuple-element.62.b_ref, bf16[2048,2048]{1,0:T(8,128)(2,1)} %all-gather.10.cloned.1.call-done.g_ref.wa_ref, bf16[2048,2048]{1,0:T(8,128)(2,1)} %all-gather.12.cloned.1.call-done.u_ref.wb_ref), custom_call_target="tpu_custom_call" | custom-call | flops 8589934592 | bytes 23068672 | tf_op jit(solution)/shard_map/two_nt/pallas_call | solution.py:334
  507.6 23.8 %convolution_convert_fusion.2 = bf16[2048,2048]{1,0:T(8,128)(2,1)} fusion(bf16[2048,2048]{1,0:T(8,128)(2,1)} %copy-done.23, bf16[2048,2048]{1,0:T(8,128)(2,1)} %get-tuple-element.61.a_ref), kind=kOutput, calls=%fused_computation.3 | convolution fusion | flops 17184063488 | bytes 25165824 | tf_op jit(solution)/shard_map/dot_general | solution.py:30
  531.4 24.0 %convolution_convert_fusion.1 = bf16[2048,2048]{1,0:T(8,128)(2,1)} fusion(bf16[2048,2048]{1,0:T(8,128)(2,1)} %copy-done.23, bf16[2048,2048]{1,0:T(8,128)(2,1)} %get-tuple-element.62.b_ref), kind=kOutput, calls=%fused_computation.2 | convolution fusion | flops 17184063488 | bytes 25165824 | tf_op jit(solution)/shard_map/dot_general | solution.py:30
  562.8 21.8 %collective-permute-done.28 = bf16[256,2048]{1,0:T(8,128)(2,1)S(1)} collective-permute-done((bf16[256,2048]{1,0:T(8,128)(2,1)S(1)}, bf16[256,2048]{1,0:T(8,128)(2,1)S(1)}, u32[]{:S(2)}, u32[]{:S(2)}) %collective-permute-start.28) | collective-permute-done | bytes 1048608 | tf_op jit(solution)/shard_map/ppermute | solution.py:348
  588.0 19.8 %collective-permute-done.24 = bf16[256,2048]{1,0:T(8,128)(2,1)S(1)} collective-permute-done((bf16[256,2048]{1,0:T(8,128)(2,1)S(1)}, bf16[256,2048]{1,0:T(8,128)(2,1)S(1)}, u32[]{:S(2)}, u32[]{:S(2)}) %collective-permute-start.24) | collective-permute-done | bytes 1048608 | tf_op jit(solution)/shard_map/ppermute | solution.py:348
  607.8 19.7 %collective-permute-done.29 = bf16[256,2048]{1,0:T(8,128)(2,1)S(1)} collective-permute-done((bf16[256,2048]{1,0:T(8,128)(2,1)S(1)}, bf16[256,2048]{1,0:T(8,128)(2,1)S(1)}, u32[]{:S(2)}, u32[]{:S(2)}) %collective-permute-start.29) | collective-permute-done | bytes 1048608 | tf_op jit(solution)/shard_map/ppermute | solution.py:348
  630.0 3.7 fusion.69
  637.8 20.5 %convolution_convert_fusion = bf16[2048,2048]{1,0:T(8,128)(2,1)} fusion(bf16[2048,2048]{1,0:T(8,128)(2,1)S(1)} %bitcast.79, bf16[2048,2048]{1,0:T(8,128)(2,1)S(1)} %bitcast.77), kind=kOutput, calls=%fused_computation.1 | convolution fusion | flops 17184063488 | bytes 25165824 | tf_op jit(solution)/shard_map/dot_general | solution.py:26
  661.1 22.8 %collective-permute-done.33 = bf16[256,2048]{1,0:T(8,128)(2,1)S(1)} collective-permute-done((bf16[256,2048]{1,0:T(8,128)(2,1)S(1)}, bf16[256,2048]{1,0:T(8,128)(2,1)S(1)}, u32[]{:S(2)}, u32[]{:S(2)}) %collective-permute-start.33) | collective-permute-done | bytes 1048608 | tf_op jit(solution)/shard_map/ppermute | solution.py:348
  688.5 14.5 %collective-permute-done.34 = bf16[256,2048]{1,0:T(8,128)(2,1)S(1)} collective-permute-done((bf16[256,2048]{1,0:T(8,128)(2,1)S(1)}, bf16[256,2048]{1,0:T(8,128)(2,1)S(1)}, u32[]{:S(2)}, u32[]{:S(2)}) %collective-permute-start.34) | collective-permute-done | bytes 1048608 | tf_op jit(solution)/shard_map/ppermute | solution.py:348
  705.2 2.8 convert_element_type.304
  708.0 9.9 convolution_convert_fusion.10.g_ref
  717.9 28.8 %attend_back.2 = bf16[1024,1536]{1,0:T(8,128)(2,1)} custom-call(s32[2]{0:T(128)} %pad_add_fusion.1.info, bf16[1024,512]{1,0:T(8,128)(2,1)} %get-tuple-element.69.q_ref, bf16[1024,512]{1,0:T(8,128)(2,1)} %get-tuple-element.70.k_ref, bf16[1024,512]{1,0:T(8,128)(2,1)} %get-tuple-element.71.v_ref, bf16[1024,512]{1,0:T(8,128)(2,1)} %get-tuple-element.48.a_ref, ...), custom_call_target="tpu_custom_call" | custom-call | flops 10737418240 | bytes 10485760 | tf_op jit(solution)/shard_map/attend_back/pallas_call | solution.py:241
  746.6 11.1 %convolution_convert_fusion.6 = bf16[1024,2048]{1,0:T(8,128)(2,1)} fusion(bf16[1024,1536]{1,0:T(8,128)(2,1)} %attend_back.2, bf16[2048,1536]{1,0:T(8,128)(2,1)} %all-gather.6.cloned.1.call-done), kind=kOutput, calls=%fused_computation.18 | convolution fusion | flops 6444548096 | bytes 13631488 | tf_op jit(solution)/shard_map/dot_general | solution.py:26
  757.8 9.5 convolution_convert_fusion.9
  767.3 22.7 %attend_back.3 = bf16[1024,1536]{1,0:T(8,128)(2,1)} custom-call(s32[2]{0:T(128)} %pad_add_fusion.info, bf16[1024,512]{1,0:T(8,128)(2,1)} %get-tuple-element.74.q_ref, bf16[1024,512]{1,0:T(8,128)(2,1)} %get-tuple-element.75.k_ref, bf16[1024,512]{1,0:T(8,128)(2,1)} %get-tuple-element.76.v_ref, bf16[1024,512]{1,0:T(8,128)(2,1)} %get-tuple-element.46.a_ref, ...), custom_call_target="tpu_custom_call" | custom-call | flops 10737418240 | bytes 10485760 | tf_op jit(solution)/shard_map/attend_back/pallas_call | solution.py:241
  790.0 19.3 %convolution_convert_fusion.4 = bf16[2048,1536]{1,0:T(8,128)(2,1)} fusion(bf16[2048,2048]{1,0:T(8,128)(2,1)} %get-tuple-element.132, bf16[1024,1536]{1,0:T(8,128)(2,1)} %attend_back.2, bf16[1024,1536]{1,0:T(8,128)(2,1)} %attend_back.3), kind=kOutput, calls=%fused_computation.5 | convolution fusion | flops 12900630528 | bytes 20971520 | tf_op jit(solution)/shard_map/dot_general | solution.py:30
  809.5 2.9 convert_element_type.328
  812.5 2.9 convert_element_type.327
  815.4 11.5 %convolution_convert_fusion.5 = bf16[1024,2048]{1,0:T(8,128)(2,1)} fusion(bf16[1024,1536]{1,0:T(8,128)(2,1)} %attend_back.3, bf16[2048,1536]{1,0:T(8,128)(2,1)} %all-gather.6.cloned.1.call-done), kind=kOutput, calls=%fused_computation.17 | convolution fusion | flops 6444548096 | bytes 13631488 | tf_op jit(solution)/shard_map/dot_general | solution.py:26
  828.8 3.2 fusion.72
  832.8 2.9 collective-permute-start.48
  837.2 3.0 collective-permute-start.52
  840.3 3.1 collective-permute-start.54
  847.7 2.9 fusion.71
  851.8 4.6 collective-permute-done.55
  856.9 12.7 %collective-permute-done.56 = f32[2,64]{1,0:T(2,128)S(1)} collective-permute-done((f32[2,64]{1,0:T(2,128)S(1)}, f32[2,64]{1,0:T(2,128)S(1)}, u32[]{:S(2)}, u32[]{:S(2)}) %collective-permute-start.56) | collective-permute-done | bytes 544 | tf_op jit(solution)/shard_map/ppermute | solution.py:407
  874.9 41.7 %collective-permute-done.57 = f32[2,64]{1,0:T(2,128)S(1)} collective-permute-done((f32[2,64]{1,0:T(2,128)S(1)}, f32[2,64]{1,0:T(2,128)S(1)}, u32[]{:S(2)}, u32[]{:S(2)}) %collective-permute-start.57) | collective-permute-done | bytes 544 | tf_op jit(solution)/shard_map/ppermute | solution.py:407
  921.2 4.2 add_convert_fusion.5
  926.9 15.8 %collective-permute-done.45 = bf16[256,2048]{1,0:T(8,128)(2,1)S(1)} collective-permute-done((bf16[256,2048]{1,0:T(8,128)(2,1)S(1)}, bf16[256,2048]{1,0:T(8,128)(2,1)S(1)}, u32[]{:S(2)}, u32[]{:S(2)}) %collective-permute-start.45) | collective-permute-done | bytes 1048608 | tf_op jit(solution)/shard_map/ppermute | solution.py:348
  944.3 22.2 %collective-permute-done.47 = bf16[256,2048]{1,0:T(8,128)(2,1)S(1)} collective-permute-done((bf16[256,2048]{1,0:T(8,128)(2,1)S(1)}, bf16[256,2048]{1,0:T(8,128)(2,1)S(1)}, u32[]{:S(2)}, u32[]{:S(2)}) %collective-permute-start.47) | collective-permute-done | bytes 1048608 | tf_op jit(solution)/shard_map/ppermute | solution.py:348
  968.0 2.7 fusion.28
  972.3 13.1 %collective-permute-done.38 = bf16[256,2048]{1,0:T(8,128)(2,1)S(1)} collective-permute-done((bf16[256,2048]{1,0:T(8,128)(2,1)S(1)}, bf16[256,2048]{1,0:T(8,128)(2,1)S(1)}, u32[]{:S(2)}, u32[]{:S(2)}) %collective-permute-start.38) | collective-permute-done | bytes 1048608 | tf_op jit(solution)/shard_map/ppermute | solution.py:348
  990.1 2.3 fusion.75
  (292 shorter events, 123.7 us)
Async XLA Ops:
  7.2 84.1 %all-gather.6.cloned.1.call-start = ((), (), s32[]{:S(2)}) async-start(), calls=%async_computation.5 | async-start | bytes 7077888 | tf_op jit(solution)/shard_map/all_gather | solution.py:432
  9.4 129.1 %all-gather.8.cloned.1.call-start = ((), (), s32[]{:S(2)}) async-start(), calls=%async_computation.6 | async-start | bytes 2359296 | tf_op jit(solution)/shard_map/all_gather | solution.py:432
  10.2 332.0 %all-gather.10.cloned.1.call-start = ((), (), s32[]{:S(2)}) async-start(), calls=%async_computation.7 | async-start | bytes 9437184 | tf_op jit(solution)/shard_map/all_gather | solution.py:432
  10.9 331.3 %all-gather.12.cloned.1.call-start = ((), (), s32[]{:S(2)}) async-start(), calls=%async_computation.8 | async-start | bytes 9437184 | tf_op jit(solution)/shard_map/all_gather | solution.py:432
  11.5 405.3 %all-gather.14.cloned.1.call-start = ((), (), s32[]{:S(2)}) async-start(), calls=%async_computation.9 | async-start | bytes 9437184 | tf_op jit(solution)/shard_map/all_gather | solution.py:432
  13.8 27.3 %collective-permute-start = (bf16[256,2048]{1,0:T(8,128)(2,1)}, bf16[256,2048]{1,0:T(8,128)(2,1)}, u32[]{:S(2)}, u32[]{:S(2)}) collective-permute-start(bf16[256,2048]{1,0:T(8,128)(2,1)} %get-tuple-element.94), channel_id=1, source_target_pairs={{0,1},{1,0},{2,3},{3,2},{4,5},{5,4},{6,7},{7,6},{8,9},{9,8},{10,11... | collective-permute-start | bytes 3145736 | tf_op jit(solution)/shard_map/ppermute | solution.py:348
  18.4 26.2 %collective-permute-start.3 = (bf16[256,2048]{1,0:T(8,128)(2,1)}, bf16[256,2048]{1,0:T(8,128)(2,1)S(1)}, u32[]{:S(2)}, u32[]{:S(2)}) collective-permute-start(bf16[256,2048]{1,0:T(8,128)(2,1)} %get-tuple-element.92), channel_id=1, source_target_pairs={{0,2},{1,3},{2,0},{3,1},{4,6},{5,7},{6,4},{7,5},{8,10},{9,11},{10,... | collective-permute-start | bytes 3145736 | tf_op jit(solution)/shard_map/ppermute | solution.py:348
  19.9 43.6 %collective-permute-start.1 = (bf16[256,2048]{1,0:T(8,128)(2,1)}, bf16[256,2048]{1,0:T(8,128)(2,1)}, u32[]{:S(2)}, u32[]{:S(2)}) collective-permute-start(bf16[256,2048]{1,0:T(8,128)(2,1)} %get-tuple-element.92), channel_id=1, source_target_pairs={{0,1},{1,0},{2,3},{3,2},{4,5},{5,4},{6,7},{7,6},{8,9},{9,8},{10,11... | collective-permute-start | bytes 3145736 | tf_op jit(solution)/shard_map/ppermute | solution.py:348
  20.4 46.8 %collective-permute-start.2 = (bf16[256,2048]{1,0:T(8,128)(2,1)}, bf16[256,2048]{1,0:T(8,128)(2,1)}, u32[]{:S(2)}, u32[]{:S(2)}) collective-permute-start(bf16[256,2048]{1,0:T(8,128)(2,1)} %get-tuple-element.94), channel_id=1, source_target_pairs={{0,2},{1,3},{2,0},{3,1},{4,6},{5,7},{6,4},{7,5},{8,10},{9,11},{10,... | collective-permute-start | bytes 3145736 | tf_op jit(solution)/shard_map/ppermute | solution.py:348
  41.0 47.1 %collective-permute-start.4 = (bf16[256,2048]{1,0:T(8,128)(2,1)}, bf16[256,2048]{1,0:T(8,128)(2,1)S(1)}, u32[]{:S(2)}, u32[]{:S(2)}) collective-permute-start(bf16[256,2048]{1,0:T(8,128)(2,1)} %collective-permute-done), channel_id=1, source_target_pairs={{0,2},{1,3},{2,0},{3,1},{4,6},{5,7},{6,4},{7,5},{8,10},{9,11},{10,... | collective-permute-start | bytes 3145736 | tf_op jit(solution)/shard_map/ppermute | solution.py:348
  44.6 45.1 %collective-permute-start.5 = (bf16[256,2048]{1,0:T(8,128)(2,1)S(1)}, bf16[256,2048]{1,0:T(8,128)(2,1)S(1)}, u32[]{:S(2)}, u32[]{:S(2)}) collective-permute-start(bf16[256,2048]{1,0:T(8,128)(2,1)S(1)} %collective-permute-done.3), channel_id=1, source_target_pairs={{0,1},{1,0},{2,3},{3,2},{4,5},{5,4},{6,7},{7,6},{8,9},{9,8},{10,11... | collective-permute-start | bytes 3145736 | tf_op jit(solution)/shard_map/ppermute | solution.py:348
  145.9 33.7 %collective-permute-start.10 = (bf16[256,2048]{1,0:T(8,128)(2,1)}, bf16[256,2048]{1,0:T(8,128)(2,1)S(1)}, u32[]{:S(2)}, u32[]{:S(2)}) collective-permute-start(bf16[256,2048]{1,0:T(8,128)(2,1)} %get-tuple-element.128), channel_id=1, source_target_pairs={{0,1},{1,0},{2,3},{3,2},{4,5},{5,4},{6,7},{7,6},{8,9},{9,8},{10,11... | collective-permute-start | bytes 3145736 | tf_op jit(solution)/shard_map/ppermute | solution.py:348
  146.2 559.0 %reduce-scatter.6.cloned.1.call-start = ((), (), s32[]{:S(2)}) async-start(), calls=%async_computation.10 | async-start | bytes 9437184 | tf_op jit(solution)/shard_map/reduce_scatter | solution.py:441
  147.4 33.8 %collective-permute-start.7 = (bf16[256,2048]{1,0:T(8,128)(2,1)}, bf16[256,2048]{1,0:T(8,128)(2,1)}, u32[]{:S(2)}, u32[]{:S(2)}) collective-permute-start(bf16[256,2048]{1,0:T(8,128)(2,1)} %get-tuple-element.129), channel_id=1, source_target_pairs={{0,2},{1,3},{2,0},{3,1},{4,6},{5,7},{6,4},{7,5},{8,10},{9,11},{10,... | collective-permute-start | bytes 3145736 | tf_op jit(solution)/shard_map/ppermute | solution.py:348
  165.9 31.5 %collective-permute-start.6 = (bf16[256,2048]{1,0:T(8,128)(2,1)}, bf16[256,2048]{1,0:T(8,128)(2,1)S(1)}, u32[]{:S(2)}, u32[]{:S(2)}) collective-permute-start(bf16[256,2048]{1,0:T(8,128)(2,1)} %get-tuple-element.127), channel_id=1, source_target_pairs={{0,2},{1,3},{2,0},{3,1},{4,6},{5,7},{6,4},{7,5},{8,10},{9,11},{10,... | collective-permute-start | bytes 3145736 | tf_op jit(solution)/shard_map/ppermute | solution.py:348
  177.7 26.1 %collective-permute-start.9 = (bf16[256,2048]{1,0:T(8,128)(2,1)S(1)}, bf16[256,2048]{1,0:T(8,128)(2,1)S(1)}, u32[]{:S(2)}, u32[]{:S(2)}) collective-permute-start(bf16[256,2048]{1,0:T(8,128)(2,1)S(1)} %slice.221), channel_id=1, source_target_pairs={{0,1},{1,0},{2,3},{3,2},{4,5},{5,4},{6,7},{7,6},{8,9},{9,8},{10,11... | collective-permute-start | bytes 3145736 | tf_op jit(solution)/shard_map/ppermute | solution.py:348
  181.2 38.7 %collective-permute-start.11 = (bf16[256,2048]{1,0:T(8,128)(2,1)S(1)}, bf16[256,2048]{1,0:T(8,128)(2,1)S(1)}, u32[]{:S(2)}, u32[]{:S(2)}) collective-permute-start(bf16[256,2048]{1,0:T(8,128)(2,1)S(1)} %add_convert_fusion.8), channel_id=1, source_target_pairs={{0,2},{1,3},{2,0},{3,1},{4,6},{5,7},{6,4},{7,5},{8,10},{9,11},{10,... | collective-permute-start | bytes 3145736 | tf_op jit(solution)/shard_map/ppermute | solution.py:348
  182.9 43.3 %collective-permute-start.8 = (bf16[256,2048]{1,0:T(8,128)(2,1)S(1)}, bf16[256,2048]{1,0:T(8,128)(2,1)S(1)}, u32[]{:S(2)}, u32[]{:S(2)}) collective-permute-start(bf16[256,2048]{1,0:T(8,128)(2,1)S(1)} %add_convert_fusion.9), channel_id=1, source_target_pairs={{0,1},{1,0},{2,3},{3,2},{4,5},{5,4},{6,7},{7,6},{8,9},{9,8},{10,11... | collective-permute-start | bytes 3145736 | tf_op jit(solution)/shard_map/ppermute | solution.py:348
  184.5 64.2 %collective-permute-start.18 = (bf16[256,2048]{1,0:T(8,128)(2,1)S(1)}, bf16[256,2048]{1,0:T(8,128)(2,1)S(1)}, u32[]{:S(2)}, u32[]{:S(2)}) collective-permute-start(bf16[256,2048]{1,0:T(8,128)(2,1)S(1)} %get-tuple-element.50), channel_id=1, source_target_pairs={{0,1},{1,0},{2,3},{3,2},{4,5},{5,4},{6,7},{7,6},{8,9},{9,8},{10,11... | collective-permute-start | bytes 3145736 | tf_op jit(solution)/shard_map/ppermute | solution.py:348
  197.4 96.2 %collective-permute-start.21 = (bf16[256,2048]{1,0:T(8,128)(2,1)S(1)}, bf16[256,2048]{1,0:T(8,128)(2,1)}, u32[]{:S(2)}, u32[]{:S(2)}) collective-permute-start(bf16[256,2048]{1,0:T(8,128)(2,1)S(1)} %get-tuple-element.51), channel_id=1, source_target_pairs={{0,2},{1,3},{2,0},{3,1},{4,6},{5,7},{6,4},{7,5},{8,10},{9,11},{10,... | collective-permute-start | bytes 3145736 | tf_op jit(solution)/shard_map/ppermute | solution.py:348
  203.7 67.4 %collective-permute-start.19 = (bf16[256,2048]{1,0:T(8,128)(2,1)S(1)}, bf16[256,2048]{1,0:T(8,128)(2,1)S(1)}, u32[]{:S(2)}, u32[]{:S(2)}) collective-permute-start(bf16[256,2048]{1,0:T(8,128)(2,1)S(1)} %get-tuple-element.51), channel_id=1, source_target_pairs={{0,1},{1,0},{2,3},{3,2},{4,5},{5,4},{6,7},{7,6},{8,9},{9,8},{10,11... | collective-permute-start | bytes 3145736 | tf_op jit(solution)/shard_map/ppermute | solution.py:348
  219.9 54.1 %collective-permute-start.20 = (bf16[256,2048]{1,0:T(8,128)(2,1)S(1)}, bf16[256,2048]{1,0:T(8,128)(2,1)S(1)}, u32[]{:S(2)}, u32[]{:S(2)}) collective-permute-start(bf16[256,2048]{1,0:T(8,128)(2,1)S(1)} %get-tuple-element.50), channel_id=1, source_target_pairs={{0,2},{1,3},{2,0},{3,1},{4,6},{5,7},{6,4},{7,5},{8,10},{9,11},{10,... | collective-permute-start | bytes 3145736 | tf_op jit(solution)/shard_map/ppermute | solution.py:348
  228.2 65.4 %collective-permute-start.12 = (bf16[256,2048]{1,0:T(8,128)(2,1)S(1)}, bf16[256,2048]{1,0:T(8,128)(2,1)S(1)}, u32[]{:S(2)}, u32[]{:S(2)}) collective-permute-start(bf16[256,2048]{1,0:T(8,128)(2,1)S(1)} %get-tuple-element.104), channel_id=1, source_target_pairs={{0,1},{1,0},{2,3},{3,2},{4,5},{5,4},{6,7},{7,6},{8,9},{9,8},{10,11... | collective-permute-start | bytes 3145736 | tf_op jit(solution)/shard_map/ppermute | solution.py:348
  248.7 47.3 %collective-permute-start.15 = (bf16[256,2048]{1,0:T(8,128)(2,1)S(1)}, bf16[256,2048]{1,0:T(8,128)(2,1)S(1)}, u32[]{:S(2)}, u32[]{:S(2)}) collective-permute-start(bf16[256,2048]{1,0:T(8,128)(2,1)S(1)} %get-tuple-element.100), channel_id=1, source_target_pairs={{0,2},{1,3},{2,0},{3,1},{4,6},{5,7},{6,4},{7,5},{8,10},{9,11},{10,... | collective-permute-start | bytes 3145736 | tf_op jit(solution)/shard_map/ppermute | solution.py:348
  271.2 44.9 %collective-permute-start.13 = (bf16[256,2048]{1,0:T(8,128)(2,1)S(1)}, bf16[256,2048]{1,0:T(8,128)(2,1)S(1)}, u32[]{:S(2)}, u32[]{:S(2)}) collective-permute-start(bf16[256,2048]{1,0:T(8,128)(2,1)S(1)} %get-tuple-element.100), channel_id=1, source_target_pairs={{0,1},{1,0},{2,3},{3,2},{4,5},{5,4},{6,7},{7,6},{8,9},{9,8},{10,11... | collective-permute-start | bytes 3145736 | tf_op jit(solution)/shard_map/ppermute | solution.py:348
  274.0 42.2 %collective-permute-start.14 = (bf16[256,2048]{1,0:T(8,128)(2,1)S(1)}, bf16[256,2048]{1,0:T(8,128)(2,1)S(1)}, u32[]{:S(2)}, u32[]{:S(2)}) collective-permute-start(bf16[256,2048]{1,0:T(8,128)(2,1)S(1)} %get-tuple-element.104), channel_id=1, source_target_pairs={{0,2},{1,3},{2,0},{3,1},{4,6},{5,7},{6,4},{7,5},{8,10},{9,11},{10,... | collective-permute-start | bytes 3145736 | tf_op jit(solution)/shard_map/ppermute | solution.py:348
  293.6 37.3 %collective-permute-start.16 = (bf16[256,2048]{1,0:T(8,128)(2,1)S(1)}, bf16[256,2048]{1,0:T(8,128)(2,1)S(1)}, u32[]{:S(2)}, u32[]{:S(2)}) collective-permute-start(bf16[256,2048]{1,0:T(8,128)(2,1)S(1)} %collective-permute-done.12), channel_id=1, source_target_pairs={{0,2},{1,3},{2,0},{3,1},{4,6},{5,7},{6,4},{7,5},{8,10},{9,11},{10,... | collective-permute-start | bytes 3145736 | tf_op jit(solution)/shard_map/ppermute | solution.py:348
  296.0 39.6 %collective-permute-start.17 = (bf16[256,2048]{1,0:T(8,128)(2,1)S(1)}, bf16[256,2048]{1,0:T(8,128)(2,1)S(1)}, u32[]{:S(2)}, u32[]{:S(2)}) collective-permute-start(bf16[256,2048]{1,0:T(8,128)(2,1)S(1)} %collective-permute-done.15), channel_id=1, source_target_pairs={{0,1},{1,0},{2,3},{3,2},{4,5},{5,4},{6,7},{7,6},{8,9},{9,8},{10,11... | collective-permute-start | bytes 3145736 | tf_op jit(solution)/shard_map/ppermute | solution.py:348
  338.9 53.0 %collective-permute-start.23 = (bf16[256,2048]{1,0:T(8,128)(2,1)}, bf16[256,2048]{1,0:T(8,128)(2,1)S(1)}, u32[]{:S(2)}, u32[]{:S(2)}) collective-permute-start(bf16[256,2048]{1,0:T(8,128)(2,1)} %collective-permute-done.21), channel_id=1, source_target_pairs={{0,1},{1,0},{2,3},{3,2},{4,5},{5,4},{6,7},{7,6},{8,9},{9,8},{10,11... | collective-permute-start | bytes 3145736 | tf_op jit(solution)/shard_map/ppermute | solution.py:348
  340.6 50.2 %collective-permute-start.22 = (bf16[256,2048]{1,0:T(8,128)(2,1)S(1)}, bf16[256,2048]{1,0:T(8,128)(2,1)S(1)}, u32[]{:S(2)}, u32[]{:S(2)}) collective-permute-start(bf16[256,2048]{1,0:T(8,128)(2,1)S(1)} %collective-permute-done.18), channel_id=1, source_target_pairs={{0,2},{1,3},{2,0},{3,1},{4,6},{5,7},{6,4},{7,5},{8,10},{9,11},{10,... | collective-permute-start | bytes 3145736 | tf_op jit(solution)/shard_map/ppermute | solution.py:348
  416.7 392.8 %reduce-scatter.10.cloned.1.call-start = ((), (), s32[]{:S(2)}) async-start(), calls=%async_computation.12 | async-start | bytes 9437184 | tf_op jit(solution)/shard_map/reduce_scatter | solution.py:441
  555.4 257.1 %reduce-scatter.8.cloned.1.call-start = ((), (), s32[]{:S(2)}) async-start(), calls=%async_computation.11 | async-start | bytes 9437184 | tf_op jit(solution)/shard_map/reduce_scatter | solution.py:441
  556.2 432.1 %reduce-scatter.14.cloned.1.call-start = ((), (), s32[]{:S(2)}) async-start(), calls=%async_computation.14 | async-start | bytes 2359296 | tf_op jit(solution)/shard_map/reduce_scatter | solution.py:441
  558.5 26.1 %collective-permute-start.28 = (bf16[256,2048]{1,0:T(8,128)(2,1)S(1)}, bf16[256,2048]{1,0:T(8,128)(2,1)S(1)}, u32[]{:S(2)}, u32[]{:S(2)}) collective-permute-start(bf16[256,2048]{1,0:T(8,128)(2,1)S(1)} %get-tuple-element.124), channel_id=1, source_target_pairs={{0,1},{1,0},{2,3},{3,2},{4,5},{5,4},{6,7},{7,6},{8,9},{9,8},{10,11... | collective-permute-start | bytes 3145736 | tf_op jit(solution)/shard_map/ppermute | solution.py:348
  559.3 27.9 %collective-permute-start.25 = (bf16[256,2048]{1,0:T(8,128)(2,1)S(1)}, bf16[256,2048]{1,0:T(8,128)(2,1)S(1)}, u32[]{:S(2)}, u32[]{:S(2)}) collective-permute-start(bf16[256,2048]{1,0:T(8,128)(2,1)S(1)} %get-tuple-element.125), channel_id=1, source_target_pairs={{0,2},{1,3},{2,0},{3,1},{4,6},{5,7},{6,4},{7,5},{8,10},{9,11},{10,... | collective-permute-start | bytes 3145736 | tf_op jit(solution)/shard_map/ppermute | solution.py:348
  559.7 48.1 %collective-permute-start.24 = (bf16[256,2048]{1,0:T(8,128)(2,1)S(1)}, bf16[256,2048]{1,0:T(8,128)(2,1)S(1)}, u32[]{:S(2)}, u32[]{:S(2)}) collective-permute-start(bf16[256,2048]{1,0:T(8,128)(2,1)S(1)} %get-tuple-element.126), channel_id=1, source_target_pairs={{0,2},{1,3},{2,0},{3,1},{4,6},{5,7},{6,4},{7,5},{8,10},{9,11},{10,... | collective-permute-start | bytes 3145736 | tf_op jit(solution)/shard_map/ppermute | solution.py:348
  561.5 46.3 %collective-permute-start.27 = (bf16[256,2048]{1,0:T(8,128)(2,1)S(1)}, bf16[256,2048]{1,0:T(8,128)(2,1)S(1)}, u32[]{:S(2)}, u32[]{:S(2)}) collective-permute-start(bf16[256,2048]{1,0:T(8,128)(2,1)S(1)} %slice.229), channel_id=1, source_target_pairs={{0,1},{1,0},{2,3},{3,2},{4,5},{5,4},{6,7},{7,6},{8,9},{9,8},{10,11... | collective-permute-start | bytes 3145736 | tf_op jit(solution)/shard_map/ppermute | solution.py:348
  586.3 41.3 %collective-permute-start.29 = (bf16[256,2048]{1,0:T(8,128)(2,1)S(1)}, bf16[256,2048]{1,0:T(8,128)(2,1)S(1)}, u32[]{:S(2)}, u32[]{:S(2)}) collective-permute-start(bf16[256,2048]{1,0:T(8,128)(2,1)S(1)} %add_convert_fusion.6), channel_id=1, source_target_pairs={{0,2},{1,3},{2,0},{3,1},{4,6},{5,7},{6,4},{7,5},{8,10},{9,11},{10,... | collective-permute-start | bytes 3145736 | tf_op jit(solution)/shard_map/ppermute | solution.py:348
  587.7 39.9 %collective-permute-start.26 = (bf16[256,2048]{1,0:T(8,128)(2,1)S(1)}, bf16[256,2048]{1,0:T(8,128)(2,1)S(1)}, u32[]{:S(2)}, u32[]{:S(2)}) collective-permute-start(bf16[256,2048]{1,0:T(8,128)(2,1)S(1)} %add_convert_fusion.7), channel_id=1, source_target_pairs={{0,1},{1,0},{2,3},{3,2},{4,5},{5,4},{6,7},{7,6},{8,9},{9,8},{10,11... | collective-permute-start | bytes 3145736 | tf_op jit(solution)/shard_map/ppermute | solution.py:348
  633.7 26.0 %collective-permute-start.30 = (bf16[256,2048]{1,0:T(8,128)(2,1)S(1)}, bf16[256,2048]{1,0:T(8,128)(2,1)S(1)}, u32[]{:S(2)}, u32[]{:S(2)}) collective-permute-start(bf16[256,2048]{1,0:T(8,128)(2,1)S(1)} %get-tuple-element.64), channel_id=1, source_target_pairs={{0,1},{1,0},{2,3},{3,2},{4,5},{5,4},{6,7},{7,6},{8,9},{9,8},{10,11... | collective-permute-start | bytes 3145736 | tf_op jit(solution)/shard_map/ppermute | solution.py:348
  635.4 51.0 %collective-permute-start.32 = (bf16[256,2048]{1,0:T(8,128)(2,1)S(1)}, bf16[256,2048]{1,0:T(8,128)(2,1)S(1)}, u32[]{:S(2)}, u32[]{:S(2)}) collective-permute-start(bf16[256,2048]{1,0:T(8,128)(2,1)S(1)} %get-tuple-element.64), channel_id=1, source_target_pairs={{0,2},{1,3},{2,0},{3,1},{4,6},{5,7},{6,4},{7,5},{8,10},{9,11},{10,... | collective-permute-start | bytes 3145736 | tf_op jit(solution)/shard_map/ppermute | solution.py:348
  635.6 49.6 %collective-permute-start.31 = (bf16[256,2048]{1,0:T(8,128)(2,1)S(1)}, bf16[256,2048]{1,0:T(8,128)(2,1)S(1)}, u32[]{:S(2)}, u32[]{:S(2)}) collective-permute-start(bf16[256,2048]{1,0:T(8,128)(2,1)S(1)} %get-tuple-element.65), channel_id=1, source_target_pairs={{0,1},{1,0},{2,3},{3,2},{4,5},{5,4},{6,7},{7,6},{8,9},{9,8},{10,11... | collective-permute-start | bytes 3145736 | tf_op jit(solution)/shard_map/ppermute | solution.py:348
  636.0 47.9 %collective-permute-start.33 = (bf16[256,2048]{1,0:T(8,128)(2,1)S(1)}, bf16[256,2048]{1,0:T(8,128)(2,1)S(1)}, u32[]{:S(2)}, u32[]{:S(2)}) collective-permute-start(bf16[256,2048]{1,0:T(8,128)(2,1)S(1)} %get-tuple-element.65), channel_id=1, source_target_pairs={{0,2},{1,3},{2,0},{3,1},{4,6},{5,7},{6,4},{7,5},{8,10},{9,11},{10,... | collective-permute-start | bytes 3145736 | tf_op jit(solution)/shard_map/ppermute | solution.py:348
  659.7 43.3 %collective-permute-start.34 = (bf16[256,2048]{1,0:T(8,128)(2,1)S(1)}, bf16[256,2048]{1,0:T(8,128)(2,1)S(1)}, u32[]{:S(2)}, u32[]{:S(2)}) collective-permute-start(bf16[256,2048]{1,0:T(8,128)(2,1)S(1)} %collective-permute-done.30), channel_id=1, source_target_pairs={{0,2},{1,3},{2,0},{3,1},{4,6},{5,7},{6,4},{7,5},{8,10},{9,11},{10,... | collective-permute-start | bytes 3145736 | tf_op jit(solution)/shard_map/ppermute | solution.py:348
  683.9 20.3 %collective-permute-start.35 = (bf16[256,2048]{1,0:T(8,128)(2,1)S(1)}, bf16[256,2048]{1,0:T(8,128)(2,1)S(1)}, u32[]{:S(2)}, u32[]{:S(2)}) collective-permute-start(bf16[256,2048]{1,0:T(8,128)(2,1)S(1)} %collective-permute-done.33), channel_id=1, source_target_pairs={{0,1},{1,0},{2,3},{3,2},{4,5},{5,4},{6,7},{7,6},{8,9},{9,8},{10,11... | collective-permute-start | bytes 3145736 | tf_op jit(solution)/shard_map/ppermute | solution.py:348
  767.2 222.8 %reduce-scatter.12.cloned.1.call-start = ((), (), s32[]{:S(2)}) async-start(), calls=%async_computation.13 | async-start | bytes 7077888 | tf_op jit(solution)/shard_map/reduce_scatter | solution.py:441
  832.0 38.6 %collective-permute-start.46 = (bf16[256,2048]{1,0:T(8,128)(2,1)}, bf16[256,2048]{1,0:T(8,128)(2,1)S(1)}, u32[]{:S(2)}, u32[]{:S(2)}) collective-permute-start(bf16[256,2048]{1,0:T(8,128)(2,1)} %get-tuple-element.122), channel_id=1, source_target_pairs={{0,1},{1,0},{2,3},{3,2},{4,5},{5,4},{6,7},{7,6},{8,9},{9,8},{10,11... | collective-permute-start | bytes 3145736 | tf_op jit(solution)/shard_map/ppermute | solution.py:348
  837.2 6.3 collective-permute-start.51
  837.2 6.4 collective-permute-start.52
  840.2 5.6 collective-permute-start.53
  843.5 29.8 %collective-permute-start.43 = (bf16[256,2048]{1,0:T(8,128)(2,1)S(1)}, bf16[256,2048]{1,0:T(8,128)(2,1)S(1)}, u32[]{:S(2)}, u32[]{:S(2)}) collective-permute-start(bf16[256,2048]{1,0:T(8,128)(2,1)S(1)} %get-tuple-element.123), channel_id=1, source_target_pairs={{0,2},{1,3},{2,0},{3,1},{4,6},{5,7},{6,4},{7,5},{8,10},{9,11},{10,... | collective-permute-start | bytes 3145736 | tf_op jit(solution)/shard_map/ppermute | solution.py:348
  845.9 10.5 %collective-permute-start.55 = (f32[2,64]{1,0:T(2,128)S(1)}, f32[2,64]{1,0:T(2,128)S(1)}, u32[]{:S(2)}, u32[]{:S(2)}) collective-permute-start(f32[2,64]{1,0:T(2,128)S(1)} %get-tuple-element.149), channel_id=1, source_target_pairs={{0,1},{1,0},{2,3},{3,2},{4,5},{5,4},{6,7},{7,6},{8,9},{9,8},{10,11... | collective-permute-start | bytes 1544 | tf_op jit(solution)/shard_map/ppermute | solution.py:407
  847.1 22.5 %collective-permute-start.56 = (f32[2,64]{1,0:T(2,128)S(1)}, f32[2,64]{1,0:T(2,128)S(1)}, u32[]{:S(2)}, u32[]{:S(2)}) collective-permute-start(f32[2,64]{1,0:T(2,128)S(1)} %get-tuple-element.151), channel_id=1, source_target_pairs={{0,2},{1,3},{2,0},{3,1},{4,6},{5,7},{6,4},{7,5},{8,10},{9,11},{10,... | collective-permute-start | bytes 1544 | tf_op jit(solution)/shard_map/ppermute | solution.py:407
  850.7 67.3 %collective-permute-start.36 = (bf16[256,2048]{1,0:T(8,128)(2,1)S(1)}, bf16[256,2048]{1,0:T(8,128)(2,1)S(1)}, u32[]{:S(2)}, u32[]{:S(2)}) collective-permute-start(bf16[256,2048]{1,0:T(8,128)(2,1)S(1)} %get-tuple-element.111), channel_id=1, source_target_pairs={{0,2},{1,3},{2,0},{3,1},{4,6},{5,7},{6,4},{7,5},{8,10},{9,11},{10,... | collective-permute-start | bytes 3145736 | tf_op jit(solution)/shard_map/ppermute | solution.py:348
  856.4 63.0 %collective-permute-start.37 = (bf16[256,2048]{1,0:T(8,128)(2,1)S(1)}, bf16[256,2048]{1,0:T(8,128)(2,1)S(1)}, u32[]{:S(2)}, u32[]{:S(2)}) collective-permute-start(bf16[256,2048]{1,0:T(8,128)(2,1)S(1)} %get-tuple-element.114), channel_id=1, source_target_pairs={{0,2},{1,3},{2,0},{3,1},{4,6},{5,7},{6,4},{7,5},{8,10},{9,11},{10,... | collective-permute-start | bytes 3145736 | tf_op jit(solution)/shard_map/ppermute | solution.py:348
  869.6 50.4 %collective-permute-start.39 = (bf16[256,2048]{1,0:T(8,128)(2,1)S(1)}, bf16[256,2048]{1,0:T(8,128)(2,1)S(1)}, u32[]{:S(2)}, u32[]{:S(2)}) collective-permute-start(bf16[256,2048]{1,0:T(8,128)(2,1)S(1)} %get-tuple-element.113), channel_id=1, source_target_pairs={{0,1},{1,0},{2,3},{3,2},{4,5},{5,4},{6,7},{7,6},{8,9},{9,8},{10,11... | collective-permute-start | bytes 3145736 | tf_op jit(solution)/shard_map/ppermute | solution.py:348
  870.7 50.5 %collective-permute-start.40 = (bf16[256,2048]{1,0:T(8,128)(2,1)S(1)}, bf16[256,2048]{1,0:T(8,128)(2,1)S(1)}, u32[]{:S(2)}, u32[]{:S(2)}) collective-permute-start(bf16[256,2048]{1,0:T(8,128)(2,1)S(1)} %get-tuple-element.112), channel_id=1, source_target_pairs={{0,1},{1,0},{2,3},{3,2},{4,5},{5,4},{6,7},{7,6},{8,9},{9,8},{10,11... | collective-permute-start | bytes 3145736 | tf_op jit(solution)/shard_map/ppermute | solution.py:348
  873.3 43.3 %collective-permute-start.57 = (f32[2,64]{1,0:T(2,128)S(1)}, f32[2,64]{1,0:T(2,128)S(1)}, u32[]{:S(2)}, u32[]{:S(2)}) collective-permute-start(f32[2,64]{1,0:T(2,128)S(1)} %get-tuple-element.150), channel_id=1, source_target_pairs={{0,3},{1,2},{2,1},{3,0},{4,7},{5,6},{6,5},{7,4},{8,11},{9,10},{10,... | collective-permute-start | bytes 1544 | tf_op jit(solution)/shard_map/ppermute | solution.py:407
  916.6 26.0 %collective-permute-start.45 = (bf16[256,2048]{1,0:T(8,128)(2,1)S(1)}, bf16[256,2048]{1,0:T(8,128)(2,1)S(1)}, u32[]{:S(2)}, u32[]{:S(2)}) collective-permute-start(bf16[256,2048]{1,0:T(8,128)(2,1)S(1)} %slice.237), channel_id=1, source_target_pairs={{0,1},{1,0},{2,3},{3,2},{4,5},{5,4},{6,7},{7,6},{8,9},{9,8},{10,11... | collective-permute-start | bytes 3145736 | tf_op jit(solution)/shard_map/ppermute | solution.py:348
  917.9 26.3 %collective-permute-start.42 = (bf16[256,2048]{1,0:T(8,128)(2,1)S(1)}, bf16[256,2048]{1,0:T(8,128)(2,1)S(1)}, u32[]{:S(2)}, u32[]{:S(2)}) collective-permute-start(bf16[256,2048]{1,0:T(8,128)(2,1)S(1)} %get-tuple-element.121), channel_id=1, source_target_pairs={{0,2},{1,3},{2,0},{3,1},{4,6},{5,7},{6,4},{7,5},{8,10},{9,11},{10,... | collective-permute-start | bytes 3145736 | tf_op jit(solution)/shard_map/ppermute | solution.py:348
  919.3 47.1 %collective-permute-start.47 = (bf16[256,2048]{1,0:T(8,128)(2,1)S(1)}, bf16[256,2048]{1,0:T(8,128)(2,1)S(1)}, u32[]{:S(2)}, u32[]{:S(2)}) collective-permute-start(bf16[256,2048]{1,0:T(8,128)(2,1)S(1)} %add_convert_fusion), channel_id=1, source_target_pairs={{0,2},{1,3},{2,0},{3,1},{4,6},{5,7},{6,4},{7,5},{8,10},{9,11},{10,... | collective-permute-start | bytes 3145736 | tf_op jit(solution)/shard_map/ppermute | solution.py:348
  920.0 46.5 %collective-permute-start.44 = (bf16[256,2048]{1,0:T(8,128)(2,1)S(1)}, bf16[256,2048]{1,0:T(8,128)(2,1)S(1)}, u32[]{:S(2)}, u32[]{:S(2)}) collective-permute-start(bf16[256,2048]{1,0:T(8,128)(2,1)S(1)} %add_convert_fusion.1), channel_id=1, source_target_pairs={{0,1},{1,0},{2,3},{3,2},{4,5},{5,4},{6,7},{7,6},{8,9},{9,8},{10,11... | collective-permute-start | bytes 3145736 | tf_op jit(solution)/shard_map/ppermute | solution.py:348
  925.5 59.9 %collective-permute-start.38 = (bf16[256,2048]{1,0:T(8,128)(2,1)S(1)}, bf16[256,2048]{1,0:T(8,128)(2,1)S(1)}, u32[]{:S(2)}, u32[]{:S(2)}) collective-permute-start(bf16[256,2048]{1,0:T(8,128)(2,1)S(1)} %get-tuple-element.110), channel_id=1, source_target_pairs={{0,1},{1,0},{2,3},{3,2},{4,5},{5,4},{6,7},{7,6},{8,9},{9,8},{10,11... | collective-permute-start | bytes 3145736 | tf_op jit(solution)/shard_map/ppermute | solution.py:348
  942.6 43.5 %collective-permute-start.41 = (bf16[256,2048]{1,0:T(8,128)(2,1)S(1)}, bf16[256,2048]{1,0:T(8,128)(2,1)S(1)}, u32[]{:S(2)}, u32[]{:S(2)}) collective-permute-start(bf16[256,2048]{1,0:T(8,128)(2,1)S(1)} %get-tuple-element.108), channel_id=1, source_target_pairs={{0,2},{1,3},{2,0},{3,1},{4,6},{5,7},{6,4},{7,5},{8,10},{9,11},{10,... | collective-permute-start | bytes 3145736 | tf_op jit(solution)/shard_map/ppermute | solution.py:348
  (51 other events, 952.5 us)
Sparse Core Ops, SparseCore 0:
  10.2 67.4 all-gather.5
  79.3 27.7 all-gather.7
  108.7 81.4 all-gather.9
  191.7 80.4 all-gather.11
  273.6 80.5 all-gather.13
  416.9 86.7 reduce-scatter.5
  555.5 86.7 reduce-scatter.9
  644.7 87.9 reduce-scatter.7
  767.4 32.4 reduce-scatter.13
  809.5 69.1 reduce-scatter.11
